TPU v7x, 256 devices: a whole 4x4x8 slice. The times are simulated.
256 devices in a mesh: gx: 8 (over z), gy: 4 (over y), gz: 8 (over x, core).
Axes of the slice: x: 4, y: 4, z: 8, core: 2. Of those that a mesh axis runs over, the one named last changes fastest.
Arguments:
- schur: bfloat16 [8, 4, 8, 2048, 2048], P('gx', 'gy', 'gz'), may hold values from -0.09375 to 0.09375
- interface_diag: float32 [8, 4, 8, 2048], P('gx', 'gy', 'gz'), may hold values from 2 to 4
- precond: float32 [8, 4, 8, 16, 128, 128], P('gx', 'gy', 'gz'), may hold values from -0.3 to 0.8
- load: bfloat16 [8, 4, 8, 2048, 256], P('gx', 'gy', 'gz'), may hold values from -170 to 170
- face_blocks: int32 [8, 4, 8, 6, 2], P('gx', 'gy', 'gz'), may hold values from 0 to 16, as said below
Outputs:
- solution: float32 [8, 4, 8, 2048, 256], P('gx', 'gy', 'gz')
- residual_norm: float32 [256], replicated
Inputs may be any that keep to these rules, and one draw needn't show every extreme that they name: `face_blocks`: for each subdomain p and direction d (0, 1: next and previous along the first grid dimension; 2, 3 and 4, 5 likewise along the second and third), slots 0 to n - 1 hold block numbers below 16 shared with the neighbour in that direction, where n (1 to 2 inside the grid, 0 across its boundary) equals the neighbour's n for the opposite direction, and the neighbour's slot k of the opposite direction holds the block that shares with p's slot k; the remaining slots hold 16; no block number appears twice in one subdomain's table; some face shares 2 blocks in every draw.
All inputs are finite; a program needn't handle non-finite values.
Results may differ from a plain program's by a relative error of at most 0.0008.
Values sent between devices are 32-bit elements; how exact they have to be, the bound alone decides.
No kernel may reach another device: no remote copies, remote signals or barrier semaphores. Data moves between devices by JAX's collectives and lax.ppermute only.
A program may use at most 128 MiB of HBM per device.

v0:
```python
import functools

import jax
import jax.numpy as jnp
from jax import lax
from jax.sharding import Mesh
from jax.sharding import PartitionSpec as P

GZ = ("gz_0", "gz_1")
GX_GY_GZ = ("gx", "gy", "gz_0", "gz_1")


epsilon = 1e-06


def extended_2(value, sides, width):
    for axis, dim in sides:
        peers, length = (lax.axis_size(axis), value.shape[dim])
        up = [(i, (i + 1) % peers) for i in range(peers - 1)]
        down = [(j, i) for i, j in up]
        last = lax.slice_in_dim(value, length - width, length, axis=dim)
        leading = lax.slice_in_dim(value, 0, width, axis=dim)
        before = lax.ppermute(last, axis, up)
        after = lax.ppermute(leading, axis, down)
        value = jnp.concatenate([before, value, after], axis=dim)
    return value


def one_axis_at_a_time(value, axes):
    return functools.reduce(lax.psum, axes, value)


def assemble(blocks, slot_index, live_mask):
    block_count, block_rows, row_width = blocks.shape
    slot_count = slot_index.shape[1]
    extended = jnp.concatenate([blocks, jnp.zeros((1, block_rows, row_width), jnp.float32)], axis=0)
    slot_flat = slot_index.reshape(-1)
    packed = extended[slot_flat].reshape(6, slot_count, block_rows, row_width)
    gx_faces = extended_2(jnp.stack([packed[1], packed[0]], 0), (("gx", 0),), 1)
    gy_faces = extended_2(jnp.stack([packed[3], packed[2]], 0), (("gy", 0),), 1)
    gz_faces = extended_2(jnp.stack([packed[5], packed[4]], 0), ((GZ, 0),), 1)
    arrived = jnp.stack(
        [gx_faces[3], gx_faces[0], gy_faces[3], gy_faces[0], gz_faces[3], gz_faces[0]], 0
    )
    extended = extended.at[slot_flat].add(arrived.reshape(6 * slot_count, block_rows, row_width))
    return extended[:block_count] * live_mask[:, None, None]


def partial_product(left_vec, right_vec):
    return 0.5 * jnp.sum(left_vec * right_vec, axis=(0, 1))


def on_device(schur, interface_diag, precond, load, face_blocks):
    block_count = precond.shape[3]
    block_rows = precond.shape[4]
    rhs_count = load.shape[-1]
    slot_index = face_blocks.reshape(6, face_blocks.shape[-1])
    slot_hits = slot_index[:, :, None] == jnp.arange(block_count, dtype=jnp.int32)
    live_mask = jnp.any(slot_hits, axis=(0, 1)).astype(jnp.float32)
    matrix = schur.reshape(schur.shape[-2], schur.shape[-1])
    diag_column = interface_diag.reshape(-1, 1)
    local_blocks = precond.reshape(block_count, block_rows, block_rows)
    assembled_load = assemble(
        load.reshape(block_count, block_rows, rhs_count).astype(jnp.float32), slot_index, live_mask
    )
    widened = jnp.pad(local_blocks, ((0, 0), (0, 0), (0, rhs_count - block_rows)))
    summed = assemble(widened, slot_index, live_mask)[:, :, :block_rows]

    def precondition(vector):
        return jnp.einsum("bij,bjr->bir", summed, vector, precision=lax.Precision.HIGHEST)

    def operate(vector):
        flattened = vector.reshape(block_count * block_rows, rhs_count)
        narrow = flattened.astype(jnp.bfloat16)
        product = jnp.dot(matrix, narrow, preferred_element_type=jnp.float32)
        partial_value = product + diag_column * flattened
        return assemble(
            partial_value.reshape(block_count, block_rows, rhs_count), slot_index, live_mask
        )

    precond_raw = precondition(assembled_load)
    working_raw = operate(precond_raw)
    load_square, cross_first, raw_square = (
        one_axis_at_a_time(partial_product(assembled_load, assembled_load), GX_GY_GZ),
        one_axis_at_a_time(partial_product(working_raw, assembled_load), GX_GY_GZ),
        one_axis_at_a_time(partial_product(working_raw, working_raw), GX_GY_GZ),
    )
    initial = jnp.sqrt(load_square + epsilon)
    rescale = 1.0 / initial
    basis_first = assembled_load * rescale
    precond_first = precond_raw * rescale
    diag_first = cross_first * rescale * rescale
    working = working_raw * rescale - diag_first * basis_first
    below_first = jnp.sqrt(
        jnp.maximum(raw_square * rescale * rescale - diag_first * diag_first, 0.0) + epsilon
    )
    basis_second = working / below_first
    precond_second = precondition(basis_second)
    working = operate(precond_second)
    upper_second, diag_second, work_square = (
        one_axis_at_a_time(partial_product(working, basis_first), GX_GY_GZ),
        one_axis_at_a_time(partial_product(working, basis_second), GX_GY_GZ),
        one_axis_at_a_time(partial_product(working, working), GX_GY_GZ),
    )
    below_second = jnp.sqrt(
        jnp.maximum(work_square - upper_second * upper_second - diag_second * diag_second, 0.0)
        + epsilon
    )
    radius_first = jnp.sqrt(diag_first * diag_first + below_first * below_first)
    cosine_first = diag_first / radius_first
    sine_first = below_first / radius_first
    rotated_top = cosine_first * upper_second + sine_first * diag_second
    rotated_low = cosine_first * diag_second - sine_first * upper_second
    radius_second = jnp.sqrt(rotated_low * rotated_low + below_second * below_second)
    cosine_second = rotated_low / radius_second
    sine_second = below_second / radius_second
    weight_second = -initial * sine_first * cosine_second / radius_second
    weight_first = (initial * cosine_first - rotated_top * weight_second) / radius_first
    solution = weight_first * precond_first + weight_second * precond_second
    residual_norm = initial * sine_first * sine_second
    return (solution.reshape(1, 1, 1, block_count * block_rows, rhs_count), residual_norm)


def solution(mesh):
    torus = Mesh(
        mesh.devices.reshape(mesh.shape["gx"], mesh.shape["gy"], 4, 2), ("gx", "gy", "gz_0", "gz_1")
    )
    in_specs = (
        P("gx", "gy", GZ, None, None),
        P("gx", "gy", GZ, None),
        P("gx", "gy", GZ, None, None, None),
        P("gx", "gy", GZ, None, None),
        P("gx", "gy", GZ, None, None),
    )
    out_specs = (P("gx", "gy", GZ, None, None), P())
    return jax.shard_map(
        on_device, mesh=torus, in_specs=in_specs, out_specs=out_specs, check_vma=False
    )
```

profile of v0, /device:TPU:1, one launch (start us, length us, event | category | flops | bytes accessed | tf_op | source)
XLA Modules:
  0.0 271.4 jit_solution(16589500102011822868)
XLA Ops:
  13.6 4.5 %collective-permute-start.11 = (f32[1,2,128,256]{3,2,1,0:T(8,128)S(1)}, f32[1,2,128,256]{3,2,1,0:T(8,128)S(1)}, u32[]{:S(2)}, u32[]{:S(2)}) collective-permute-start(f32[1,2,128,256]{3,2,1,0:T(8,128)S(1)} %get-tuple-element.49), channel_id=1, source_target_pairs={{0,1},{1,2},{2,3},{3,4},{4,5},{5,6},{6,7},{8,9},{9,10},{10,11},{11... | collective-permute-start | bytes 786440 | tf_op jit(solution)/shard_map/ppermute | solution.py:23
  20.0 4.9 %collective-permute-start.7 = (f32[1,2,128,256]{3,2,1,0:T(8,128)S(1)}, f32[1,2,128,256]{3,2,1,0:T(8,128)S(1)}, u32[]{:S(2)}, u32[]{:S(2)}) collective-permute-start(f32[1,2,128,256]{3,2,1,0:T(8,128)S(1)} %copy-done.6), channel_id=1, source_target_pairs={{0,32},{32,64},{64,96},{96,128},{128,160},{160,192},{192,224},{1,3... | collective-permute-start | bytes 786440 | tf_op jit(solution)/shard_map/ppermute | solution.py:23
  28.0 4.0 %collective-permute-start.9 = (f32[1,2,128,256]{3,2,1,0:T(8,128)S(1)}, f32[1,2,128,256]{3,2,1,0:T(8,128)S(1)}, u32[]{:S(2)}, u32[]{:S(2)}) collective-permute-start(f32[1,2,128,256]{3,2,1,0:T(8,128)S(1)} %copy-done.4), channel_id=1, source_target_pairs={{0,8},{8,16},{16,24},{1,9},{9,17},{17,25},{2,10},{10,18},{18,26},{... | collective-permute-start | bytes 786440 | tf_op jit(solution)/shard_map/ppermute | solution.py:23
  32.7 4.5 %collective-permute-start.5 = (f32[1,2,128,256]{3,2,1,0:T(8,128)S(1)}, f32[1,2,128,256]{3,2,1,0:T(8,128)}, u32[]{:S(2)}, u32[]{:S(2)}) collective-permute-start(f32[1,2,128,256]{3,2,1,0:T(8,128)S(1)} %get-tuple-element.55), channel_id=1, source_target_pairs={{0,1},{1,2},{2,3},{3,4},{4,5},{5,6},{6,7},{8,9},{9,10},{10,11},{11... | collective-permute-start | bytes 786440 | tf_op jit(solution)/shard_map/ppermute | solution.py:23
  40.6 3.6 %collective-permute-start.1 = (f32[1,2,128,256]{3,2,1,0:T(8,128)S(1)}, f32[1,2,128,256]{3,2,1,0:T(8,128)S(1)}, u32[]{:S(2)}, u32[]{:S(2)}) collective-permute-start(f32[1,2,128,256]{3,2,1,0:T(8,128)S(1)} %get-tuple-element.59), channel_id=1, source_target_pairs={{0,32},{32,64},{64,96},{96,128},{128,160},{160,192},{192,224},{1,3... | collective-permute-start | bytes 786440 | tf_op jit(solution)/shard_map/ppermute | solution.py:23
  47.0 4.0 %collective-permute-start.3 = (f32[1,2,128,256]{3,2,1,0:T(8,128)S(1)}, f32[1,2,128,256]{3,2,1,0:T(8,128)S(1)}, u32[]{:S(2)}, u32[]{:S(2)}) collective-permute-start(f32[1,2,128,256]{3,2,1,0:T(8,128)S(1)} %get-tuple-element.57), channel_id=1, source_target_pairs={{0,8},{8,16},{16,24},{1,9},{9,17},{17,25},{2,10},{10,18},{18,26},{... | collective-permute-start | bytes 786440 | tf_op jit(solution)/shard_map/ppermute | solution.py:23
  54.7 4.5 %scatter_fusion.1 = f32[17,128,256]{2,1,0:T(8,128)} fusion(f32[17,128,256]{2,1,0:T(8,128)} %copy-done, s32[12]{0:T(128)S(1)} %fusion.26, f32[12,128,256]{2,1,0:T(8,128)} %bitcast.17), kind=kCustom, calls=%fused_computation.5 | custom fusion | flops 393216 | bytes 4718640 | tf_op jit(solution)/shard_map/scatter-add | solution.py:45
  66.4 3.1 %scatter_fusion = f32[17,128,256]{2,1,0:T(8,128)S(1)} fusion(f32[17,128,256]{2,1,0:T(8,128)S(1)} %pad_convert_fusion, s32[12]{0:T(128)S(1)} %fusion.26, f32[12,128,256]{2,1,0:T(8,128)} %bitcast.8), kind=kCustom, calls=%fused_computation.4 | custom fusion | flops 393216 | bytes 4718640 | tf_op jit(solution)/shard_map/scatter-add | solution.py:45
  69.5 4.7 %fusion.29 = (bf16[16,128,256]{2,1,0:T(8,128)(2,1)S(1)}, f32[16,128,256]{2,1,0:T(8,128)}) fusion(f32[17,128,256]{2,1,0:T(8,128)S(1)} %scatter_fusion, f32[16]{0:T(128)S(1)} %convert_element_type.26, f32[16,128,256]{2,1,0:T(8,128)} %slice.233), kind=kOutput, calls=%fused_computation.110 | convolution fusion | flops 806617088 | bytes 6292480 | tf_op jit(solution)/shard_map/bij,bjr->bir/dot_general | solution.py:70
  77.1 7.7 %fusion.13 = f32[2048,256]{0,1:T(8,128)} fusion(bf16[2048,256]{1,0:T(8,128)(2,1)S(1)} %bitcast.97, bf16[1,1,1,2048,2048]{4,3,2,1,0:T(8,128)(2,1)} %param.5, f32[2048,256]{0,1:T(8,128)} %copy.20, f32[2048]{0:T(1024)S(1)} %bitcast.99), kind=kOutput, calls=%fused_computation.15 | convolution fusion | flops 2148532224 | bytes 13639680 | tf_op jit(solution)/shard_map/dot_general | solution.py:75
  87.8 3.2 %concatenate.17 = f32[17,128,256]{2,1,0:T(8,128)} pad(f32[16,128,256]{2,1,0:T(8,128)} %bitcast.92, f32[]{:T(128)} %constant.4.clone.1), padding=0_1x0_0x0_0 | pad | bytes 4325380 | tf_op jit(solution)/shard_map/concatenate | solution.py:36
  91.0 3.4 %gather_fusion.2 = f32[12,128,256]{2,1,0:T(8,128)} fusion(f32[17,128,256]{2,1,0:T(8,128)} %concatenate.17, s32[1024]{0:T(1024)S(1)} %pad_clamp_fusion), kind=kCustom, calls=%fused_computation.2 | custom fusion | bytes 3145776 | tf_op jit(solution)/shard_map/gather | solution.py:38
  97.3 4.0 %collective-permute-start.13 = (f32[1,2,128,256]{3,2,1,0:T(8,128)S(1)}, f32[1,2,128,256]{3,2,1,0:T(8,128)S(1)}, u32[]{:S(2)}, u32[]{:S(2)}) collective-permute-start(f32[1,2,128,256]{3,2,1,0:T(8,128)S(1)} %get-tuple-element.47), channel_id=1, source_target_pairs={{0,32},{32,64},{64,96},{96,128},{128,160},{160,192},{192,224},{1,3... | collective-permute-start | bytes 786440 | tf_op jit(solution)/shard_map/ppermute | solution.py:23
  102.6 5.2 %collective-permute-start.17 = (f32[1,2,128,256]{3,2,1,0:T(8,128)S(1)}, f32[1,2,128,256]{3,2,1,0:T(8,128)S(1)}, u32[]{:S(2)}, u32[]{:S(2)}) collective-permute-start(f32[1,2,128,256]{3,2,1,0:T(8,128)S(1)} %get-tuple-element.43), channel_id=1, source_target_pairs={{0,1},{1,2},{2,3},{3,4},{4,5},{5,6},{6,7},{8,9},{9,10},{10,11},{11... | collective-permute-start | bytes 786440 | tf_op jit(solution)/shard_map/ppermute | solution.py:23
  109.7 4.5 %collective-permute-start.15 = (f32[1,2,128,256]{3,2,1,0:T(8,128)S(1)}, f32[1,2,128,256]{3,2,1,0:T(8,128)S(1)}, u32[]{:S(2)}, u32[]{:S(2)}) collective-permute-start(f32[1,2,128,256]{3,2,1,0:T(8,128)S(1)} %get-tuple-element.45), channel_id=1, source_target_pairs={{0,8},{8,16},{16,24},{1,9},{9,17},{17,25},{2,10},{10,18},{18,26},{... | collective-permute-start | bytes 786440 | tf_op jit(solution)/shard_map/ppermute | solution.py:23
  119.8 4.5 %scatter_fusion.2 = f32[17,128,256]{2,1,0:T(8,128)} fusion(f32[17,128,256]{2,1,0:T(8,128)} %concatenate.17, s32[12]{0:T(128)S(1)} %fusion.26, f32[12,128,256]{2,1,0:T(8,128)} %bitcast.30), kind=kCustom, calls=%fused_computation.6 | custom fusion | flops 393216 | bytes 4718640 | tf_op jit(solution)/shard_map/scatter-add | solution.py:45
  126.5 15.3 %all-reduce.6 = (f32[256]{0:T(256)S(1)}, f32[256]{0:T(256)S(1)}, f32[256]{0:T(256)S(1)}) all-reduce(f32[256]{0:T(256)S(1)} %broadcast_multiply_fusion.5, f32[256]{0:T(256)S(1)} %get-tuple-element.66, f32[256]{0:T(256)S(1)} %get-tuple-element.67), channel_id=1, replica_groups=mesh['gx'=8,'gy'=4,'gz_0'=4,'gz_1'=2] {'gx'}, use_global_device_ids=true, to_apply=%region_3.4 | all-reduce | flops 768 | bytes 6144 | tf_op jit(solution)/shard_map/psum | solution.py:30
  141.8 9.4 %all-reduce.10 = (f32[256]{0:T(256)S(1)}, f32[256]{0:T(256)S(1)}, f32[256]{0:T(256)S(1)}) all-reduce(f32[256]{0:T(256)S(1)} %get-tuple-element.11, f32[256]{0:T(256)S(1)} %get-tuple-element.12, f32[256]{0:T(256)S(1)} %get-tuple-element.13), channel_id=1, replica_groups=mesh['gx'=8,'gy'=4,'gz_0'=4,'gz_1'=2] {'gy'}, use_global_device_ids=true, to_apply=%region_4.5 | all-reduce | flops 768 | bytes 6144 | tf_op jit(solution)/shard_map/psum | solution.py:30
  151.2 8.9 %all-reduce.8 = (f32[256]{0:T(256)S(1)}, f32[256]{0:T(256)S(1)}, f32[256]{0:T(256)S(1)}) all-reduce(f32[256]{0:T(256)S(1)} %get-tuple-element.23, f32[256]{0:T(256)S(1)} %get-tuple-element.24, f32[256]{0:T(256)S(1)} %get-tuple-element.25), channel_id=1, replica_groups=mesh['gx'=8,'gy'=4,'gz_0'=4,'gz_1'=2] {'gz_0'}, use_global_device_ids=true, to_apply=%region_5.6 | all-reduce | flops 768 | bytes 6144 | tf_op jit(solution)/shard_map/psum | solution.py:30
  160.1 11.5 %all-reduce.12 = (f32[256]{0:T(256)S(1)}, f32[256]{0:T(256)S(1)}, f32[256]{0:T(256)S(1)}) all-reduce(f32[256]{0:T(256)S(1)} %get-tuple-element.17, f32[256]{0:T(256)S(1)} %get-tuple-element.18, f32[256]{0:T(256)S(1)} %get-tuple-element.19), channel_id=1, replica_groups=mesh['gx'=8,'gy'=4,'gz_0'=4,'gz_1'=2] {'gz_1'}, use_global_device_ids=true, to_apply=%region_6.7 | all-reduce | flops 768 | bytes 6144 | tf_op jit(solution)/shard_map/psum | solution.py:30
  174.0 3.3 %fusion.30 = (bf16[16,128,256]{2,1,0:T(8,128)(2,1)S(1)}, f32[16,128,256]{2,1,0:T(8,128)}) fusion(f32[16,128,256]{2,1,0:T(8,128)S(1)} %subtract_divide_fusion, f32[16,128,256]{2,1,0:T(8,128)S(1)} %copy-done.2, f32[16]{0:T(128)S(1)} %convert_element_type.26), kind=kOutput, calls=%fused_computation.111 | convolution fusion | flops 806092800 | bytes 6291968 | tf_op jit(solution)/shard_map/bij,bjr->bir/dot_general | solution.py:70
  180.3 7.7 %fusion.10 = f32[2048,256]{0,1:T(8,128)} fusion(bf16[2048,256]{1,0:T(8,128)(2,1)S(1)} %bitcast.95, bf16[1,1,1,2048,2048]{4,3,2,1,0:T(8,128)(2,1)} %param.5, f32[2048,256]{0,1:T(8,128)} %copy.24, f32[2048]{0:T(1024)S(1)} %bitcast.100), kind=kOutput, calls=%fused_computation.14 | convolution fusion | flops 2148532224 | bytes 13639680 | tf_op jit(solution)/shard_map/dot_general | solution.py:75
  190.9 3.2 %concatenate.18 = f32[17,128,256]{2,1,0:T(8,128)} pad(f32[16,128,256]{2,1,0:T(8,128)} %bitcast.91, f32[]{:T(128)} %constant.4.clone.1), padding=0_1x0_0x0_0 | pad | bytes 4325380 | tf_op jit(solution)/shard_map/concatenate | solution.py:36
  194.1 3.4 %gather_fusion.3 = f32[12,128,256]{2,1,0:T(8,128)} fusion(f32[17,128,256]{2,1,0:T(8,128)} %concatenate.18, s32[1024]{0:T(1024)S(1)} %pad_clamp_fusion), kind=kCustom, calls=%fused_computation.3 | custom fusion | bytes 3145776 | tf_op jit(solution)/shard_map/gather | solution.py:38
  200.4 4.0 %collective-permute-start.19 = (f32[1,2,128,256]{3,2,1,0:T(8,128)S(1)}, f32[1,2,128,256]{3,2,1,0:T(8,128)S(1)}, u32[]{:S(2)}, u32[]{:S(2)}) collective-permute-start(f32[1,2,128,256]{3,2,1,0:T(8,128)S(1)} %get-tuple-element.41), channel_id=1, source_target_pairs={{0,32},{32,64},{64,96},{96,128},{128,160},{160,192},{192,224},{1,3... | collective-permute-start | bytes 786440 | tf_op jit(solution)/shard_map/ppermute | solution.py:23
  210.5 4.3 %collective-permute-start.21 = (f32[1,2,128,256]{3,2,1,0:T(8,128)S(1)}, f32[1,2,128,256]{3,2,1,0:T(8,128)S(1)}, u32[]{:S(2)}, u32[]{:S(2)}) collective-permute-start(f32[1,2,128,256]{3,2,1,0:T(8,128)S(1)} %get-tuple-element.39), channel_id=1, source_target_pairs={{0,8},{8,16},{16,24},{1,9},{9,17},{17,25},{2,10},{10,18},{18,26},{... | collective-permute-start | bytes 786440 | tf_op jit(solution)/shard_map/ppermute | solution.py:23
  222.2 4.5 %scatter_fusion.3 = f32[17,128,256]{2,1,0:T(8,128)} fusion(f32[17,128,256]{2,1,0:T(8,128)} %concatenate.18, s32[12]{0:T(128)S(1)} %fusion.26, f32[12,128,256]{2,1,0:T(8,128)} %bitcast.41), kind=kCustom, calls=%fused_computation.7 | custom fusion | flops 393216 | bytes 4718640 | tf_op jit(solution)/shard_map/scatter-add | solution.py:45
  229.7 12.0 %all-reduce.5 = (f32[256]{0:T(256)S(1)}, f32[256]{0:T(256)S(1)}, f32[256]{0:T(256)S(1)}) all-reduce(f32[256]{0:T(256)S(1)} %broadcast_multiply_fusion.1, f32[256]{0:T(256)S(1)} %broadcast_multiply_fusion, f32[256]{0:T(256)S(1)} %broadcast_multiply_fusion.2), channel_id=1, replica_groups=mesh['gx'=8,'gy'=4,'gz_0'=4,'gz_1'=2] {'gx'}, use_global_device_ids=true, to_apply=%region_26.27 | all-reduce | flops 768 | bytes 6144 | tf_op jit(solution)/shard_map/psum | solution.py:30
  241.6 8.0 %all-reduce.9 = (f32[256]{0:T(256)S(1)}, f32[256]{0:T(256)S(1)}, f32[256]{0:T(256)S(1)}) all-reduce(f32[256]{0:T(256)S(1)} %get-tuple-element.8, f32[256]{0:T(256)S(1)} %get-tuple-element.9, f32[256]{0:T(256)S(1)} %get-tuple-element.10), channel_id=1, replica_groups=mesh['gx'=8,'gy'=4,'gz_0'=4,'gz_1'=2] {'gy'}, use_global_device_ids=true, to_apply=%region_27.28 | all-reduce | flops 768 | bytes 6144 | tf_op jit(solution)/shard_map/psum | solution.py:30
  249.7 6.0 %all-reduce.7 = (f32[256]{0:T(256)S(1)}, f32[256]{0:T(256)S(1)}, f32[256]{0:T(256)S(1)}) all-reduce(f32[256]{0:T(256)S(1)} %get-tuple-element.20, f32[256]{0:T(256)S(1)} %get-tuple-element.21, f32[256]{0:T(256)S(1)} %get-tuple-element.22), channel_id=1, replica_groups=mesh['gx'=8,'gy'=4,'gz_0'=4,'gz_1'=2] {'gz_0'}, use_global_device_ids=true, to_apply=%region_28.29 | all-reduce | flops 768 | bytes 6144 | tf_op jit(solution)/shard_map/psum | solution.py:30
  255.7 11.2 %all-reduce.11 = (f32[256]{0:T(256)S(1)}, f32[256]{0:T(256)S(1)}, f32[256]{0:T(256)S(1)}) all-reduce(f32[256]{0:T(256)S(1)} %get-tuple-element.14, f32[256]{0:T(256)S(1)} %get-tuple-element.15, f32[256]{0:T(256)S(1)} %get-tuple-element.16), channel_id=1, replica_groups=mesh['gx'=8,'gy'=4,'gz_0'=4,'gz_1'=2] {'gz_1'}, use_global_device_ids=true, to_apply=%region_29.30 | all-reduce | flops 768 | bytes 6144 | tf_op jit(solution)/shard_map/psum | solution.py:30
  267.5 3.9 %multiply_add_fusion = f32[16,128,256]{2,1,0:T(8,128)} fusion(f32[16,128,256]{2,1,0:T(8,128)} %get-tuple-element.65, f32[16,128,256]{2,1,0:T(8,128)} %get-tuple-element.63, f32[256]{0:T(256)S(1)} %get-tuple-element.33, f32[256]{0:T(256)S(1)} %get-tuple-element.32, f32[256]{0:T(256)S(1)} %get-tuple-element.36), kind=kLoop, calls=%fused_computation.19 | loop fusion | flops 2097152 | bytes 6294528 | tf_op jit(solution)/shard_map/add | solution.py:119
  (108 shorter events, 83.4 us)
Async XLA Ops:
  3.0 4.4 %copy-start = (f32[17,128,256]{2,1,0:T(8,128)}, f32[17,128,256]{2,1,0:T(8,128)S(1)}, u32[]{:S(2)}) copy-start(f32[17,128,256]{2,1,0:T(8,128)S(1)} %pad.14) | copy-start | bytes 6684676
  4.8 3.8 %copy-start.3 = (bf16[1,1,1,2048,256]{4,3,2,1,0:T(8,128)(2,1)S(1)}, bf16[1,1,1,2048,256]{4,3,2,1,0:T(8,128)(2,1)}, u32[]{:S(2)}) copy-start(bf16[1,1,1,2048,256]{4,3,2,1,0:T(8,128)(2,1)} %param.8) | copy-start | bytes 3145732
  7.3 17.7 %collective-permute-start.6 = (f32[1,2,128,256]{3,2,1,0:T(8,128)}, f32[1,2,128,256]{3,2,1,0:T(8,128)}, u32[]{:S(2)}, u32[]{:S(2)}) collective-permute-start(f32[1,2,128,256]{3,2,1,0:T(8,128)} %get-tuple-element.54), channel_id=1, source_target_pairs={{32,0},{64,32},{96,64},{128,96},{160,128},{192,160},{224,192},{33,... | collective-permute-start | bytes 786440 | tf_op jit(solution)/shard_map/ppermute | solution.py:24
  10.7 9.3 %copy-start.6 = (f32[1,2,128,256]{3,2,1,0:T(8,128)S(1)}, f32[1,2,128,256]{3,2,1,0:T(8,128)}, u32[]{:S(2)}) copy-start(f32[1,2,128,256]{3,2,1,0:T(8,128)} %get-tuple-element.53) | copy-start | bytes 786436
  10.7 14.3 %copy-start.7 = (s32[1,1,1,6,2]{3,4,2,1,0:T(2,128)S(1)}, s32[1,1,1,6,2]{3,4,2,1,0:T(2,128)}, u32[]{:S(2)}) copy-start(s32[1,1,1,6,2]{3,4,2,1,0:T(2,128)} %param.9) | copy-start | bytes 148
  10.7 14.4 %copy-start.5 = (f32[1,2,128,256]{3,2,1,0:T(8,128)S(1)}, f32[1,2,128,256]{3,2,1,0:T(8,128)}, u32[]{:S(2)}) copy-start(f32[1,2,128,256]{3,2,1,0:T(8,128)} %get-tuple-element.52) | copy-start | bytes 786436
  10.7 17.4 %copy-start.4 = (f32[1,2,128,256]{3,2,1,0:T(8,128)S(1)}, f32[1,2,128,256]{3,2,1,0:T(8,128)}, u32[]{:S(2)}) copy-start(f32[1,2,128,256]{3,2,1,0:T(8,128)} %get-tuple-element.51) | copy-start | bytes 786436
  12.3 15.8 %collective-permute-start = (f32[1,2,128,256]{3,2,1,0:T(8,128)S(1)}, f32[1,2,128,256]{3,2,1,0:T(8,128)S(1)}, u32[]{:S(2)}, u32[]{:S(2)}) collective-permute-start(f32[1,2,128,256]{3,2,1,0:T(8,128)S(1)} %get-tuple-element.60), channel_id=1, source_target_pairs={{32,0},{64,32},{96,64},{128,96},{160,128},{192,160},{224,192},{33,... | collective-permute-start | bytes 786440 | tf_op jit(solution)/shard_map/ppermute | solution.py:24
  13.6 33.4 %collective-permute-start.11 = (f32[1,2,128,256]{3,2,1,0:T(8,128)S(1)}, f32[1,2,128,256]{3,2,1,0:T(8,128)S(1)}, u32[]{:S(2)}, u32[]{:S(2)}) collective-permute-start(f32[1,2,128,256]{3,2,1,0:T(8,128)S(1)} %get-tuple-element.49), channel_id=1, source_target_pairs={{0,1},{1,2},{2,3},{3,4},{4,5},{5,6},{6,7},{8,9},{9,10},{10,11},{11... | collective-permute-start | bytes 786440 | tf_op jit(solution)/shard_map/ppermute | solution.py:23
  18.1 26.9 %collective-permute-start.10 = (f32[1,2,128,256]{3,2,1,0:T(8,128)S(1)}, f32[1,2,128,256]{3,2,1,0:T(8,128)S(1)}, u32[]{:S(2)}, u32[]{:S(2)}) collective-permute-start(f32[1,2,128,256]{3,2,1,0:T(8,128)S(1)} %get-tuple-element.50), channel_id=1, source_target_pairs={{1,0},{2,1},{3,2},{4,3},{5,4},{6,5},{7,6},{9,8},{10,9},{11,10},{12... | collective-permute-start | bytes 786440 | tf_op jit(solution)/shard_map/ppermute | solution.py:24
  20.0 12.7 %collective-permute-start.7 = (f32[1,2,128,256]{3,2,1,0:T(8,128)S(1)}, f32[1,2,128,256]{3,2,1,0:T(8,128)S(1)}, u32[]{:S(2)}, u32[]{:S(2)}) collective-permute-start(f32[1,2,128,256]{3,2,1,0:T(8,128)S(1)} %copy-done.6), channel_id=1, source_target_pairs={{0,32},{32,64},{64,96},{96,128},{128,160},{160,192},{192,224},{1,3... | collective-permute-start | bytes 786440 | tf_op jit(solution)/shard_map/ppermute | solution.py:23
  25.1 12.9 %collective-permute-start.8 = (f32[1,2,128,256]{3,2,1,0:T(8,128)S(1)}, f32[1,2,128,256]{3,2,1,0:T(8,128)S(1)}, u32[]{:S(2)}, u32[]{:S(2)}) collective-permute-start(f32[1,2,128,256]{3,2,1,0:T(8,128)S(1)} %copy-done.5), channel_id=1, source_target_pairs={{8,0},{16,8},{24,16},{9,1},{17,9},{25,17},{10,2},{18,10},{26,18},{... | collective-permute-start | bytes 786440 | tf_op jit(solution)/shard_map/ppermute | solution.py:24
  28.0 12.6 %collective-permute-start.9 = (f32[1,2,128,256]{3,2,1,0:T(8,128)S(1)}, f32[1,2,128,256]{3,2,1,0:T(8,128)S(1)}, u32[]{:S(2)}, u32[]{:S(2)}) collective-permute-start(f32[1,2,128,256]{3,2,1,0:T(8,128)S(1)} %copy-done.4), channel_id=1, source_target_pairs={{0,8},{8,16},{16,24},{1,9},{9,17},{17,25},{2,10},{10,18},{18,26},{... | collective-permute-start | bytes 786440 | tf_op jit(solution)/shard_map/ppermute | solution.py:23
  32.7 32.0 %collective-permute-start.5 = (f32[1,2,128,256]{3,2,1,0:T(8,128)S(1)}, f32[1,2,128,256]{3,2,1,0:T(8,128)}, u32[]{:S(2)}, u32[]{:S(2)}) collective-permute-start(f32[1,2,128,256]{3,2,1,0:T(8,128)S(1)} %get-tuple-element.55), channel_id=1, source_target_pairs={{0,1},{1,2},{2,3},{3,4},{4,5},{5,6},{6,7},{8,9},{9,10},{10,11},{11... | collective-permute-start | bytes 786440 | tf_op jit(solution)/shard_map/ppermute | solution.py:23
  38.0 25.1 %collective-permute-start.4 = (f32[1,2,128,256]{3,2,1,0:T(8,128)S(1)}, f32[1,2,128,256]{3,2,1,0:T(8,128)}, u32[]{:S(2)}, u32[]{:S(2)}) collective-permute-start(f32[1,2,128,256]{3,2,1,0:T(8,128)S(1)} %get-tuple-element.56), channel_id=1, source_target_pairs={{1,0},{2,1},{3,2},{4,3},{5,4},{6,5},{7,6},{9,8},{10,9},{11,10},{12... | collective-permute-start | bytes 786440 | tf_op jit(solution)/shard_map/ppermute | solution.py:24
  40.6 11.1 %collective-permute-start.1 = (f32[1,2,128,256]{3,2,1,0:T(8,128)S(1)}, f32[1,2,128,256]{3,2,1,0:T(8,128)S(1)}, u32[]{:S(2)}, u32[]{:S(2)}) collective-permute-start(f32[1,2,128,256]{3,2,1,0:T(8,128)S(1)} %get-tuple-element.59), channel_id=1, source_target_pairs={{0,32},{32,64},{64,96},{96,128},{128,160},{160,192},{192,224},{1,3... | collective-permute-start | bytes 786440 | tf_op jit(solution)/shard_map/ppermute | solution.py:23
  45.0 9.0 %collective-permute-start.2 = (f32[1,2,128,256]{3,2,1,0:T(8,128)S(1)}, f32[1,2,128,256]{3,2,1,0:T(8,128)S(1)}, u32[]{:S(2)}, u32[]{:S(2)}) collective-permute-start(f32[1,2,128,256]{3,2,1,0:T(8,128)S(1)} %get-tuple-element.58), channel_id=1, source_target_pairs={{8,0},{16,8},{24,16},{9,1},{17,9},{25,17},{10,2},{18,10},{26,18},{... | collective-permute-start | bytes 786440 | tf_op jit(solution)/shard_map/ppermute | solution.py:24
  47.0 15.3 %collective-permute-start.3 = (f32[1,2,128,256]{3,2,1,0:T(8,128)S(1)}, f32[1,2,128,256]{3,2,1,0:T(8,128)S(1)}, u32[]{:S(2)}, u32[]{:S(2)}) collective-permute-start(f32[1,2,128,256]{3,2,1,0:T(8,128)S(1)} %get-tuple-element.57), channel_id=1, source_target_pairs={{0,8},{8,16},{16,24},{1,9},{9,17},{17,25},{2,10},{10,18},{18,26},{... | collective-permute-start | bytes 786440 | tf_op jit(solution)/shard_map/ppermute | solution.py:23
  74.2 3.0 %copy-start.8 = (f32[1,1,1,2048]{3,2,1,0:T(1,128)S(1)}, f32[1,1,1,2048]{3,2,1,0:T(1,128)}, u32[]{:S(2)}) copy-start(f32[1,1,1,2048]{3,2,1,0:T(1,128)} %param.6) | copy-start | bytes 24580
  96.0 13.7 %collective-permute-start.12 = (f32[1,2,128,256]{3,2,1,0:T(8,128)S(1)}, f32[1,2,128,256]{3,2,1,0:T(8,128)S(1)}, u32[]{:S(2)}, u32[]{:S(2)}) collective-permute-start(f32[1,2,128,256]{3,2,1,0:T(8,128)S(1)} %get-tuple-element.48), channel_id=1, source_target_pairs={{32,0},{64,32},{96,64},{128,96},{160,128},{192,160},{224,192},{33,... | collective-permute-start | bytes 786440 | tf_op jit(solution)/shard_map/ppermute | solution.py:24
  97.3 17.6 %collective-permute-start.13 = (f32[1,2,128,256]{3,2,1,0:T(8,128)S(1)}, f32[1,2,128,256]{3,2,1,0:T(8,128)S(1)}, u32[]{:S(2)}, u32[]{:S(2)}) collective-permute-start(f32[1,2,128,256]{3,2,1,0:T(8,128)S(1)} %get-tuple-element.47), channel_id=1, source_target_pairs={{0,32},{32,64},{64,96},{96,128},{128,160},{160,192},{192,224},{1,3... | collective-permute-start | bytes 786440 | tf_op jit(solution)/shard_map/ppermute | solution.py:23
  101.3 14.4 %collective-permute-start.14 = (f32[1,2,128,256]{3,2,1,0:T(8,128)S(1)}, f32[1,2,128,256]{3,2,1,0:T(8,128)S(1)}, u32[]{:S(2)}, u32[]{:S(2)}) collective-permute-start(f32[1,2,128,256]{3,2,1,0:T(8,128)S(1)} %get-tuple-element.46), channel_id=1, source_target_pairs={{8,0},{16,8},{24,16},{9,1},{17,9},{25,17},{10,2},{18,10},{26,18},{... | collective-permute-start | bytes 786440 | tf_op jit(solution)/shard_map/ppermute | solution.py:24
  102.6 16.5 %collective-permute-start.17 = (f32[1,2,128,256]{3,2,1,0:T(8,128)S(1)}, f32[1,2,128,256]{3,2,1,0:T(8,128)S(1)}, u32[]{:S(2)}, u32[]{:S(2)}) collective-permute-start(f32[1,2,128,256]{3,2,1,0:T(8,128)S(1)} %get-tuple-element.43), channel_id=1, source_target_pairs={{0,1},{1,2},{2,3},{3,4},{4,5},{5,6},{6,7},{8,9},{9,10},{10,11},{11... | collective-permute-start | bytes 786440 | tf_op jit(solution)/shard_map/ppermute | solution.py:23
  107.8 10.5 %collective-permute-start.16 = (f32[1,2,128,256]{3,2,1,0:T(8,128)S(1)}, f32[1,2,128,256]{3,2,1,0:T(8,128)S(1)}, u32[]{:S(2)}, u32[]{:S(2)}) collective-permute-start(f32[1,2,128,256]{3,2,1,0:T(8,128)S(1)} %get-tuple-element.44), channel_id=1, source_target_pairs={{1,0},{2,1},{3,2},{4,3},{5,4},{6,5},{7,6},{9,8},{10,9},{11,10},{12... | collective-permute-start | bytes 786440 | tf_op jit(solution)/shard_map/ppermute | solution.py:24
  109.7 7.9 %collective-permute-start.15 = (f32[1,2,128,256]{3,2,1,0:T(8,128)S(1)}, f32[1,2,128,256]{3,2,1,0:T(8,128)S(1)}, u32[]{:S(2)}, u32[]{:S(2)}) collective-permute-start(f32[1,2,128,256]{3,2,1,0:T(8,128)S(1)} %get-tuple-element.45), channel_id=1, source_target_pairs={{0,8},{8,16},{16,24},{1,9},{9,17},{17,25},{2,10},{10,18},{18,26},{... | collective-permute-start | bytes 786440 | tf_op jit(solution)/shard_map/ppermute | solution.py:23
  174.0 3.3 %copy-start.1 = (f32[16,128,256]{2,1,0:T(8,128)}, f32[16,128,256]{2,1,0:T(8,128)S(1)}, u32[]{:S(2)}) copy-start(f32[16,128,256]{2,1,0:T(8,128)S(1)} %subtract_divide_fusion) | copy-start | bytes 6291460
  199.1 11.4 %collective-permute-start.18 = (f32[1,2,128,256]{3,2,1,0:T(8,128)S(1)}, f32[1,2,128,256]{3,2,1,0:T(8,128)S(1)}, u32[]{:S(2)}, u32[]{:S(2)}) collective-permute-start(f32[1,2,128,256]{3,2,1,0:T(8,128)S(1)} %get-tuple-element.42), channel_id=1, source_target_pairs={{32,0},{64,32},{96,64},{128,96},{160,128},{192,160},{224,192},{33,... | collective-permute-start | bytes 786440 | tf_op jit(solution)/shard_map/ppermute | solution.py:24
  200.4 15.1 %collective-permute-start.19 = (f32[1,2,128,256]{3,2,1,0:T(8,128)S(1)}, f32[1,2,128,256]{3,2,1,0:T(8,128)S(1)}, u32[]{:S(2)}, u32[]{:S(2)}) collective-permute-start(f32[1,2,128,256]{3,2,1,0:T(8,128)S(1)} %get-tuple-element.41), channel_id=1, source_target_pairs={{0,32},{32,64},{64,96},{96,128},{128,160},{160,192},{192,224},{1,3... | collective-permute-start | bytes 786440 | tf_op jit(solution)/shard_map/ppermute | solution.py:23
  204.4 11.8 %collective-permute-start.20 = (f32[1,2,128,256]{3,2,1,0:T(8,128)S(1)}, f32[1,2,128,256]{3,2,1,0:T(8,128)S(1)}, u32[]{:S(2)}, u32[]{:S(2)}) collective-permute-start(f32[1,2,128,256]{3,2,1,0:T(8,128)S(1)} %get-tuple-element.40), channel_id=1, source_target_pairs={{8,0},{16,8},{24,16},{9,1},{17,9},{25,17},{10,2},{18,10},{26,18},{... | collective-permute-start | bytes 786440 | tf_op jit(solution)/shard_map/ppermute | solution.py:24
  205.7 15.8 %collective-permute-start.23 = (f32[1,2,128,256]{3,2,1,0:T(8,128)S(1)}, f32[1,2,128,256]{3,2,1,0:T(8,128)S(1)}, u32[]{:S(2)}, u32[]{:S(2)}) collective-permute-start(f32[1,2,128,256]{3,2,1,0:T(8,128)S(1)} %get-tuple-element.37), channel_id=1, source_target_pairs={{0,1},{1,2},{2,3},{3,4},{4,5},{5,6},{6,7},{8,9},{9,10},{10,11},{11... | collective-permute-start | bytes 786440 | tf_op jit(solution)/shard_map/ppermute | solution.py:23
  208.6 12.2 %collective-permute-start.22 = (f32[1,2,128,256]{3,2,1,0:T(8,128)S(1)}, f32[1,2,128,256]{3,2,1,0:T(8,128)S(1)}, u32[]{:S(2)}, u32[]{:S(2)}) collective-permute-start(f32[1,2,128,256]{3,2,1,0:T(8,128)S(1)} %get-tuple-element.38), channel_id=1, source_target_pairs={{1,0},{2,1},{3,2},{4,3},{5,4},{6,5},{7,6},{9,8},{10,9},{11,10},{12... | collective-permute-start | bytes 786440 | tf_op jit(solution)/shard_map/ppermute | solution.py:24
  210.5 9.6 %collective-permute-start.21 = (f32[1,2,128,256]{3,2,1,0:T(8,128)S(1)}, f32[1,2,128,256]{3,2,1,0:T(8,128)S(1)}, u32[]{:S(2)}, u32[]{:S(2)}) collective-permute-start(f32[1,2,128,256]{3,2,1,0:T(8,128)S(1)} %get-tuple-element.39), channel_id=1, source_target_pairs={{0,8},{8,16},{16,24},{1,9},{9,17},{17,25},{2,10},{10,18},{18,26},{... | collective-permute-start | bytes 786440 | tf_op jit(solution)/shard_map/ppermute | solution.py:23
  (1 other events, 2.4 us)
where the time goes:
time: 273 us; the launch traced here: 271 us
  blocking collectives  82.3 us (30%)
  starting transfers between devices  68.3 us (25%)
  local copies, waits for them, and re-layouts  61.4 us (22%)
  other arithmetic  29 us (11%)
  matrix products  23.4 us (9%)
  waiting for transfers between devices  5.95 us (2%)
    psum x8, blocking collectives, one_axis_at_a_time(): return functools.reduce(lax.psum, axes, value)  82.3 us
    ppermute x12, starting transfers between devices, extended_2(): before = lax.ppermute(last, axis, up)  50.3 us
    ppermute x12, starting transfers between devices, extended_2(): after = lax.ppermute(leading, axis, down)  18 us
    unnamed x39, local copies, waits for them, and re-layouts  17.2 us
    scatter-add x4, other arithmetic, assemble(): extended.at[slot_flat]  16.6 us
    dot_general x2, matrix products, operate(): product = jnp.dot(matrix, narrow, preferred_element_type=jnp.float32)  15.4 us
    gather x4, local copies, waits for them, and re-layouts, assemble(): packed = extended[slot_flat].reshape(6, slot_count, block_rows, row_width)  10.5 us
    dot_general x2, matrix products, precondition(): jnp.einsum('bij,bjr->bir', summed, vector, precision=lax.Precision.HIGHEST)  7.94 us
  transfers between devices with their start and end apart: 24, of which 3 were waited for; matrix products, arithmetic and copies ran while one was open for 10% of the time, Pallas kernels for 0%

commit v1 on v0

v1 whole, which is shorter than its diff:
```python
import jax
import jax.numpy as jnp
from jax import lax
from jax.experimental import pallas as pl
from jax.experimental.pallas import tpu as pltpu
from jax.sharding import Mesh
from jax.sharding import PartitionSpec as P

GZ = ("gz_0", "gz_1")
INNER = ("gy", "gz_0", "gz_1")

epsilon = 1e-06
F32 = jnp.float32
BF16 = jnp.bfloat16
VMEM_MIB = 28


def call(body, outs, operands, scratch=(), smem=1, raw=()):
    specs = []
    operands = list(operands)
    for i in range(len(operands)):
        if i < smem:
            specs.append(pl.BlockSpec(memory_space=pltpu.SMEM))
        elif i in raw:
            specs.append(pl.BlockSpec(memory_space=pltpu.HBM))
            operands[i] = pltpu.with_memory_space_constraint(operands[i], pltpu.HBM)
        else:
            specs.append(pl.BlockSpec(memory_space=pltpu.VMEM))
    return pl.pallas_call(
        body,
        out_shape=[jax.ShapeDtypeStruct(s, t) for s, t in outs],
        in_specs=specs,
        out_specs=[pl.BlockSpec(memory_space=pltpu.VMEM) for _ in outs],
        scratch_shapes=list(scratch),
        compiler_params=pltpu.CompilerParams(vmem_limit_bytes=VMEM_MIB * 2**20),
    )(*operands)


def shifts(axis):
    n = lax.axis_size(axis)
    up = [(i, (i + 1) % n) for i in range(n)]
    return up, [(j, i) for i, j in up]


def exchange(faces):
    got = [None] * 6
    for a, axis in enumerate(("gx", "gy", GZ)):
        up, down = shifts(axis)
        got[2 * a] = lax.ppermute(faces[2 * a + 1], axis, down)
        got[2 * a + 1] = lax.ppermute(faces[2 * a], axis, up)
    return got


def exchange_once(messages):
    got = []
    for message, axis in zip(messages, ("gx", "gy")):
        n = lax.axis_size(axis)
        pairs = []
        for i in range(n):
            pairs += [(2 * i, 2 * ((i + 1) % n)), (2 * i + 1, 2 * ((i - 1) % n) + 1)]
        got.append(lax.ppermute(message, (axis, "gz_1"), pairs))
    got.append(lax.ppermute(messages[2], GZ, shifts(GZ)[0]))
    return got


def gather_sum(rows, axes):
    n = lax.axis_size(axes)
    wide = jnp.broadcast_to(rows[None], (n,) + rows.shape).reshape(n * rows.shape[0], rows.shape[1])
    wide = lax.all_to_all(wide, axes, 0, 0, tiled=True)
    return jnp.sum(wide.reshape((n,) + rows.shape), axis=0)


def total(rows):
    return gather_sum(gather_sum(rows, INNER), ("gx",))


def split(x):
    hi = x.astype(BF16)
    return hi, (x - hi.astype(F32)).astype(BF16)


def apply_block(mcat, vec):
    blk = mcat.shape[0]
    hi, lo = split(vec)
    out = jnp.dot(mcat, jnp.concatenate([hi, hi], axis=0), preferred_element_type=F32)
    return out + jnp.dot(mcat[:, :blk], lo, preferred_element_type=F32)


def column(row, blk):
    r = lax.broadcasted_iota(jnp.int32, (blk, blk), 0)
    c = lax.broadcasted_iota(jnp.int32, (blk, blk), 1)
    return jnp.sum(jnp.where(r == c, jnp.broadcast_to(row, (blk, blk)), 0.0), axis=1, keepdims=True)


def colsum(x):
    return jnp.sum(x, axis=0, keepdims=True)


def on_device(schur, interface_diag, precond, load, face_blocks):
    nblk, blk = precond.shape[3], precond.shape[4]
    cols = load.shape[-1]
    order = nblk * blk
    cap = face_blocks.shape[-1]
    slots = 6 * cap
    rows = cap * blk
    table = face_blocks.reshape(slots)
    core = lax.axis_index("gz_1").reshape(1).astype(jnp.int32)
    matrix = schur.reshape(order, order)
    diag = interface_diag.reshape(nblk, blk)

    def pick(table_ref, i):
        b = table_ref[i]
        return jnp.minimum(b, nblk - 1), (b < nblk).astype(F32), b

    def pack(table_ref, load_ref, pre_ref, *faces):
        for i in range(slots):
            b, m, _ = pick(table_ref, i)
            d, at = i // cap, (i % cap) * blk
            faces[d][at : at + blk, :cols] = load_ref[pl.ds(b * blk, blk), :].astype(F32) * m
            faces[d][at : at + blk, cols:] = pre_ref[b] * m

    faces = call(
        pack,
        [((rows, cols + blk), F32)] * 6,
        (table, load.reshape(order, cols), precond.reshape(nblk, blk, blk)),
    )
    came = exchange(faces)

    def spread(table_ref, zb_ref, i, value):
        b = table_ref[i]

        @pl.when(b < nblk)
        def _():
            zb_ref[pl.ds(pl.multiple_of(b * blk, blk), blk), :] = value.astype(BF16)

    def local_schur(table_ref, d, s_tile, zb_ref, z_ref, diag_ref):
        product = jnp.dot(s_tile, zb_ref[...], preferred_element_type=F32)
        parts = []
        for k in range(cap):
            i = d * cap + k
            b, m, _ = pick(table_ref, i)
            z = z_ref[i * blk : (i + 1) * blk, :]
            dcol = column(diag_ref[pl.ds(b, 1), :], blk)
            parts.append((product[k * blk : (k + 1) * blk] + dcol * z) * m)
        return parts

    def fetch(table_ref, matrix_ref, s_ref, sems):
        copies = []
        for i in range(slots):
            b, _, _ = pick(table_ref, i)
            copy = pltpu.make_async_copy(
                matrix_ref.at[pl.ds(pl.multiple_of(b * blk, blk), blk), :],
                s_ref.at[pl.ds(i * blk, blk), :],
                sems.at[i],
            )
            copy.start()
            copies.append(copy)
        return copies

    def first(table_ref, *refs):
        own, got = refs[:6], refs[6:12]
        diag_ref, matrix_ref = refs[12], refs[13]
        r_ref, z_ref, m_ref, sum_ref = refs[14:18]
        y_refs = refs[18:24]
        zb_ref, s_ref, sems = refs[24:27]
        copies = fetch(table_ref, matrix_ref, s_ref, sems)
        zb_ref[...] = jnp.zeros_like(zb_ref)
        square = jnp.zeros((1, cols), F32)
        for i in range(slots):
            d, at = i // cap, (i % cap) * blk
            r = own[d][at : at + blk, :cols] + got[d][at : at + blk, :cols]
            m = own[d][at : at + blk, cols:] + got[d][at : at + blk, cols:]
            hi, lo = split(m)
            mcat = jnp.concatenate([hi, lo], axis=1)
            m_ref[i * blk : (i + 1) * blk, :] = mcat
            r_ref[i * blk : (i + 1) * blk, :] = r
            square += colsum(r * r)
            z = apply_block(mcat, r)
            z_ref[i * blk : (i + 1) * blk, :] = z
            spread(table_ref, zb_ref, i, z)
        cross = jnp.zeros((1, cols), F32)
        for d in range(6):
            for k in range(cap):
                copies[d * cap + k].wait()
            parts = local_schur(
                table_ref, d, s_ref[d * rows : (d + 1) * rows, :], zb_ref, z_ref, diag_ref
            )
            for k in range(cap):
                i = d * cap + k
                y_refs[d][k * blk : (k + 1) * blk, :] = parts[k]
                cross += colsum(parts[k] * r_ref[i * blk : (i + 1) * blk, :])
        sum_ref[...] = jnp.zeros_like(sum_ref)
        sum_ref[0:1, :] = 0.5 * square
        sum_ref[1:2, :] = cross

    scratch = (
        pltpu.VMEM((order, cols), BF16),
        pltpu.VMEM((slots * blk, order), BF16),
        pltpu.SemaphoreType.DMA((slots,)),
    )
    r, z1, mcat, sums, *ys = call(
        first,
        [
            ((slots * blk, cols), F32),
            ((slots * blk, cols), F32),
            ((slots * blk, 2 * blk), BF16),
            ((8, cols), F32),
        ]
        + [((rows, cols), F32)] * 6,
        (table, *faces, *came, diag, matrix),
        scratch=scratch,
        raw=(14,),
    )
    came = exchange(ys)
    first_sums = total(sums)

    def second(table_ref, core_ref, *refs):
        own, got = refs[:6], refs[6:12]
        r_ref, m_ref, diag_ref, red_ref, matrix_ref = refs[12:17]
        z_ref, sum_ref = refs[17:19]
        y_refs, msgs = refs[19:25], refs[25:28]
        zb_ref, s_ref, sems, w_ref = refs[28:32]
        copies = fetch(table_ref, matrix_ref, s_ref, sems)
        inv = 1.0 / jnp.sqrt(red_ref[0:1, :] + epsilon)
        h11 = red_ref[1:2, :] * inv * inv
        zb_ref[...] = jnp.zeros_like(zb_ref)
        square = jnp.zeros((1, cols), F32)
        for i in range(slots):
            d, at = i // cap, (i % cap) * blk
            w = own[d][at : at + blk, :] + got[d][at : at + blk, :]
            w = (w - h11 * r_ref[i * blk : (i + 1) * blk, :]) * inv
            w_ref[i * blk : (i + 1) * blk, :] = w
            square += colsum(w * w)
            z = apply_block(m_ref[i * blk : (i + 1) * blk, :], w)
            z_ref[i * blk : (i + 1) * blk, :] = z
            spread(table_ref, zb_ref, i, z)
        on_first = jnp.zeros((1, cols), F32)
        on_second = jnp.zeros((1, cols), F32)
        low = core_ref[0] == 0
        for d in range(6):
            for k in range(cap):
                copies[d * cap + k].wait()
            parts = local_schur(
                table_ref, d, s_ref[d * rows : (d + 1) * rows, :], zb_ref, z_ref, diag_ref
            )
            for k in range(cap):
                i = d * cap + k
                y_refs[d][k * blk : (k + 1) * blk, :] = parts[k]
                on_first += colsum(parts[k] * r_ref[i * blk : (i + 1) * blk, :])
                on_second += colsum(parts[k] * w_ref[i * blk : (i + 1) * blk, :])
        for a in range(2):

            @pl.when(low)
            def _():
                msgs[a][...] = y_refs[2 * a][...]

            @pl.when(jnp.logical_not(low))
            def _():
                msgs[a][...] = y_refs[2 * a + 1][...]

        msgs[2][...] = y_refs[4][...]
        sum_ref[...] = jnp.zeros_like(sum_ref)
        sum_ref[0:1, :] = 0.5 * square
        sum_ref[1:2, :] = on_first * inv
        sum_ref[2:3, :] = on_second

    z2, sums, *rest = call(
        second,
        [((slots * blk, cols), F32), ((8, cols), F32)] + [((rows, cols), F32)] * 9,
        (table, core, *ys, *came, r, mcat, diag, first_sums, matrix),
        scratch=scratch + (pltpu.VMEM((slots * blk, cols), F32),),
        smem=2,
        raw=(18,),
    )
    ys, msgs = rest[:6], rest[6:]
    came = exchange_once(msgs)

    def norms(core_ref, *refs):
        own, got, in_ref, out_ref, acc_ref = refs[:6], refs[6:9], refs[9], refs[10], refs[11]
        low = core_ref[0] == 0
        out_ref[...] = in_ref[...]
        both = own[5][...] + got[2][...]
        acc_ref[...] = colsum(both * both)
        for a in range(2):

            @pl.when(low)
            def _():
                both = own[2 * a + 1][...] + got[a][...]
                acc_ref[...] += colsum(both * both)

            @pl.when(jnp.logical_not(low))
            def _():
                both = own[2 * a][...] + got[a][...]
                acc_ref[...] += colsum(both * both)

        out_ref[3:4, :] = acc_ref[...]

    (sums,) = call(
        norms,
        [((8, cols), F32)],
        (core, *ys, *came, sums),
        scratch=(pltpu.VMEM((1, cols), F32),),
    )
    second_sums = total(sums)

    def finish(table_ref, z1_ref, z2_ref, one_ref, two_ref, out_ref, res_ref):
        load_square = one_ref[0:1, :]
        initial = jnp.sqrt(load_square + epsilon)
        rescale = 1.0 / initial
        h11 = one_ref[1:2, :] * rescale * rescale
        w_square = two_ref[0:1, :]
        h21 = jnp.sqrt(w_square + epsilon)
        down = 1.0 / h21
        h12 = two_ref[1:2, :] * down
        dot22 = two_ref[2:3, :] * down * down
        square = two_ref[3:4, :] * down * down
        g11 = load_square * rescale * rescale
        g22 = w_square * down * down
        g12 = h11 * (epsilon * rescale * rescale) * down
        h22 = dot22 - h12 * g12
        left = square - h12 * h12 * (2.0 - g11) - h22 * (2.0 * dot22 - h22 * g22) + 2.0 * h12 * h22 * g12
        h32 = jnp.sqrt(jnp.maximum(left, 0.0) + epsilon)
        r1 = jnp.sqrt(h11 * h11 + h21 * h21)
        c1, s1 = h11 / r1, h21 / r1
        top = c1 * h12 + s1 * h22
        bottom = c1 * h22 - s1 * h12
        r2 = jnp.sqrt(bottom * bottom + h32 * h32)
        c2, s2 = bottom / r2, h32 / r2
        y2 = -initial * s1 * c2 / r2
        y1 = (initial * c1 - top * y2) / r1
        res_ref[...] = initial * s1 * s2
        a1 = y1 * rescale
        a2 = y2 * down
        out_ref[...] = jnp.zeros_like(out_ref)
        for i in range(slots):
            b = table_ref[i]

            @pl.when(b < nblk)
            def _():
                z = a1 * z1_ref[i * blk : (i + 1) * blk, :] + a2 * z2_ref[i * blk : (i + 1) * blk, :]
                out_ref[pl.ds(pl.multiple_of(b * blk, blk), blk), :] = z

    out, res = call(
        finish,
        [((order, cols), F32), ((1, cols), F32)],
        (table, z1, z2, first_sums, second_sums),
    )
    return out.reshape(1, 1, 1, order, cols), res.reshape(cols)


def solution(mesh):
    torus = Mesh(
        mesh.devices.reshape(mesh.shape["gx"], mesh.shape["gy"], 4, 2), ("gx", "gy", "gz_0", "gz_1")
    )
    in_specs = (
        P("gx", "gy", GZ, None, None),
        P("gx", "gy", GZ, None),
        P("gx", "gy", GZ, None, None, None),
        P("gx", "gy", GZ, None, None),
        P("gx", "gy", GZ, None, None),
    )
    out_specs = (P("gx", "gy", GZ, None, None), P())
    return jax.shard_map(
        on_device, mesh=torus, in_specs=in_specs, out_specs=out_specs, check_vma=False
    )
```

time: 273 us -> 125 us (0.46)
  blocking collectives: 82.3 us -> 27.5 us
  local copies, waits for them, and re-layouts: 61.4 us -> 17.5 us
  starting transfers between devices: 68.3 us -> 37.1 us
  other arithmetic: 29 us -> 1.04 us
  matrix products: 23.4 us -> 0 us
  Pallas kernels: 0 us -> 19.3 us
  waiting for transfers between devices: 5.95 us -> 21.1 us
    psum x8 -> x0, blocking collectives: 82.3 us -> none  [one_axis_at_a_time(): return functools.reduce(lax.psum, axes, value)]
    ppermute x24 -> x15, starting transfers between devices: 68.3 us -> 24.4 us  [the longest x6 10.6 us: exchange(): got[2 * a] = lax.ppermute(faces[2 * a + 1], axis, down)]
    all_to_all x0 -> x2, blocking collectives: none -> 27.5 us  [gather_sum(): wide = lax.all_to_all(wide, axes, 0, 0, tiled=True)]
    dot_general x4 -> x0, matrix products: 23.4 us -> none  [the longest x2 15.4 us: operate(): product = jnp.dot(matrix, narrow, preferred_element_type=jnp.float32)]
    pallas_call x0 -> x5, Pallas kernels: none -> 19.3 us  [call(): pl.pallas_call(body, out_shape=[jax.ShapeDtypeStruct(s, t) for s, t in ou...]
    scatter-add x4 -> x0, other arithmetic: 16.6 us -> none  [assemble(): extended.at[slot_flat]]
    all_to_all x0 -> x2, starting transfers between devices: none -> 12.7 us  [gather_sum(): wide = lax.all_to_all(wide, axes, 0, 0, tiled=True)]
    gather x4 -> x0, local copies, waits for them, and re-layouts: 10.5 us -> none  [assemble(): packed = extended[slot_flat].reshape(6, slot_count, block_rows, row_width)]
  transfers between devices with their start and end apart: 24 -> 17, of which waited for: 3 -> 8; matrix products, arithmetic and copies ran while one was open for 10% -> 2% of each run, Pallas kernels for 0% -> 0%
where the time goes in v1:
time: 125 us; the launch traced here: 124 us
  starting transfers between devices  37.1 us (30%)
  blocking collectives  27.5 us (22%)
  waiting for transfers between devices  21.1 us (17%)
  Pallas kernels  19.3 us (15%)
  local copies, waits for them, and re-layouts  17.5 us (14%)
    all_to_all x2, blocking collectives, gather_sum(): wide = lax.all_to_all(wide, axes, 0, 0, tiled=True)  27.5 us
    pallas_call x5, Pallas kernels, call(): pl.pallas_call(body, out_shape=[jax.ShapeDtypeStruct(s, t) for s, t in ou...  19.3 us
    unnamed x43, local copies, waits for them, and re-layouts  15.9 us
    all_to_all x2, starting transfers between devices, gather_sum(): wide = lax.all_to_all(wide, axes, 0, 0, tiled=True)  12.7 us
    ppermute x6, starting transfers between devices, exchange(): got[2 * a] = lax.ppermute(faces[2 * a + 1], axis, down)  10.6 us
    ppermute x6, starting transfers between devices, exchange(): got[2 * a + 1] = lax.ppermute(faces[2 * a], axis, up)  10.3 us
    all_to_all x2, waiting for transfers between devices, gather_sum(): wide = lax.all_to_all(wide, axes, 0, 0, tiled=True)  7.73 us
    ppermute x6, waiting for transfers between devices, exchange(): got[2 * a] = lax.ppermute(faces[2 * a + 1], axis, down)  5.49 us
  transfers between devices with their start and end apart: 17, of which 8 were waited for; matrix products, arithmetic and copies ran while one was open for 2% of the time, Pallas kernels for 0%

profile of v1, /device:TPU:1, one launch (start us, length us, event | category | flops | bytes accessed | tf_op | source)
XLA Modules:
  0.0 124.2 jit_solution(3600569810005872168)
XLA Ops:
  1.5 1.2 copy-done.2
  2.7 1.2 copy-done.3
  4.7 2.5 %collective-permute-start.1 = (f32[256,384]{1,0:T(8,128)S(1)}, f32[256,384]{1,0:T(8,128)S(1)}, u32[]{:S(2)}, u32[]{:S(2)}) collective-permute-start(f32[256,384]{1,0:T(8,128)S(1)} %get-tuple-element.31.refs_0_), channel_id=1, source_target_pairs={{0,32},{32,64},{64,96},{96,128},{128,160},{160,192},{192,224},{224... | collective-permute-start | bytes 1179656 | tf_op jit(solution)/shard_map/ppermute | solution.py:50
  7.2 4.0 %collective-permute-start = (f32[256,384]{1,0:T(8,128)S(1)}, f32[256,384]{1,0:T(8,128)S(1)}, u32[]{:S(2)}, u32[]{:S(2)}) collective-permute-start(f32[256,384]{1,0:T(8,128)S(1)} %get-tuple-element.32.refs_1_), channel_id=1, source_target_pairs={{32,0},{64,32},{96,64},{128,96},{160,128},{192,160},{224,192},{0,2... | collective-permute-start | bytes 1179656 | tf_op jit(solution)/shard_map/ppermute | solution.py:49
  11.2 1.3 %collective-permute-start.3 = (f32[256,384]{1,0:T(8,128)S(1)}, f32[256,384]{1,0:T(8,128)S(1)}, u32[]{:S(2)}, u32[]{:S(2)}) collective-permute-start(f32[256,384]{1,0:T(8,128)S(1)} %get-tuple-element.33.refs_2_), channel_id=1, source_target_pairs={{0,8},{8,16},{16,24},{24,0},{1,9},{9,17},{17,25},{25,1},{2,10},{10... | collective-permute-start | bytes 1179656 | tf_op jit(solution)/shard_map/ppermute | solution.py:50
  12.5 1.4 %collective-permute-start.2 = (f32[256,384]{1,0:T(8,128)S(1)}, f32[256,384]{1,0:T(8,128)S(1)}, u32[]{:S(2)}, u32[]{:S(2)}) collective-permute-start(f32[256,384]{1,0:T(8,128)S(1)} %get-tuple-element.34.refs_3_), channel_id=1, source_target_pairs={{8,0},{16,8},{24,16},{0,24},{9,1},{17,9},{25,17},{1,25},{10,2},{18... | collective-permute-start | bytes 1179656 | tf_op jit(solution)/shard_map/ppermute | solution.py:49
  14.0 2.6 %collective-permute-start.5 = (f32[256,384]{1,0:T(8,128)S(1)}, f32[256,384]{1,0:T(8,128)S(1)}, u32[]{:S(2)}, u32[]{:S(2)}) collective-permute-start(f32[256,384]{1,0:T(8,128)S(1)} %get-tuple-element.35.refs_4_), channel_id=1, source_target_pairs={{0,1},{1,2},{2,3},{3,4},{4,5},{5,6},{6,7},{7,0},{8,9},{9,10},{10,1... | collective-permute-start | bytes 1179656 | tf_op jit(solution)/shard_map/ppermute | solution.py:50
  16.5 3.4 %collective-permute-done.1.refs_7_ = f32[256,384]{1,0:T(8,128)S(1)} collective-permute-done((f32[256,384]{1,0:T(8,128)S(1)}, f32[256,384]{1,0:T(8,128)S(1)}, u32[]{:S(2)}, u32[]{:S(2)}) %collective-permute-start.1) | collective-permute-done | bytes 393248 | tf_op jit(solution)/shard_map/ppermute | solution.py:50
  19.9 1.3 %collective-permute-start.4 = (f32[256,384]{1,0:T(8,128)S(1)}, f32[256,384]{1,0:T(8,128)S(1)}, u32[]{:S(2)}, u32[]{:S(2)}) collective-permute-start(f32[256,384]{1,0:T(8,128)S(1)} %get-tuple-element.36.refs_5_), channel_id=1, source_target_pairs={{1,0},{2,1},{3,2},{4,3},{5,4},{6,5},{7,6},{0,7},{9,8},{10,9},{11,1... | collective-permute-start | bytes 1179656 | tf_op jit(solution)/shard_map/ppermute | solution.py:49
  21.2 1.1 collective-permute-done.3.refs_9_
  22.3 5.5 %collective-permute-done.4.refs_10_ = f32[256,384]{1,0:T(8,128)S(1)} collective-permute-done((f32[256,384]{1,0:T(8,128)S(1)}, f32[256,384]{1,0:T(8,128)S(1)}, u32[]{:S(2)}, u32[]{:S(2)}) %collective-permute-start.4) | collective-permute-done | bytes 393248 | tf_op jit(solution)/shard_map/ppermute | solution.py:49
  27.8 7.6 %shard_map.69 = (f32[1536,256]{1,0:T(8,128)S(1)}, f32[1536,256]{1,0:T(8,128)S(1)}, bf16[1536,256]{1,0:T(8,128)(2,1)S(1)}, f32[8,256]{1,0:T(8,128)S(1)}, f32[256,...) custom-call(s32[12]{0:T(128)S(1)} %reshape.56.table_ref, ...), custom_call_target="tpu_custom_call" | custom-call | tf_op jit(solution)/shard_map/pallas_call | solution.py:29
  35.3 1.1 copy-done
  38.3 7.6 %all-to-all-start = ((f32[32,8,256]{2,1,0:T(8,128)}), f32[32,8,256]{2,1,0:T(8,128)}, u32[]{:S(2)}, u32[]{:S(2)}) async-start(f32[32,8,256]{2,1,0:T(8,128)} %broadcast_in_dim.8), calls=%async_computation | async-start | bytes 524288 | tf_op jit(solution)/shard_map/all_to_all | solution.py:69
  45.9 2.6 %collective-permute-start.6 = (f32[256,256]{1,0:T(8,128)S(1)}, f32[256,256]{1,0:T(8,128)}, u32[]{:S(2)}, u32[]{:S(2)}) collective-permute-start(f32[256,256]{1,0:T(8,128)S(1)} %get-tuple-element.39.refs_1_), channel_id=1, source_target_pairs={{32,0},{64,32},{96,64},{128,96},{160,128},{192,160},{224,192},{0,2... | collective-permute-start | bytes 786440 | tf_op jit(solution)/shard_map/ppermute | solution.py:49
  48.5 1.4 %collective-permute-start.9 = (f32[256,256]{1,0:T(8,128)S(1)}, f32[256,256]{1,0:T(8,128)}, u32[]{:S(2)}, u32[]{:S(2)}) collective-permute-start(f32[256,256]{1,0:T(8,128)S(1)} %get-tuple-element.40.refs_2_), channel_id=1, source_target_pairs={{0,8},{8,16},{16,24},{24,0},{1,9},{9,17},{17,25},{25,1},{2,10},{10... | collective-permute-start | bytes 786440 | tf_op jit(solution)/shard_map/ppermute | solution.py:50
  49.9 1.3 %collective-permute-start.8 = (f32[256,256]{1,0:T(8,128)S(1)}, f32[256,256]{1,0:T(8,128)}, u32[]{:S(2)}, u32[]{:S(2)}) collective-permute-start(f32[256,256]{1,0:T(8,128)S(1)} %get-tuple-element.41.refs_3_), channel_id=1, source_target_pairs={{8,0},{16,8},{24,16},{0,24},{9,1},{17,9},{25,17},{1,25},{10,2},{18... | collective-permute-start | bytes 786440 | tf_op jit(solution)/shard_map/ppermute | solution.py:49
  51.2 2.5 %collective-permute-start.11 = (f32[256,256]{1,0:T(8,128)S(1)}, f32[256,256]{1,0:T(8,128)}, u32[]{:S(2)}, u32[]{:S(2)}) collective-permute-start(f32[256,256]{1,0:T(8,128)S(1)} %get-tuple-element.42.refs_4_), channel_id=1, source_target_pairs={{0,1},{1,2},{2,3},{3,4},{4,5},{5,6},{6,7},{7,0},{8,9},{9,10},{10,1... | collective-permute-start | bytes 786440 | tf_op jit(solution)/shard_map/ppermute | solution.py:50
  54.9 1.0 reduce_sum.36
  56.5 5.1 %all-to-all-start.1 = ((f32[8,8,256]{2,1,0:T(8,128)}), f32[8,8,256]{2,1,0:T(8,128)S(1)}, u32[]{:S(2)}, u32[]{:S(2)}) async-start(f32[8,8,256]{2,1,0:T(8,128)} %broadcast_in_dim.9), calls=%async_computation.1 | async-start | bytes 131072 | tf_op jit(solution)/shard_map/all_to_all | solution.py:69
  61.6 7.2 %all-to-all-done.1 = f32[8,8,256]{2,1,0:T(8,128)S(1)} async-done(((f32[8,8,256]{2,1,0:T(8,128)}), f32[8,8,256]{2,1,0:T(8,128)S(1)}, u32[]{:S(2)}, u32[]{:S(2)}) %all-to-all-start.1) | async-done | bytes 65568 | tf_op jit(solution)/shard_map/all_to_all | solution.py:69
  69.6 1.4 %copy-done.1 = f32[1536,256]{1,0:T(8,128)S(1)} copy-done((f32[1536,256]{1,0:T(8,128)S(1)}, f32[1536,256]{1,0:T(8,128)}, u32[]{:S(2)}) %copy-start.1) | copy-done | bytes 1572888
  71.0 1.1 copy-done.5
  72.2 0.9 copy-done.7
  78.8 8.6 %shard_map.70 = (f32[1536,256]{1,0:T(8,128)S(1)}, f32[8,256]{1,0:T(8,128)S(1)}, f32[256,256]{1,0:T(8,128)S(1)}, f32[256,256]{1,0:T(8,128)S(1)}, f32[256,256]{1,0...) custom-call(s32[12]{0:T(128)S(1)} %reshape.56.table_ref, ...), custom_call_target="tpu_custom_call" | custom-call | tf_op jit(solution)/shard_map/pallas_call | solution.py:29
  87.6 1.1 collective-permute-start.13
  88.7 2.2 %collective-permute-start.14 = (f32[256,256]{1,0:T(8,128)S(1)}, f32[256,256]{1,0:T(8,128)S(1)}, u32[]{:S(2)}, u32[]{:S(2)}) collective-permute-start(f32[256,256]{1,0:T(8,128)S(1)} %get-tuple-element.56), channel_id=1, source_target_pairs={{0,1},{1,2},{2,3},{3,4},{4,5},{5,6},{6,7},{7,0},{8,9},{9,10},{10,1... | collective-permute-start | bytes 786440 | tf_op jit(solution)/shard_map/ppermute | solution.py:62
  90.9 1.8 %collective-permute-done.12.refs_6_ = f32[256,256]{1,0:T(8,128)S(1)} collective-permute-done((f32[256,256]{1,0:T(8,128)S(1)}, f32[256,256]{1,0:T(8,128)S(1)}, u32[]{:S(2)}, u32[]{:S(2)}) %collective-permute-start.12) | collective-permute-done | bytes 262176 | tf_op jit(solution)/shard_map/ppermute | solution.py:61
  92.9 1.4 %collective-permute-done.14.refs_8_ = f32[256,256]{1,0:T(8,128)S(1)} collective-permute-done((f32[256,256]{1,0:T(8,128)S(1)}, f32[256,256]{1,0:T(8,128)S(1)}, u32[]{:S(2)}, u32[]{:S(2)}) %collective-permute-start.14) | collective-permute-done | bytes 262176 | tf_op jit(solution)/shard_map/ppermute | solution.py:62
  94.4 16.9 %all_to_all.24 = f32[32,8,256]{2,1,0:T(8,128)S(1)} all-to-all(f32[32,8,256]{2,1,0:T(8,128)S(1)} %broadcast_in_dim.10), channel_id=1, replica_groups=mesh['gx'=8,'gy'=4,'gz_0'=4,'gz_1'=2] {'gy','gz_0','gz_1'}, dimensions={0} | all-to-all | bytes 524288 | tf_op jit(solution)/shard_map/all_to_all | solution.py:69
  111.4 10.6 %all_to_all.25 = f32[8,8,256]{2,1,0:T(8,128)S(1)} all-to-all(f32[8,8,256]{2,1,0:T(8,128)S(1)} %broadcast_in_dim.11), channel_id=1, replica_groups=mesh['gx'=8,'gy'=4,'gz_0'=4,'gz_1'=2] {'gx'}, dimensions={0} | all-to-all | bytes 131072 | tf_op jit(solution)/shard_map/all_to_all | solution.py:69
  122.0 2.2 %shard_map.72 = (f32[2048,256]{1,0:T(8,128)}, f32[1,256]{1,0:T(1,128)}) custom-call(s32[12]{0:T(128)S(1)} %reshape.56.table_ref, f32[1536,256]{1,0:T(8,128)S(1)} %get-tuple-element.37.z1_ref, f32[1536,256]{1,0:T(8,128)S(1)} %get-tuple-element.47.z2_ref, f32[8,256]{1,0:T(8,128)S(1)} %reduce_sum.37.refs_15_.one_ref, f32[8,256]{1,0:T(8,128)S(1)} %reduce_sum.39.two_ref), custom_call_target="tpu_custom_call" | custom-call | tf_op jit(solution)/shard_map/pallas_call | solution.py:29
  (61 shorter events, 12.1 us)
Async XLA Ops:
  0.6 27.1 %copy-start.20 = (f32[1,1,1,2048]{3,2,1,0:T(1,128)S(1)}, f32[1,1,1,2048]{3,2,1,0:T(1,128)}, u32[]{:S(2)}) copy-start(f32[1,1,1,2048]{3,2,1,0:T(1,128)} %param.6) | copy-start | bytes 24580
  1.5 1.2 copy-start.2
  2.7 1.2 copy-start.3
  4.7 15.3 %collective-permute-start.1 = (f32[256,384]{1,0:T(8,128)S(1)}, f32[256,384]{1,0:T(8,128)S(1)}, u32[]{:S(2)}, u32[]{:S(2)}) collective-permute-start(f32[256,384]{1,0:T(8,128)S(1)} %get-tuple-element.31.refs_0_), channel_id=1, source_target_pairs={{0,32},{32,64},{64,96},{96,128},{128,160},{160,192},{192,224},{224... | collective-permute-start | bytes 1179656 | tf_op jit(solution)/shard_map/ppermute | solution.py:50
  7.2 14.0 %collective-permute-start = (f32[256,384]{1,0:T(8,128)S(1)}, f32[256,384]{1,0:T(8,128)S(1)}, u32[]{:S(2)}, u32[]{:S(2)}) collective-permute-start(f32[256,384]{1,0:T(8,128)S(1)} %get-tuple-element.32.refs_1_), channel_id=1, source_target_pairs={{32,0},{64,32},{96,64},{128,96},{160,128},{192,160},{224,192},{0,2... | collective-permute-start | bytes 1179656 | tf_op jit(solution)/shard_map/ppermute | solution.py:49
  11.2 11.1 %collective-permute-start.3 = (f32[256,384]{1,0:T(8,128)S(1)}, f32[256,384]{1,0:T(8,128)S(1)}, u32[]{:S(2)}, u32[]{:S(2)}) collective-permute-start(f32[256,384]{1,0:T(8,128)S(1)} %get-tuple-element.33.refs_2_), channel_id=1, source_target_pairs={{0,8},{8,16},{16,24},{24,0},{1,9},{9,17},{17,25},{25,1},{2,10},{10... | collective-permute-start | bytes 1179656 | tf_op jit(solution)/shard_map/ppermute | solution.py:50
  12.5 9.8 %collective-permute-start.2 = (f32[256,384]{1,0:T(8,128)S(1)}, f32[256,384]{1,0:T(8,128)S(1)}, u32[]{:S(2)}, u32[]{:S(2)}) collective-permute-start(f32[256,384]{1,0:T(8,128)S(1)} %get-tuple-element.34.refs_3_), channel_id=1, source_target_pairs={{8,0},{16,8},{24,16},{0,24},{9,1},{17,9},{25,17},{1,25},{10,2},{18... | collective-permute-start | bytes 1179656 | tf_op jit(solution)/shard_map/ppermute | solution.py:49
  14.0 8.3 %collective-permute-start.5 = (f32[256,384]{1,0:T(8,128)S(1)}, f32[256,384]{1,0:T(8,128)S(1)}, u32[]{:S(2)}, u32[]{:S(2)}) collective-permute-start(f32[256,384]{1,0:T(8,128)S(1)} %get-tuple-element.35.refs_4_), channel_id=1, source_target_pairs={{0,1},{1,2},{2,3},{3,4},{4,5},{5,6},{6,7},{7,0},{8,9},{9,10},{10,1... | collective-permute-start | bytes 1179656 | tf_op jit(solution)/shard_map/ppermute | solution.py:50
  19.9 7.8 %collective-permute-start.4 = (f32[256,384]{1,0:T(8,128)S(1)}, f32[256,384]{1,0:T(8,128)S(1)}, u32[]{:S(2)}, u32[]{:S(2)}) collective-permute-start(f32[256,384]{1,0:T(8,128)S(1)} %get-tuple-element.36.refs_5_), channel_id=1, source_target_pairs={{1,0},{2,1},{3,2},{4,3},{5,4},{6,5},{7,6},{0,7},{9,8},{10,9},{11,1... | collective-permute-start | bytes 1179656 | tf_op jit(solution)/shard_map/ppermute | solution.py:49
  35.3 1.1 copy-start
  37.4 32.2 %copy-start.6 = (f32[256,256]{1,0:T(8,128)}, f32[256,256]{1,0:T(8,128)S(1)}, u32[]{:S(2)}) copy-start(f32[256,256]{1,0:T(8,128)S(1)} %get-tuple-element.39.refs_1_) | copy-start | bytes 786436
  37.4 32.2 %copy-start.8 = (f32[256,256]{1,0:T(8,128)}, f32[256,256]{1,0:T(8,128)S(1)}, u32[]{:S(2)}) copy-start(f32[256,256]{1,0:T(8,128)S(1)} %get-tuple-element.40.refs_2_) | copy-start | bytes 786436
  37.4 32.2 %copy-start.10 = (f32[256,256]{1,0:T(8,128)}, f32[256,256]{1,0:T(8,128)S(1)}, u32[]{:S(2)}) copy-start(f32[256,256]{1,0:T(8,128)S(1)} %get-tuple-element.41.refs_3_) | copy-start | bytes 786436
  37.4 32.2 %copy-start.12 = (f32[256,256]{1,0:T(8,128)}, f32[256,256]{1,0:T(8,128)S(1)}, u32[]{:S(2)}) copy-start(f32[256,256]{1,0:T(8,128)S(1)} %get-tuple-element.42.refs_4_) | copy-start | bytes 786436
  37.4 32.2 %copy-start.14 = (f32[256,256]{1,0:T(8,128)}, f32[256,256]{1,0:T(8,128)S(1)}, u32[]{:S(2)}) copy-start(f32[256,256]{1,0:T(8,128)S(1)} %get-tuple-element.43.refs_5_) | copy-start | bytes 786436
  37.4 16.3 %collective-permute-start.7 = (f32[256,256]{1,0:T(8,128)S(1)}, f32[256,256]{1,0:T(8,128)S(1)}, u32[]{:S(2)}, u32[]{:S(2)}) collective-permute-start(f32[256,256]{1,0:T(8,128)S(1)} %get-tuple-element.38.refs_0_), channel_id=1, source_target_pairs={{0,32},{32,64},{64,96},{96,128},{128,160},{160,192},{192,224},{224... | collective-permute-start | bytes 786440 | tf_op jit(solution)/shard_map/ppermute | solution.py:50
  38.3 16.5 %all-to-all-start = ((f32[32,8,256]{2,1,0:T(8,128)}), f32[32,8,256]{2,1,0:T(8,128)}, u32[]{:S(2)}, u32[]{:S(2)}) async-start(f32[32,8,256]{2,1,0:T(8,128)} %broadcast_in_dim.8), calls=%async_computation | async-start | bytes 524288 | tf_op jit(solution)/shard_map/all_to_all | solution.py:69
  45.9 22.9 %collective-permute-start.6 = (f32[256,256]{1,0:T(8,128)S(1)}, f32[256,256]{1,0:T(8,128)}, u32[]{:S(2)}, u32[]{:S(2)}) collective-permute-start(f32[256,256]{1,0:T(8,128)S(1)} %get-tuple-element.39.refs_1_), channel_id=1, source_target_pairs={{32,0},{64,32},{96,64},{128,96},{160,128},{192,160},{224,192},{0,2... | collective-permute-start | bytes 786440 | tf_op jit(solution)/shard_map/ppermute | solution.py:49
  48.5 20.3 %collective-permute-start.9 = (f32[256,256]{1,0:T(8,128)S(1)}, f32[256,256]{1,0:T(8,128)}, u32[]{:S(2)}, u32[]{:S(2)}) collective-permute-start(f32[256,256]{1,0:T(8,128)S(1)} %get-tuple-element.40.refs_2_), channel_id=1, source_target_pairs={{0,8},{8,16},{16,24},{24,0},{1,9},{9,17},{17,25},{25,1},{2,10},{10... | collective-permute-start | bytes 786440 | tf_op jit(solution)/shard_map/ppermute | solution.py:50
  49.9 19.0 %collective-permute-start.8 = (f32[256,256]{1,0:T(8,128)S(1)}, f32[256,256]{1,0:T(8,128)}, u32[]{:S(2)}, u32[]{:S(2)}) collective-permute-start(f32[256,256]{1,0:T(8,128)S(1)} %get-tuple-element.41.refs_3_), channel_id=1, source_target_pairs={{8,0},{16,8},{24,16},{0,24},{9,1},{17,9},{25,17},{1,25},{10,2},{18... | collective-permute-start | bytes 786440 | tf_op jit(solution)/shard_map/ppermute | solution.py:49
  51.2 17.7 %collective-permute-start.11 = (f32[256,256]{1,0:T(8,128)S(1)}, f32[256,256]{1,0:T(8,128)}, u32[]{:S(2)}, u32[]{:S(2)}) collective-permute-start(f32[256,256]{1,0:T(8,128)S(1)} %get-tuple-element.42.refs_4_), channel_id=1, source_target_pairs={{0,1},{1,2},{2,3},{3,4},{4,5},{5,6},{6,7},{7,0},{8,9},{9,10},{10,1... | collective-permute-start | bytes 786440 | tf_op jit(solution)/shard_map/ppermute | solution.py:50
  54.4 14.5 %collective-permute-start.10 = (f32[256,256]{1,0:T(8,128)S(1)}, f32[256,256]{1,0:T(8,128)S(1)}, u32[]{:S(2)}, u32[]{:S(2)}) collective-permute-start(f32[256,256]{1,0:T(8,128)S(1)} %get-tuple-element.43.refs_5_), channel_id=1, source_target_pairs={{1,0},{2,1},{3,2},{4,3},{5,4},{6,5},{7,6},{0,7},{9,8},{10,9},{11,1... | collective-permute-start | bytes 786440 | tf_op jit(solution)/shard_map/ppermute | solution.py:49
  56.5 12.3 %all-to-all-start.1 = ((f32[8,8,256]{2,1,0:T(8,128)}), f32[8,8,256]{2,1,0:T(8,128)S(1)}, u32[]{:S(2)}, u32[]{:S(2)}) async-start(f32[8,8,256]{2,1,0:T(8,128)} %broadcast_in_dim.9), calls=%async_computation.1 | async-start | bytes 131072 | tf_op jit(solution)/shard_map/all_to_all | solution.py:69
  69.6 1.4 %copy-start.1 = (f32[1536,256]{1,0:T(8,128)S(1)}, f32[1536,256]{1,0:T(8,128)}, u32[]{:S(2)}) copy-start(f32[1536,256]{1,0:T(8,128)} %copy-done) | copy-start | bytes 4718596
  71.0 1.1 copy-start.5
  72.2 0.9 copy-start.7
  73.1 0.9 copy-start.9
  74.1 0.9 copy-start.11
  75.0 0.9 copy-start.13
  87.5 5.3 %collective-permute-start.12 = (f32[256,256]{1,0:T(8,128)S(1)}, f32[256,256]{1,0:T(8,128)S(1)}, u32[]{:S(2)}, u32[]{:S(2)}) collective-permute-start(f32[256,256]{1,0:T(8,128)S(1)} %get-tuple-element.54), channel_id=1, source_target_pairs={{0,32},{1,225},{32,64},{33,1},{64,96},{65,33},{96,128},{97,65},{12... | collective-permute-start | bytes 786440 | tf_op jit(solution)/shard_map/ppermute | solution.py:61
  87.6 5.3 %collective-permute-start.13 = (f32[256,256]{1,0:T(8,128)S(1)}, f32[256,256]{1,0:T(8,128)S(1)}, u32[]{:S(2)}, u32[]{:S(2)}) collective-permute-start(f32[256,256]{1,0:T(8,128)S(1)} %get-tuple-element.55), channel_id=1, source_target_pairs={{0,8},{1,25},{8,16},{9,1},{16,24},{17,9},{24,0},{25,17},{2,10},{3,... | collective-permute-start | bytes 786440 | tf_op jit(solution)/shard_map/ppermute | solution.py:61
  88.7 5.5 %collective-permute-start.14 = (f32[256,256]{1,0:T(8,128)S(1)}, f32[256,256]{1,0:T(8,128)S(1)}, u32[]{:S(2)}, u32[]{:S(2)}) collective-permute-start(f32[256,256]{1,0:T(8,128)S(1)} %get-tuple-element.56), channel_id=1, source_target_pairs={{0,1},{1,2},{2,3},{3,4},{4,5},{5,6},{6,7},{7,0},{8,9},{9,10},{10,1... | collective-permute-start | bytes 786440 | tf_op jit(solution)/shard_map/ppermute | solution.py:62
  (6 other events, 5.1 us)

commit v2 on v1

--- a/solution.py
+++ b/solution.py
@@ -12,10 +12,9 @@
 epsilon = 1e-06
 F32 = jnp.float32
 BF16 = jnp.bfloat16
-VMEM_MIB = 28
-
-
-def call(body, outs, operands, scratch=(), smem=1, raw=()):
+
+
+def call(body, outs, operands, scratch=(), smem=1, raw=(), flops=0, mib=16):
     specs = []
     operands = list(operands)
     for i in range(len(operands)):
@@ -32,7 +31,8 @@
         in_specs=specs,
         out_specs=[pl.BlockSpec(memory_space=pltpu.VMEM) for _ in outs],
         scratch_shapes=list(scratch),
-        compiler_params=pltpu.CompilerParams(vmem_limit_bytes=VMEM_MIB * 2**20),
+        compiler_params=pltpu.CompilerParams(vmem_limit_bytes=mib * 2**20),
+        cost_estimate=pl.CostEstimate(flops=flops, transcendentals=0, bytes_accessed=2**20),
     )(*operands)
 
 
@@ -103,51 +103,54 @@
     cap = face_blocks.shape[-1]
     slots = 6 * cap
     rows = cap * blk
-    table = face_blocks.reshape(slots)
-    core = lax.axis_index("gz_1").reshape(1).astype(jnp.int32)
+    table = face_blocks.reshape(6, cap).T
     matrix = schur.reshape(order, order)
     diag = interface_diag.reshape(nblk, blk)
 
     def pick(table_ref, i):
-        b = table_ref[i]
-        return jnp.minimum(b, nblk - 1), (b < nblk).astype(F32), b
-
-    def pack(table_ref, load_ref, pre_ref, *faces):
-        for i in range(slots):
-            b, m, _ = pick(table_ref, i)
+        b = table_ref[i % cap, i // cap]
+        return jnp.minimum(b, nblk - 1), (b < nblk).astype(F32)
+
+    def pack(table_ref, load_ref, pre_ref, *refs):
+        faces, (load_buf, pre_buf, load_sems, pre_sems) = refs[:6], refs[6:]
+        copies = []
+        for i in range(slots):
+            b, _ = pick(table_ref, i)
+            at = pl.multiple_of(b * blk, blk)
+            copies.append(
+                (
+                    pltpu.make_async_copy(load_ref.at[pl.ds(at, blk), :], load_buf.at[i], load_sems.at[i]),
+                    pltpu.make_async_copy(pre_ref.at[b], pre_buf.at[i], pre_sems.at[i]),
+                )
+            )
+            for copy in copies[-1]:
+                copy.start()
+        for i in range(slots):
+            _, m = pick(table_ref, i)
             d, at = i // cap, (i % cap) * blk
-            faces[d][at : at + blk, :cols] = load_ref[pl.ds(b * blk, blk), :].astype(F32) * m
-            faces[d][at : at + blk, cols:] = pre_ref[b] * m
+            for copy in copies[i]:
+                copy.wait()
+            faces[d][at : at + blk, :cols] = load_buf[i].astype(F32) * m
+            faces[d][at : at + blk, cols:] = pre_buf[i] * m
 
     faces = call(
         pack,
         [((rows, cols + blk), F32)] * 6,
         (table, load.reshape(order, cols), precond.reshape(nblk, blk, blk)),
+        scratch=(
+            pltpu.VMEM((slots, blk, cols), BF16),
+            pltpu.VMEM((slots, blk, blk), F32),
+            pltpu.SemaphoreType.DMA((slots,)),
+            pltpu.SemaphoreType.DMA((slots,)),
+        ),
+        raw=(1, 2),
     )
     came = exchange(faces)
-
-    def spread(table_ref, zb_ref, i, value):
-        b = table_ref[i]
-
-        @pl.when(b < nblk)
-        def _():
-            zb_ref[pl.ds(pl.multiple_of(b * blk, blk), blk), :] = value.astype(BF16)
-
-    def local_schur(table_ref, d, s_tile, zb_ref, z_ref, diag_ref):
-        product = jnp.dot(s_tile, zb_ref[...], preferred_element_type=F32)
-        parts = []
-        for k in range(cap):
-            i = d * cap + k
-            b, m, _ = pick(table_ref, i)
-            z = z_ref[i * blk : (i + 1) * blk, :]
-            dcol = column(diag_ref[pl.ds(b, 1), :], blk)
-            parts.append((product[k * blk : (k + 1) * blk] + dcol * z) * m)
-        return parts
 
     def fetch(table_ref, matrix_ref, s_ref, sems):
         copies = []
         for i in range(slots):
-            b, _, _ = pick(table_ref, i)
+            b, _ = pick(table_ref, i)
             copy = pltpu.make_async_copy(
                 matrix_ref.at[pl.ds(pl.multiple_of(b * blk, blk), blk), :],
                 s_ref.at[pl.ds(i * blk, blk), :],
@@ -155,15 +158,42 @@
             )
             copy.start()
             copies.append(copy)
-        return copies
+        for copy in copies:
+            copy.wait()
+
+    (sel,) = call(
+        fetch,
+        [((slots * blk, order), BF16)],
+        (table, matrix),
+        scratch=(pltpu.SemaphoreType.DMA((slots,)),),
+        raw=(1,),
+        flops=2 * 10**9,
+    )
+
+    def spread(table_ref, zb_ref, i, value):
+        b = table_ref[i % cap, i // cap]
+
+        @pl.when(b < nblk)
+        def _():
+            zb_ref[pl.ds(pl.multiple_of(b * blk, blk), blk), :] = value.astype(BF16)
+
+    def local_schur(table_ref, d, s_tile, zb_ref, z_ref, diag_ref):
+        product = jnp.dot(s_tile, zb_ref[...], preferred_element_type=F32)
+        parts = []
+        for k in range(cap):
+            i = d * cap + k
+            b, m = pick(table_ref, i)
+            z = z_ref[i * blk : (i + 1) * blk, :]
+            dcol = column(diag_ref[pl.ds(b, 1), :], blk)
+            parts.append((product[k * blk : (k + 1) * blk] + dcol * z) * m)
+        return parts
 
     def first(table_ref, *refs):
         own, got = refs[:6], refs[6:12]
-        diag_ref, matrix_ref = refs[12], refs[13]
+        diag_ref, s_ref = refs[12:14]
         r_ref, z_ref, m_ref, sum_ref = refs[14:18]
         y_refs = refs[18:24]
-        zb_ref, s_ref, sems = refs[24:27]
-        copies = fetch(table_ref, matrix_ref, s_ref, sems)
+        zb_ref = refs[24]
         zb_ref[...] = jnp.zeros_like(zb_ref)
         square = jnp.zeros((1, cols), F32)
         for i in range(slots):
@@ -180,8 +210,6 @@
             spread(table_ref, zb_ref, i, z)
         cross = jnp.zeros((1, cols), F32)
         for d in range(6):
-            for k in range(cap):
-                copies[d * cap + k].wait()
             parts = local_schur(
                 table_ref, d, s_ref[d * rows : (d + 1) * rows, :], zb_ref, z_ref, diag_ref
             )
@@ -193,42 +221,29 @@
         sum_ref[0:1, :] = 0.5 * square
         sum_ref[1:2, :] = cross
 
-    scratch = (
-        pltpu.VMEM((order, cols), BF16),
-        pltpu.VMEM((slots * blk, order), BF16),
-        pltpu.SemaphoreType.DMA((slots,)),
-    )
+    spread_z = (pltpu.VMEM((order, cols), BF16),)
+    long = slots * blk
     r, z1, mcat, sums, *ys = call(
         first,
-        [
-            ((slots * blk, cols), F32),
-            ((slots * blk, cols), F32),
-            ((slots * blk, 2 * blk), BF16),
-            ((8, cols), F32),
-        ]
+        [((long, cols), F32), ((long, cols), F32), ((long, 2 * blk), BF16), ((8, cols), F32)]
         + [((rows, cols), F32)] * 6,
-        (table, *faces, *came, diag, matrix),
-        scratch=scratch,
-        raw=(14,),
+        (table, *faces, *came, diag, sel),
+        scratch=spread_z,
+        flops=2 * 10**9,
     )
     came = exchange(ys)
-    first_sums = total(sums)
-
-    def second(table_ref, core_ref, *refs):
+
+    def second(table_ref, *refs):
         own, got = refs[:6], refs[6:12]
-        r_ref, m_ref, diag_ref, red_ref, matrix_ref = refs[12:17]
+        r_ref, m_ref, diag_ref, in_ref, s_ref = refs[12:17]
         z_ref, sum_ref = refs[17:19]
         y_refs, msgs = refs[19:25], refs[25:28]
-        zb_ref, s_ref, sems, w_ref = refs[28:32]
-        copies = fetch(table_ref, matrix_ref, s_ref, sems)
-        inv = 1.0 / jnp.sqrt(red_ref[0:1, :] + epsilon)
-        h11 = red_ref[1:2, :] * inv * inv
+        zb_ref, w_ref = refs[28:30]
         zb_ref[...] = jnp.zeros_like(zb_ref)
         square = jnp.zeros((1, cols), F32)
         for i in range(slots):
             d, at = i // cap, (i % cap) * blk
             w = own[d][at : at + blk, :] + got[d][at : at + blk, :]
-            w = (w - h11 * r_ref[i * blk : (i + 1) * blk, :]) * inv
             w_ref[i * blk : (i + 1) * blk, :] = w
             square += colsum(w * w)
             z = apply_block(m_ref[i * blk : (i + 1) * blk, :], w)
@@ -236,10 +251,8 @@
             spread(table_ref, zb_ref, i, z)
         on_first = jnp.zeros((1, cols), F32)
         on_second = jnp.zeros((1, cols), F32)
-        low = core_ref[0] == 0
+        low = lax.axis_index("gz_1") == 0
         for d in range(6):
-            for k in range(cap):
-                copies[d * cap + k].wait()
             parts = local_schur(
                 table_ref, d, s_ref[d * rows : (d + 1) * rows, :], zb_ref, z_ref, diag_ref
             )
@@ -259,25 +272,24 @@
                 msgs[a][...] = y_refs[2 * a + 1][...]
 
         msgs[2][...] = y_refs[4][...]
-        sum_ref[...] = jnp.zeros_like(sum_ref)
-        sum_ref[0:1, :] = 0.5 * square
-        sum_ref[1:2, :] = on_first * inv
-        sum_ref[2:3, :] = on_second
+        sum_ref[...] = in_ref[...]
+        sum_ref[2:3, :] = 0.5 * square
+        sum_ref[3:4, :] = on_first
+        sum_ref[4:5, :] = on_second
 
     z2, sums, *rest = call(
         second,
-        [((slots * blk, cols), F32), ((8, cols), F32)] + [((rows, cols), F32)] * 9,
-        (table, core, *ys, *came, r, mcat, diag, first_sums, matrix),
-        scratch=scratch + (pltpu.VMEM((slots * blk, cols), F32),),
-        smem=2,
-        raw=(18,),
+        [((long, cols), F32), ((8, cols), F32)] + [((rows, cols), F32)] * 9,
+        (table, *ys, *came, r, mcat, diag, sums, sel),
+        scratch=spread_z + (pltpu.VMEM((long, cols), F32),),
+        flops=2 * 10**9,
     )
     ys, msgs = rest[:6], rest[6:]
     came = exchange_once(msgs)
 
-    def norms(core_ref, *refs):
+    def norms(*refs):
         own, got, in_ref, out_ref, acc_ref = refs[:6], refs[6:9], refs[9], refs[10], refs[11]
-        low = core_ref[0] == 0
+        low = lax.axis_index("gz_1") == 0
         out_ref[...] = in_ref[...]
         both = own[5][...] + got[2][...]
         acc_ref[...] = colsum(both * both)
@@ -293,30 +305,36 @@
                 both = own[2 * a][...] + got[a][...]
                 acc_ref[...] += colsum(both * both)
 
-        out_ref[3:4, :] = acc_ref[...]
+        out_ref[5:6, :] = acc_ref[...]
 
     (sums,) = call(
         norms,
         [((8, cols), F32)],
-        (core, *ys, *came, sums),
+        (*ys, *came, sums),
         scratch=(pltpu.VMEM((1, cols), F32),),
-    )
-    second_sums = total(sums)
-
-    def finish(table_ref, z1_ref, z2_ref, one_ref, two_ref, out_ref, res_ref):
-        load_square = one_ref[0:1, :]
+        smem=0,
+    )
+    sums = total(sums)
+
+    def finish(table_ref, z1_ref, z2_ref, gram_ref, out_ref, res_ref):
+        load_square = gram_ref[0:1, :]
         initial = jnp.sqrt(load_square + epsilon)
         rescale = 1.0 / initial
-        h11 = one_ref[1:2, :] * rescale * rescale
-        w_square = two_ref[0:1, :]
+        scale2 = rescale * rescale
+        h11 = gram_ref[1:2, :] * scale2
+        b11 = gram_ref[2:3, :] * scale2
+        c1v = gram_ref[3:4, :] * scale2
+        c11 = gram_ref[4:5, :] * scale2
+        e11 = gram_ref[5:6, :] * scale2
+        g11 = load_square * scale2
+        w_square = jnp.maximum(b11 - h11 * h11 * (2.0 - g11), 0.0)
         h21 = jnp.sqrt(w_square + epsilon)
         down = 1.0 / h21
-        h12 = two_ref[1:2, :] * down
-        dot22 = two_ref[2:3, :] * down * down
-        square = two_ref[3:4, :] * down * down
-        g11 = load_square * rescale * rescale
         g22 = w_square * down * down
-        g12 = h11 * (epsilon * rescale * rescale) * down
+        g12 = h11 * (epsilon * scale2) * down
+        h12 = (c1v - h11 * h11) * down
+        dot22 = ((c11 - h11 * c1v) - h11 * (b11 - h11 * h11)) * down * down
+        square = ((e11 - h11 * c11) - h11 * (c11 - h11 * b11)) * down * down
         h22 = dot22 - h12 * g12
         left = square - h12 * h12 * (2.0 - g11) - h22 * (2.0 * dot22 - h22 * g22) + 2.0 * h12 * h22 * g12
         h32 = jnp.sqrt(jnp.maximum(left, 0.0) + epsilon)
@@ -329,11 +347,11 @@
         y2 = -initial * s1 * c2 / r2
         y1 = (initial * c1 - top * y2) / r1
         res_ref[...] = initial * s1 * s2
-        a1 = y1 * rescale
-        a2 = y2 * down
+        a2 = y2 * down * rescale
+        a1 = y1 * rescale - a2 * h11
         out_ref[...] = jnp.zeros_like(out_ref)
         for i in range(slots):
-            b = table_ref[i]
+            b = table_ref[i % cap, i // cap]
 
             @pl.when(b < nblk)
             def _():
@@ -343,7 +361,7 @@
     out, res = call(
         finish,
         [((order, cols), F32), ((1, cols), F32)],
-        (table, z1, z2, first_sums, second_sums),
+        (table, z1, z2, sums),
     )
     return out.reshape(1, 1, 1, order, cols), res.reshape(cols)
 

time: 125 us -> 90.7 us (0.73)
  local copies, waits for them, and re-layouts: 17.5 us -> 0.71 us
  starting transfers between devices: 37.1 us -> 25.1 us
  waiting for transfers between devices: 21.1 us -> 15.2 us
  blocking collectives: 27.5 us -> 29.4 us
    unnamed x43 -> x6, local copies, waits for them, and re-layouts: 15.9 us -> 0.68 us
    all_to_all x2 -> x0, starting transfers between devices: 12.7 us -> none  [gather_sum(): wide = lax.all_to_all(wide, axes, 0, 0, tiled=True)]
    all_to_all x2 -> x0, waiting for transfers between devices: 7.73 us -> none  [gather_sum(): wide = lax.all_to_all(wide, axes, 0, 0, tiled=True)]
    ppermute x2, starting transfers between devices: 1.24 us -> 3.63 us  [exchange_once(): got.append(lax.ppermute(message, (axis, 'gz_1'), pairs))]
    ppermute x1, starting transfers between devices: 2.23 us -> 0.01 us  [exchange_once(): got.append(lax.ppermute(messages[2], GZ, shifts(GZ)[0]))]
    ppermute x6, starting transfers between devices: 10.6 us -> 12.8 us  [exchange(): got[2 * a] = lax.ppermute(faces[2 * a + 1], axis, down)]
    all_to_all x2, blocking collectives: 27.5 us -> 29.4 us  [gather_sum(): wide = lax.all_to_all(wide, axes, 0, 0, tiled=True)]
    ppermute x6, starting transfers between devices: 10.3 us -> 8.66 us  [exchange(): got[2 * a + 1] = lax.ppermute(faces[2 * a], axis, up)]
  transfers between devices with their start and end apart: 17 -> 15, of which waited for: 8 -> 7; matrix products, arithmetic and copies ran while one was open for 2% -> 0% of each run, Pallas kernels for 0% -> 4%
where the time goes in v2:
time: 90.7 us; the launch traced here: 90.5 us
  blocking collectives  29.4 us (32%)
  starting transfers between devices  25.1 us (28%)
  Pallas kernels  19.4 us (21%)
  waiting for transfers between devices  15.2 us (17%)
    all_to_all x2, blocking collectives, gather_sum(): wide = lax.all_to_all(wide, axes, 0, 0, tiled=True)  29.4 us
    pallas_call x6, Pallas kernels, call(): pl.pallas_call(body, out_shape=[jax.ShapeDtypeStruct(s, t) for s, t in ou...  19.4 us
    ppermute x6, starting transfers between devices, exchange(): got[2 * a] = lax.ppermute(faces[2 * a + 1], axis, down)  12.8 us
    ppermute x6, starting transfers between devices, exchange(): got[2 * a + 1] = lax.ppermute(faces[2 * a], axis, up)  8.66 us
    ppermute x6, waiting for transfers between devices, exchange(): got[2 * a] = lax.ppermute(faces[2 * a + 1], axis, down)  6.23 us
    ppermute x6, waiting for transfers between devices, exchange(): got[2 * a + 1] = lax.ppermute(faces[2 * a], axis, up)  5.61 us
    ppermute x2, starting transfers between devices, exchange_once(): got.append(lax.ppermute(message, (axis, 'gz_1'), pairs))  3.63 us
    ppermute x2, waiting for transfers between devices, exchange_once(): got.append(lax.ppermute(message, (axis, 'gz_1'), pairs))  3.31 us
  transfers between devices with their start and end apart: 15, of which 7 were waited for; matrix products, arithmetic and copies ran while one was open for 0% of the time, Pallas kernels for 4%

profile of v2, /device:TPU:1, one launch (start us, length us, event | category | flops | bytes accessed | tf_op | source)
XLA Modules:
  0.0 90.5 jit_solution(804044514090517316)
XLA Ops:
  0.6 0.0 copy-start.1
  0.6 0.7 copy-done.1
  1.3 2.4 %shard_map.68 = (f32[256,384]{1,0:T(8,128)S(1)}, f32[256,384]{1,0:T(8,128)S(1)}, f32[256,384]{1,0:T(8,128)S(1)}, f32[256,384]{1,0:T(8,128)S(1)}, f32[256,384]{1,0:T(8,128)S(1)}, /*index=5*/f32[256,384]{1,0:T(8,128)S(1)}) custom-call(s32[2,6]{1,0:T(2,128)S(1)} %bitcast.11, bf16[2048,256]{1,0:T(8,128)(2,1)} %bitcast.17, f32[16,128,128]{2,1,0:T(8,128)} %bitcast.18), custom_call_target="tpu_custom_call" | custom-call | bytes 1048576 | tf_op jit(solution)/shard_map/pallas_call | solution.py:28
  3.7 2.4 %collective-permute-start.1 = (f32[256,384]{1,0:T(8,128)S(1)}, f32[256,384]{1,0:T(8,128)S(1)}, u32[]{:S(2)}, u32[]{:S(2)}) collective-permute-start(f32[256,384]{1,0:T(8,128)S(1)} %get-tuple-element.31.refs_0_), channel_id=1, source_target_pairs={{0,32},{32,64},{64,96},{96,128},{128,160},{160,192},{192,224},{224... | collective-permute-start | bytes 1179656 | tf_op jit(solution)/shard_map/ppermute | solution.py:50
  6.2 3.9 %collective-permute-start = (f32[256,384]{1,0:T(8,128)S(1)}, f32[256,384]{1,0:T(8,128)S(1)}, u32[]{:S(2)}, u32[]{:S(2)}) collective-permute-start(f32[256,384]{1,0:T(8,128)S(1)} %get-tuple-element.32.refs_1_), channel_id=1, source_target_pairs={{32,0},{64,32},{96,64},{128,96},{160,128},{192,160},{224,192},{0,2... | collective-permute-start | bytes 1179656 | tf_op jit(solution)/shard_map/ppermute | solution.py:49
  10.1 1.3 %collective-permute-start.3 = (f32[256,384]{1,0:T(8,128)S(1)}, f32[256,384]{1,0:T(8,128)S(1)}, u32[]{:S(2)}, u32[]{:S(2)}) collective-permute-start(f32[256,384]{1,0:T(8,128)S(1)} %get-tuple-element.33.refs_2_), channel_id=1, source_target_pairs={{0,8},{8,16},{16,24},{24,0},{1,9},{9,17},{17,25},{25,1},{2,10},{10... | collective-permute-start | bytes 1179656 | tf_op jit(solution)/shard_map/ppermute | solution.py:50
  11.4 1.6 %collective-permute-start.2 = (f32[256,384]{1,0:T(8,128)S(1)}, f32[256,384]{1,0:T(8,128)S(1)}, u32[]{:S(2)}, u32[]{:S(2)}) collective-permute-start(f32[256,384]{1,0:T(8,128)S(1)} %get-tuple-element.34.refs_3_), channel_id=1, source_target_pairs={{8,0},{16,8},{24,16},{0,24},{9,1},{17,9},{25,17},{1,25},{10,2},{18... | collective-permute-start | bytes 1179656 | tf_op jit(solution)/shard_map/ppermute | solution.py:49
  13.0 2.6 %collective-permute-start.5 = (f32[256,384]{1,0:T(8,128)S(1)}, f32[256,384]{1,0:T(8,128)S(1)}, u32[]{:S(2)}, u32[]{:S(2)}) collective-permute-start(f32[256,384]{1,0:T(8,128)S(1)} %get-tuple-element.35.refs_4_), channel_id=1, source_target_pairs={{0,1},{1,2},{2,3},{3,4},{4,5},{5,6},{6,7},{7,0},{8,9},{9,10},{10,1... | collective-permute-start | bytes 1179656 | tf_op jit(solution)/shard_map/ppermute | solution.py:50
  15.6 3.0 %collective-permute-done.1.refs_7_ = f32[256,384]{1,0:T(8,128)S(1)} collective-permute-done((f32[256,384]{1,0:T(8,128)S(1)}, f32[256,384]{1,0:T(8,128)S(1)}, u32[]{:S(2)}, u32[]{:S(2)}) %collective-permute-start.1) | collective-permute-done | bytes 393248 | tf_op jit(solution)/shard_map/ppermute | solution.py:50
  18.5 1.5 %collective-permute-start.4 = (f32[256,384]{1,0:T(8,128)S(1)}, f32[256,384]{1,0:T(8,128)S(1)}, u32[]{:S(2)}, u32[]{:S(2)}) collective-permute-start(f32[256,384]{1,0:T(8,128)S(1)} %get-tuple-element.36.refs_5_), channel_id=1, source_target_pairs={{1,0},{2,1},{3,2},{4,3},{5,4},{6,5},{7,6},{0,7},{9,8},{10,9},{11,1... | collective-permute-start | bytes 1179656 | tf_op jit(solution)/shard_map/ppermute | solution.py:49
  20.1 3.8 %shard_map.69.refs_13_.refs_16_ = bf16[1536,2048]{1,0:T(8,128)(2,1)S(1)} custom-call(s32[2,6]{1,0:T(2,128)S(1)} %bitcast.12, bf16[2048,2048]{1,0:T(8,128)(2,1)} %bitcast.16), custom_call_target="tpu_custom_call" | custom-call | flops 2000000000 | bytes 1048576 | tf_op jit(solution)/shard_map/pallas_call | solution.py:28
  23.9 2.8 %collective-permute-done.4.refs_10_ = f32[256,384]{1,0:T(8,128)S(1)} collective-permute-done((f32[256,384]{1,0:T(8,128)S(1)}, f32[256,384]{1,0:T(8,128)S(1)}, u32[]{:S(2)}, u32[]{:S(2)}) %collective-permute-start.4) | collective-permute-done | bytes 393248 | tf_op jit(solution)/shard_map/ppermute | solution.py:49
  26.7 5.2 %shard_map.70 = (f32[1536,256]{1,0:T(8,128)S(1)}, f32[1536,256]{1,0:T(8,128)S(1)}, bf16[1536,256]{1,0:T(8,128)(2,1)S(1)}, f32[8,256]{1,0:T(8,128)S(1)}, f32[256,...) custom-call(s32[2,6]{1,0:T(2,128)S(1)} %bitcast.13, ...), custom_call_target="tpu_custom_call" | custom-call | flops 2000000000 | bytes 1048576 | tf_op jit(solution)/shard_map/pallas_call | solution.py:28
  31.9 0.1 collective-permute-start.7
  32.0 2.7 %collective-permute-start.6 = (f32[256,256]{1,0:T(8,128)S(1)}, f32[256,256]{1,0:T(8,128)S(1)}, u32[]{:S(2)}, u32[]{:S(2)}) collective-permute-start(f32[256,256]{1,0:T(8,128)S(1)} %get-tuple-element.39.refs_1_), channel_id=1, source_target_pairs={{32,0},{64,32},{96,64},{128,96},{160,128},{192,160},{224,192},{0,2... | collective-permute-start | bytes 786440 | tf_op jit(solution)/shard_map/ppermute | solution.py:49
  34.6 1.4 %collective-permute-start.9 = (f32[256,256]{1,0:T(8,128)S(1)}, f32[256,256]{1,0:T(8,128)S(1)}, u32[]{:S(2)}, u32[]{:S(2)}) collective-permute-start(f32[256,256]{1,0:T(8,128)S(1)} %get-tuple-element.40.refs_2_), channel_id=1, source_target_pairs={{0,8},{8,16},{16,24},{24,0},{1,9},{9,17},{17,25},{25,1},{2,10},{10... | collective-permute-start | bytes 786440 | tf_op jit(solution)/shard_map/ppermute | solution.py:50
  36.0 1.4 %collective-permute-start.8 = (f32[256,256]{1,0:T(8,128)S(1)}, f32[256,256]{1,0:T(8,128)S(1)}, u32[]{:S(2)}, u32[]{:S(2)}) collective-permute-start(f32[256,256]{1,0:T(8,128)S(1)} %get-tuple-element.41.refs_3_), channel_id=1, source_target_pairs={{8,0},{16,8},{24,16},{0,24},{9,1},{17,9},{25,17},{1,25},{10,2},{18... | collective-permute-start | bytes 786440 | tf_op jit(solution)/shard_map/ppermute | solution.py:49
  37.4 0.9 collective-permute-start.11
  38.3 1.9 %collective-permute-done.7.refs_7_ = f32[256,256]{1,0:T(8,128)S(1)} collective-permute-done((f32[256,256]{1,0:T(8,128)S(1)}, f32[256,256]{1,0:T(8,128)S(1)}, u32[]{:S(2)}, u32[]{:S(2)}) %collective-permute-start.7) | collective-permute-done | bytes 262176 | tf_op jit(solution)/shard_map/ppermute | solution.py:50
  40.2 1.7 %collective-permute-start.10 = (f32[256,256]{1,0:T(8,128)S(1)}, f32[256,256]{1,0:T(8,128)S(1)}, u32[]{:S(2)}, u32[]{:S(2)}) collective-permute-start(f32[256,256]{1,0:T(8,128)S(1)} %get-tuple-element.43.refs_5_), channel_id=1, source_target_pairs={{1,0},{2,1},{3,2},{4,3},{5,4},{6,5},{7,6},{0,7},{9,8},{10,9},{11,1... | collective-permute-start | bytes 786440 | tf_op jit(solution)/shard_map/ppermute | solution.py:49
  41.9 0.7 collective-permute-done.9.refs_9_
  42.6 0.0 collective-permute-done.8.refs_8_
  42.6 3.4 %collective-permute-done.10.refs_10_ = f32[256,256]{1,0:T(8,128)S(1)} collective-permute-done((f32[256,256]{1,0:T(8,128)S(1)}, f32[256,256]{1,0:T(8,128)S(1)}, u32[]{:S(2)}, u32[]{:S(2)}) %collective-permute-start.10) | collective-permute-done | bytes 262176 | tf_op jit(solution)/shard_map/ppermute | solution.py:49
  46.0 5.7 %shard_map.71 = (f32[1536,256]{1,0:T(8,128)S(1)}, f32[8,256]{1,0:T(8,128)S(1)}, f32[256,256]{1,0:T(8,128)S(1)}, f32[256,256]{1,0:T(8,128)S(1)}, f32[256,256]{1,0...) custom-call(s32[2,6]{1,0:T(2,128)S(1)} %bitcast.14, ...), custom_call_target="tpu_custom_call" | custom-call | flops 2000000000 | bytes 1048576 | tf_op jit(solution)/shard_map/pallas_call | solution.py:28
  51.7 0.6 collective-permute-start.12
  52.3 3.0 %collective-permute-start.13 = (f32[256,256]{1,0:T(8,128)S(1)}, f32[256,256]{1,0:T(8,128)S(1)}, u32[]{:S(2)}, u32[]{:S(2)}) collective-permute-start(f32[256,256]{1,0:T(8,128)S(1)} %get-tuple-element.55), channel_id=1, source_target_pairs={{0,8},{1,25},{8,16},{9,1},{16,24},{17,9},{24,0},{25,17},{2,10},{3,... | collective-permute-start | bytes 786440 | tf_op jit(solution)/shard_map/ppermute | solution.py:61
  55.3 1.7 %collective-permute-done.12.refs_6_ = f32[256,256]{1,0:T(8,128)S(1)} collective-permute-done((f32[256,256]{1,0:T(8,128)S(1)}, f32[256,256]{1,0:T(8,128)S(1)}, u32[]{:S(2)}, u32[]{:S(2)}) %collective-permute-start.12) | collective-permute-done | bytes 262176 | tf_op jit(solution)/shard_map/ppermute | solution.py:61
  57.0 1.6 %collective-permute-done.13.refs_7_ = f32[256,256]{1,0:T(8,128)S(1)} collective-permute-done((f32[256,256]{1,0:T(8,128)S(1)}, f32[256,256]{1,0:T(8,128)S(1)}, u32[]{:S(2)}, u32[]{:S(2)}) %collective-permute-start.13) | collective-permute-done | bytes 262176 | tf_op jit(solution)/shard_map/ppermute | solution.py:61
  58.6 0.2 shard_map.72
  58.8 17.1 %all_to_all.12 = f32[32,8,256]{2,1,0:T(8,128)S(1)} all-to-all(f32[32,8,256]{2,1,0:T(8,128)S(1)} %broadcast_in_dim.4), channel_id=1, replica_groups=mesh['gx'=8,'gy'=4,'gz_0'=4,'gz_1'=2] {'gy','gz_0','gz_1'}, dimensions={0} | all-to-all | bytes 524288 | tf_op jit(solution)/shard_map/all_to_all | solution.py:69
  76.0 12.3 %all_to_all.13 = f32[8,8,256]{2,1,0:T(8,128)S(1)} all-to-all(f32[8,8,256]{2,1,0:T(8,128)S(1)} %broadcast_in_dim.5), channel_id=1, replica_groups=mesh['gx'=8,'gy'=4,'gz_0'=4,'gz_1'=2] {'gx'}, dimensions={0} | all-to-all | bytes 131072 | tf_op jit(solution)/shard_map/all_to_all | solution.py:69
  88.3 2.2 %shard_map.73 = (f32[2048,256]{1,0:T(8,128)}, f32[1,256]{1,0:T(1,128)}) custom-call(s32[2,6]{1,0:T(2,128)S(1)} %bitcast.15, f32[1536,256]{1,0:T(8,128)S(1)} %get-tuple-element.37.z1_ref, f32[1536,256]{1,0:T(8,128)S(1)} %get-tuple-element.47.z2_ref, f32[8,256]{1,0:T(8,128)S(1)} %reduce_sum.19.gram_ref), custom_call_target="tpu_custom_call" | custom-call | bytes 1048576 | tf_op jit(solution)/shard_map/pallas_call | solution.py:28
  (16 shorter events, 0.1 us)
Async XLA Ops:
  0.6 0.7 copy-start.1
  3.7 14.8 %collective-permute-start.1 = (f32[256,384]{1,0:T(8,128)S(1)}, f32[256,384]{1,0:T(8,128)S(1)}, u32[]{:S(2)}, u32[]{:S(2)}) collective-permute-start(f32[256,384]{1,0:T(8,128)S(1)} %get-tuple-element.31.refs_0_), channel_id=1, source_target_pairs={{0,32},{32,64},{64,96},{96,128},{128,160},{160,192},{192,224},{224... | collective-permute-start | bytes 1179656 | tf_op jit(solution)/shard_map/ppermute | solution.py:50
  6.2 17.7 %collective-permute-start = (f32[256,384]{1,0:T(8,128)S(1)}, f32[256,384]{1,0:T(8,128)S(1)}, u32[]{:S(2)}, u32[]{:S(2)}) collective-permute-start(f32[256,384]{1,0:T(8,128)S(1)} %get-tuple-element.32.refs_1_), channel_id=1, source_target_pairs={{32,0},{64,32},{96,64},{128,96},{160,128},{192,160},{224,192},{0,2... | collective-permute-start | bytes 1179656 | tf_op jit(solution)/shard_map/ppermute | solution.py:49
  10.1 13.8 %collective-permute-start.3 = (f32[256,384]{1,0:T(8,128)S(1)}, f32[256,384]{1,0:T(8,128)S(1)}, u32[]{:S(2)}, u32[]{:S(2)}) collective-permute-start(f32[256,384]{1,0:T(8,128)S(1)} %get-tuple-element.33.refs_2_), channel_id=1, source_target_pairs={{0,8},{8,16},{16,24},{24,0},{1,9},{9,17},{17,25},{25,1},{2,10},{10... | collective-permute-start | bytes 1179656 | tf_op jit(solution)/shard_map/ppermute | solution.py:50
  11.4 12.5 %collective-permute-start.2 = (f32[256,384]{1,0:T(8,128)S(1)}, f32[256,384]{1,0:T(8,128)S(1)}, u32[]{:S(2)}, u32[]{:S(2)}) collective-permute-start(f32[256,384]{1,0:T(8,128)S(1)} %get-tuple-element.34.refs_3_), channel_id=1, source_target_pairs={{8,0},{16,8},{24,16},{0,24},{9,1},{17,9},{25,17},{1,25},{10,2},{18... | collective-permute-start | bytes 1179656 | tf_op jit(solution)/shard_map/ppermute | solution.py:49
  13.0 10.9 %collective-permute-start.5 = (f32[256,384]{1,0:T(8,128)S(1)}, f32[256,384]{1,0:T(8,128)S(1)}, u32[]{:S(2)}, u32[]{:S(2)}) collective-permute-start(f32[256,384]{1,0:T(8,128)S(1)} %get-tuple-element.35.refs_4_), channel_id=1, source_target_pairs={{0,1},{1,2},{2,3},{3,4},{4,5},{5,6},{6,7},{7,0},{8,9},{9,10},{10,1... | collective-permute-start | bytes 1179656 | tf_op jit(solution)/shard_map/ppermute | solution.py:50
  18.5 8.1 %collective-permute-start.4 = (f32[256,384]{1,0:T(8,128)S(1)}, f32[256,384]{1,0:T(8,128)S(1)}, u32[]{:S(2)}, u32[]{:S(2)}) collective-permute-start(f32[256,384]{1,0:T(8,128)S(1)} %get-tuple-element.36.refs_5_), channel_id=1, source_target_pairs={{1,0},{2,1},{3,2},{4,3},{5,4},{6,5},{7,6},{0,7},{9,8},{10,9},{11,1... | collective-permute-start | bytes 1179656 | tf_op jit(solution)/shard_map/ppermute | solution.py:49
  20.1 6.6 %copy-start = (f32[1,1,1,2048]{3,2,1,0:T(1,128)S(1)}, f32[1,1,1,2048]{3,2,1,0:T(1,128)}, u32[]{:S(2)}) copy-start(f32[1,1,1,2048]{3,2,1,0:T(1,128)} %param.6) | copy-start | bytes 24580
  31.9 8.3 %collective-permute-start.7 = (f32[256,256]{1,0:T(8,128)S(1)}, f32[256,256]{1,0:T(8,128)S(1)}, u32[]{:S(2)}, u32[]{:S(2)}) collective-permute-start(f32[256,256]{1,0:T(8,128)S(1)} %get-tuple-element.38.refs_0_), channel_id=1, source_target_pairs={{0,32},{32,64},{64,96},{96,128},{128,160},{160,192},{192,224},{224... | collective-permute-start | bytes 786440 | tf_op jit(solution)/shard_map/ppermute | solution.py:50
  32.0 9.9 %collective-permute-start.6 = (f32[256,256]{1,0:T(8,128)S(1)}, f32[256,256]{1,0:T(8,128)S(1)}, u32[]{:S(2)}, u32[]{:S(2)}) collective-permute-start(f32[256,256]{1,0:T(8,128)S(1)} %get-tuple-element.39.refs_1_), channel_id=1, source_target_pairs={{32,0},{64,32},{96,64},{128,96},{160,128},{192,160},{224,192},{0,2... | collective-permute-start | bytes 786440 | tf_op jit(solution)/shard_map/ppermute | solution.py:49
  34.6 7.9 %collective-permute-start.9 = (f32[256,256]{1,0:T(8,128)S(1)}, f32[256,256]{1,0:T(8,128)S(1)}, u32[]{:S(2)}, u32[]{:S(2)}) collective-permute-start(f32[256,256]{1,0:T(8,128)S(1)} %get-tuple-element.40.refs_2_), channel_id=1, source_target_pairs={{0,8},{8,16},{16,24},{24,0},{1,9},{9,17},{17,25},{25,1},{2,10},{10... | collective-permute-start | bytes 786440 | tf_op jit(solution)/shard_map/ppermute | solution.py:50
  36.0 6.6 %collective-permute-start.8 = (f32[256,256]{1,0:T(8,128)S(1)}, f32[256,256]{1,0:T(8,128)S(1)}, u32[]{:S(2)}, u32[]{:S(2)}) collective-permute-start(f32[256,256]{1,0:T(8,128)S(1)} %get-tuple-element.41.refs_3_), channel_id=1, source_target_pairs={{8,0},{16,8},{24,16},{0,24},{9,1},{17,9},{25,17},{1,25},{10,2},{18... | collective-permute-start | bytes 786440 | tf_op jit(solution)/shard_map/ppermute | solution.py:49
  37.4 5.2 %collective-permute-start.11 = (f32[256,256]{1,0:T(8,128)S(1)}, f32[256,256]{1,0:T(8,128)S(1)}, u32[]{:S(2)}, u32[]{:S(2)}) collective-permute-start(f32[256,256]{1,0:T(8,128)S(1)} %get-tuple-element.42.refs_4_), channel_id=1, source_target_pairs={{0,1},{1,2},{2,3},{3,4},{4,5},{5,6},{6,7},{7,0},{8,9},{9,10},{10,1... | collective-permute-start | bytes 786440 | tf_op jit(solution)/shard_map/ppermute | solution.py:50
  40.2 5.8 %collective-permute-start.10 = (f32[256,256]{1,0:T(8,128)S(1)}, f32[256,256]{1,0:T(8,128)S(1)}, u32[]{:S(2)}, u32[]{:S(2)}) collective-permute-start(f32[256,256]{1,0:T(8,128)S(1)} %get-tuple-element.43.refs_5_), channel_id=1, source_target_pairs={{1,0},{2,1},{3,2},{4,3},{5,4},{6,5},{7,6},{0,7},{9,8},{10,9},{11,1... | collective-permute-start | bytes 786440 | tf_op jit(solution)/shard_map/ppermute | solution.py:49
  51.7 36.6 %copy-start.2 = (s32[1,1,1,6,2]{3,4,2,1,0:T(2,128)S(1)}, s32[1,1,1,6,2]{3,4,2,1,0:T(2,128)}, u32[]{:S(2)}) copy-start(s32[1,1,1,6,2]{3,4,2,1,0:T(2,128)} %param.9) | copy-start | bytes 148
  51.7 5.3 %collective-permute-start.12 = (f32[256,256]{1,0:T(8,128)S(1)}, f32[256,256]{1,0:T(8,128)S(1)}, u32[]{:S(2)}, u32[]{:S(2)}) collective-permute-start(f32[256,256]{1,0:T(8,128)S(1)} %get-tuple-element.54), channel_id=1, source_target_pairs={{0,32},{1,225},{32,64},{33,1},{64,96},{65,33},{96,128},{97,65},{12... | collective-permute-start | bytes 786440 | tf_op jit(solution)/shard_map/ppermute | solution.py:61
  52.3 6.3 %collective-permute-start.13 = (f32[256,256]{1,0:T(8,128)S(1)}, f32[256,256]{1,0:T(8,128)S(1)}, u32[]{:S(2)}, u32[]{:S(2)}) collective-permute-start(f32[256,256]{1,0:T(8,128)S(1)} %get-tuple-element.55), channel_id=1, source_target_pairs={{0,8},{1,25},{8,16},{9,1},{16,24},{17,9},{24,0},{25,17},{2,10},{3,... | collective-permute-start | bytes 786440 | tf_op jit(solution)/shard_map/ppermute | solution.py:61
  55.3 3.3 %collective-permute-start.14 = (f32[256,256]{1,0:T(8,128)S(1)}, f32[256,256]{1,0:T(8,128)S(1)}, u32[]{:S(2)}, u32[]{:S(2)}) collective-permute-start(f32[256,256]{1,0:T(8,128)S(1)} %get-tuple-element.56), channel_id=1, source_target_pairs={{0,1},{1,2},{2,3},{3,4},{4,5},{5,6},{6,7},{7,0},{8,9},{9,10},{10,1... | collective-permute-start | bytes 786440 | tf_op jit(solution)/shard_map/ppermute | solution.py:62

commit v3 on v2

v3 whole, which is shorter than its diff:
```python
import jax
import jax.numpy as jnp
from jax import lax
from jax.experimental import pallas as pl
from jax.experimental.pallas import tpu as pltpu
from jax.sharding import Mesh
from jax.sharding import PartitionSpec as P

GZ = ("gz_0", "gz_1")
AXES = ("gx", "gy", GZ)
INNER = ("gy", "gz_0", "gz_1")


epsilon = 1e-06
F32 = jnp.float32
BF16 = jnp.bfloat16


def call(body, outs, operands, scratch=(), smem=1, raw=(), hbm_out=(), flops=0, mib=16):
    specs = []
    operands = list(operands)
    for i in range(len(operands)):
        if i < smem:
            specs.append(pl.BlockSpec(memory_space=pltpu.SMEM))
            operands[i] = pltpu.with_memory_space_constraint(operands[i], pltpu.HBM)
        elif i in raw:
            specs.append(pl.BlockSpec(memory_space=pltpu.HBM))
            operands[i] = pltpu.with_memory_space_constraint(operands[i], pltpu.HBM)
        else:
            specs.append(pl.BlockSpec(memory_space=pltpu.VMEM))
    return pl.pallas_call(
        body,
        out_shape=[jax.ShapeDtypeStruct(s, t) for s, t in outs],
        in_specs=specs,
        out_specs=[
            pl.BlockSpec(memory_space=pltpu.HBM if i in hbm_out else pltpu.VMEM) for i in range(len(outs))
        ],
        scratch_shapes=list(scratch),
        compiler_params=pltpu.CompilerParams(vmem_limit_bytes=mib * 2**20),
        cost_estimate=pl.CostEstimate(flops=flops, transcendentals=0, bytes_accessed=2**20),
    )(*operands)


def shifts(axis):
    n = lax.axis_size(axis)
    up = [(i, (i + 1) % n) for i in range(n)]
    return up, [(j, i) for i, j in up]


def exchange(to_next, to_previous, axis):
    up, down = shifts(axis)
    return [lax.ppermute(to_previous, axis, down), lax.ppermute(to_next, axis, up)]


def exchange_once(message, axis):
    if axis == GZ:
        return lax.ppermute(message, GZ, shifts(GZ)[0])
    n = lax.axis_size(axis)
    pairs = []
    for i in range(n):
        pairs += [(2 * i, 2 * ((i + 1) % n)), (2 * i + 1, 2 * ((i - 1) % n) + 1)]
    return lax.ppermute(message, (axis, "gz_1"), pairs)


def gather_sum(rows, axes):
    n = lax.axis_size(axes)
    wide = jnp.broadcast_to(rows[None], (n,) + rows.shape).reshape(n * rows.shape[0], rows.shape[1])
    wide = lax.all_to_all(wide, axes, 0, 0, tiled=True)
    return jnp.sum(wide.reshape((n,) + rows.shape), axis=0)


def total(rows):
    return gather_sum(gather_sum(rows, INNER), ("gx",))


def split(x):
    hi = x.astype(BF16)
    return hi, (x - hi.astype(F32)).astype(BF16)


def apply_block(mcat, vec):
    blk = mcat.shape[0]
    hi, lo = split(vec)
    out = jnp.dot(mcat, jnp.concatenate([hi, hi], axis=0), preferred_element_type=F32)
    return out + jnp.dot(mcat[:, :blk], lo, preferred_element_type=F32)


def column(row, blk):
    r = lax.broadcasted_iota(jnp.int32, (blk, blk), 0)
    c = lax.broadcasted_iota(jnp.int32, (blk, blk), 1)
    return jnp.sum(jnp.where(r == c, jnp.broadcast_to(row, (blk, blk)), 0.0), axis=1, keepdims=True)


def colsum(x):
    return jnp.sum(x, axis=0, keepdims=True)


def on_device(schur, interface_diag, precond, load, face_blocks):
    nblk, blk = precond.shape[3], precond.shape[4]
    cols = load.shape[-1]
    order = nblk * blk
    cap = face_blocks.shape[-1]
    slots = 6 * cap
    rows = cap * blk
    table = face_blocks.reshape(6, cap).T
    matrix = schur.reshape(order, order)
    diag = interface_diag.reshape(nblk, blk)

    def pick(table_ref, i):
        b = table_ref[i % cap, i // cap]
        return jnp.minimum(b, nblk - 1), (b < nblk).astype(F32)

    def pack(table_ref, load_ref, pre_ref, *refs):
        faces, (load_buf, pre_buf, load_sems, pre_sems) = refs[:6], refs[6:]
        copies = []
        for i in range(slots):
            b, _ = pick(table_ref, i)
            at = pl.multiple_of(b * blk, blk)
            copies.append(
                (
                    pltpu.make_async_copy(load_ref.at[pl.ds(at, blk), :], load_buf.at[i], load_sems.at[i]),
                    pltpu.make_async_copy(pre_ref.at[b], pre_buf.at[i], pre_sems.at[i]),
                )
            )
            for copy in copies[-1]:
                copy.start()
        for i in range(slots):
            _, m = pick(table_ref, i)
            d, at = i // cap, (i % cap) * blk
            for copy in copies[i]:
                copy.wait()
            faces[d][at : at + blk, :cols] = load_buf[i].astype(F32) * m
            faces[d][at : at + blk, cols:] = pre_buf[i] * m

    faces = call(
        pack,
        [((rows, cols + blk), F32)] * 6,
        (table, load.reshape(order, cols), precond.reshape(nblk, blk, blk)),
        scratch=(
            pltpu.VMEM((slots, blk, cols), BF16),
            pltpu.VMEM((slots, blk, blk), F32),
            pltpu.SemaphoreType.DMA((slots,)),
            pltpu.SemaphoreType.DMA((slots,)),
        ),
        raw=(1, 2),
    )
    came = [x for a in range(3) for x in exchange(faces[2 * a], faces[2 * a + 1], AXES[a])]

    def fetch(table_ref, matrix_ref, s_ref, sems):
        copies = []
        for i in range(slots):
            b, _ = pick(table_ref, i)
            copy = pltpu.make_async_copy(
                matrix_ref.at[pl.ds(pl.multiple_of(b * blk, blk), blk), :],
                s_ref.at[pl.ds(i * blk, blk), :],
                sems.at[i],
            )
            copy.start()
            copies.append(copy)
        for copy in copies:
            copy.wait()

    (sel,) = call(
        fetch,
        [((slots * blk, order), BF16)],
        (table, matrix),
        scratch=(pltpu.SemaphoreType.DMA((slots,)),),
        raw=(1,),
        flops=2 * 10**9,
    )

    def spread(table_ref, zb_ref, i, value):
        b = table_ref[i % cap, i // cap]

        @pl.when(b < nblk)
        def _():
            zb_ref[pl.ds(pl.multiple_of(b * blk, blk), blk), :] = value.astype(BF16)

    def local_schur(table_ref, d, s_ref, zb_ref, z_ref, diag_ref, out_ref):
        base = pl.multiple_of(d * rows, rows)
        product = jnp.dot(s_ref[pl.ds(base, rows), :], zb_ref[...], preferred_element_type=F32)
        for k in range(cap):
            b = table_ref[k, d]
            m = (b < nblk).astype(F32)
            dcol = column(diag_ref[pl.ds(jnp.minimum(b, nblk - 1), 1), :], blk)
            z = z_ref[pl.ds(base + k * blk, blk), :]
            out_ref[k * blk : (k + 1) * blk, :] = (product[k * blk : (k + 1) * blk] + dcol * z) * m

    long = slots * blk
    tall = (long, cols)
    flat = (rows, cols)

    def first(table_ref, *refs):
        own, got = refs[:6], refs[6:12]
        diag_ref, s_ref = refs[12:14]
        r_ref, z_ref, m_ref, zb_ref, up_ref, down_ref = refs[14:20]
        zb_ref[...] = jnp.zeros_like(zb_ref)
        for i in range(slots):
            d, at = i // cap, (i % cap) * blk
            r = own[d][at : at + blk, :cols] + got[d][at : at + blk, :cols]
            m = own[d][at : at + blk, cols:] + got[d][at : at + blk, cols:]
            hi, lo = split(m)
            mcat = jnp.concatenate([hi, lo], axis=1)
            m_ref[i * blk : (i + 1) * blk, :] = mcat
            r_ref[i * blk : (i + 1) * blk, :] = r
            z = apply_block(mcat, r)
            z_ref[i * blk : (i + 1) * blk, :] = z
            spread(table_ref, zb_ref, i, z)
        local_schur(table_ref, 0, s_ref, zb_ref, z_ref, diag_ref, up_ref)
        local_schur(table_ref, 1, s_ref, zb_ref, z_ref, diag_ref, down_ref)

    def pair(axis):
        def body(table_ref, zb_ref, z_ref, diag_ref, s_ref, up_ref, down_ref):
            local_schur(table_ref, 2 * axis, s_ref, zb_ref, z_ref, diag_ref, up_ref)
            local_schur(table_ref, 2 * axis + 1, s_ref, zb_ref, z_ref, diag_ref, down_ref)

        return body

    r, z1, mcat, zb, up, down = call(
        first,
        [(tall, F32), (tall, F32), ((long, 2 * blk), BF16), ((order, cols), BF16), (flat, F32), (flat, F32)],
        (table, *faces, *came, diag, sel),
        flops=2 * 10**9,
    )
    ys = [up, down]
    came = exchange(up, down, AXES[0])
    for a in (1, 2):
        up, down = call(
            pair(a), [(flat, F32)] * 2, (table, zb, z1, diag, sel), flops=10**9
        )
        ys += [up, down]
        came += exchange(up, down, AXES[a])

    def sides(axis):
        if axis == 2:
            return 4, 5
        low = lax.axis_index("gz_1") == 0
        return jnp.where(low, 2 * axis, 2 * axis + 1), jnp.where(low, 2 * axis + 1, 2 * axis)

    def second(table_ref, *refs):
        own, got = refs[:6], refs[6:12]
        m_ref, diag_ref, s_ref = refs[12:15]
        w_ref, z_ref, zb_ref, msg_ref, keep_ref = refs[15:20]
        zb_ref[...] = jnp.zeros_like(zb_ref)
        for i in range(slots):
            d, at = i // cap, (i % cap) * blk
            w = own[d][at : at + blk, :] + got[d][at : at + blk, :]
            w_ref[i * blk : (i + 1) * blk, :] = w
            z = apply_block(m_ref[i * blk : (i + 1) * blk, :], w)
            z_ref[i * blk : (i + 1) * blk, :] = z
            spread(table_ref, zb_ref, i, z)
        send, meet = sides(0)
        local_schur(table_ref, send, s_ref, zb_ref, z_ref, diag_ref, msg_ref)
        local_schur(table_ref, meet, s_ref, zb_ref, z_ref, diag_ref, keep_ref)

    def pair_once(axis):
        def body(table_ref, zb_ref, z_ref, diag_ref, s_ref, msg_ref, keep_ref):
            send, meet = sides(axis)
            local_schur(table_ref, send, s_ref, zb_ref, z_ref, diag_ref, msg_ref)
            local_schur(table_ref, meet, s_ref, zb_ref, z_ref, diag_ref, keep_ref)

        return body

    w1, z2, zb, msg, keep = call(
        second,
        [(tall, F32), (tall, F32), ((order, cols), BF16), (flat, F32), (flat, F32)],
        (table, *ys, *came, mcat, diag, sel),
        flops=2 * 10**9,
    )
    msgs, keeps = [msg], [keep]
    came = [exchange_once(msg, AXES[0])]
    for a in (1, 2):
        msg, keep = call(pair_once(a), [(flat, F32)] * 2, (table, zb, z2, diag, sel), flops=10**9)
        msgs.append(msg)
        keeps.append(keep)
        came.append(exchange_once(msg, AXES[a]))

    def dots(*refs):
        y_refs, msg_refs, keep_refs = refs[:6], refs[6:9], refs[9:12]
        r_ref, w_ref, out_ref = refs[12:15]
        sums = [jnp.zeros((1, cols), F32) for _ in range(5)]
        for d in range(6):
            r = r_ref[d * rows : (d + 1) * rows, :]
            w = w_ref[d * rows : (d + 1) * rows, :]
            sums[0] += 0.5 * colsum(r * r)
            sums[1] += colsum(r * y_refs[d][...])
            sums[2] += 0.5 * colsum(w * w)
        for a in range(3):
            for d, ref in zip(sides(a), (msg_refs[a], keep_refs[a])):
                at = pl.ds(pl.multiple_of(d * rows, rows), rows)
                y = ref[...]
                sums[3] += colsum(y * r_ref[at, :])
                sums[4] += colsum(y * w_ref[at, :])
        out_ref[...] = jnp.zeros_like(out_ref)
        for i in range(5):
            out_ref[i : i + 1, :] = sums[i]

    (sums,) = call(
        dots, [((8, cols), F32)], (*ys, *msgs, *keeps, r, w1), smem=0, flops=10**9
    )

    def norms(*refs):
        keep_refs, got, in_ref, out_ref = refs[:3], refs[3:6], refs[6], refs[7]
        out_ref[...] = in_ref[...]
        square = jnp.zeros((1, cols), F32)
        for a in range(3):
            both = keep_refs[a][...] + got[a][...]
            square += colsum(both * both)
        out_ref[5:6, :] = square

    (sums,) = call(norms, [((8, cols), F32)], (*keeps, *came, sums), smem=0)
    sums = total(sums)

    def finish(table_ref, z1_ref, z2_ref, gram_ref, out_ref, res_ref, z_buf, zero_buf, z_sems, zero_sems):
        def live_copy(i):
            b = table_ref[i % cap, i // cap]
            to = out_ref.at[pl.ds(pl.multiple_of(b * blk, blk), blk), :]
            return pltpu.make_async_copy(z_buf.at[i], to, z_sems.at[i])

        def dead_copy(b):
            return pltpu.make_async_copy(zero_buf, out_ref.at[pl.ds(b * blk, blk), :], zero_sems.at[b])

        zero_buf[...] = jnp.zeros_like(zero_buf)
        dead = []
        for b in range(nblk):
            hits = jnp.int32(0)
            for i in range(slots):
                hits += (table_ref[i % cap, i // cap] == b).astype(jnp.int32)
            dead.append(hits == 0)

            @pl.when(dead[b])
            def _():
                dead_copy(b).start()

        load_square = gram_ref[0:1, :]
        initial = jnp.sqrt(load_square + epsilon)
        rescale = 1.0 / initial
        scale2 = rescale * rescale
        h11 = gram_ref[1:2, :] * scale2
        b11 = gram_ref[2:3, :] * scale2
        c1v = gram_ref[3:4, :] * scale2
        c11 = gram_ref[4:5, :] * scale2
        e11 = gram_ref[5:6, :] * scale2
        g11 = load_square * scale2
        w_square = jnp.maximum(b11 - h11 * h11 * (2.0 - g11), 0.0)
        h21 = jnp.sqrt(w_square + epsilon)
        down = 1.0 / h21
        g22 = w_square * down * down
        g12 = h11 * (epsilon * scale2) * down
        h12 = (c1v - h11 * h11) * down
        dot22 = ((c11 - h11 * c1v) - h11 * (b11 - h11 * h11)) * down * down
        square = ((e11 - h11 * c11) - h11 * (c11 - h11 * b11)) * down * down
        h22 = dot22 - h12 * g12
        left = square - h12 * h12 * (2.0 - g11) - h22 * (2.0 * dot22 - h22 * g22) + 2.0 * h12 * h22 * g12
        h32 = jnp.sqrt(jnp.maximum(left, 0.0) + epsilon)
        r1 = jnp.sqrt(h11 * h11 + h21 * h21)
        c1, s1 = h11 / r1, h21 / r1
        top = c1 * h12 + s1 * h22
        bottom = c1 * h22 - s1 * h12
        r2 = jnp.sqrt(bottom * bottom + h32 * h32)
        c2, s2 = bottom / r2, h32 / r2
        y2 = -initial * s1 * c2 / r2
        y1 = (initial * c1 - top * y2) / r1
        res_ref[...] = initial * s1 * s2
        a2 = y2 * down * rescale
        a1 = y1 * rescale - a2 * h11
        for i in range(slots):
            z_buf[i] = a1 * z1_ref[i * blk : (i + 1) * blk, :] + a2 * z2_ref[i * blk : (i + 1) * blk, :]

            @pl.when(table_ref[i % cap, i // cap] < nblk)
            def _():
                live_copy(i).start()

        for b in range(nblk):

            @pl.when(dead[b])
            def _():
                dead_copy(b).wait()

        for i in range(slots):

            @pl.when(table_ref[i % cap, i // cap] < nblk)
            def _():
                live_copy(i).wait()

    out, res = call(
        finish,
        [((order, cols), F32), ((1, cols), F32)],
        (table, z1, z2, sums),
        scratch=(
            pltpu.VMEM((slots, blk, cols), F32),
            pltpu.VMEM((blk, cols), F32),
            pltpu.SemaphoreType.DMA((slots,)),
            pltpu.SemaphoreType.DMA((nblk,)),
        ),
        hbm_out=(0,),
    )
    return out.reshape(1, 1, 1, order, cols), res.reshape(cols)


def solution(mesh):
    torus = Mesh(
        mesh.devices.reshape(mesh.shape["gx"], mesh.shape["gy"], 4, 2), ("gx", "gy", "gz_0", "gz_1")
    )
    in_specs = (
        P("gx", "gy", GZ, None, None),
        P("gx", "gy", GZ, None),
        P("gx", "gy", GZ, None, None, None),
        P("gx", "gy", GZ, None, None),
        P("gx", "gy", GZ, None, None),
    )
    out_specs = (P("gx", "gy", GZ, None, None), P())
    return jax.shard_map(
        on_device, mesh=torus, in_specs=in_specs, out_specs=out_specs, check_vma=False
    )
```

time: 90.7 us -> 94.9 us (1.046)
  Pallas kernels: 19.4 us -> 23.4 us
  starting transfers between devices: 25.1 us -> 28.6 us
  waiting for transfers between devices: 15.2 us -> 13 us
  blocking collectives: 29.4 us -> 28.4 us
    pallas_call x6 -> x11, Pallas kernels: 19.4 us -> 23.4 us  [call(): pl.pallas_call(body, out_shape=[jax.ShapeDtypeStruct(s, t) for s, t in ou...]
    ppermute x15, starting transfers between devices: 25.1 us -> 28.6 us  [the longest x6 13.4 us: exchange(): lax.ppermute(to_previous, axis, down)]
    ppermute x15, waiting for transfers between devices: 15.2 us -> 13 us  [the longest x6 6.33 us: exchange(): lax.ppermute(to_next, axis, up)]
    all_to_all x2, blocking collectives: 29.4 us -> 28.4 us  [gather_sum(): wide = lax.all_to_all(wide, axes, 0, 0, tiled=True)]
  transfers between devices with their start and end apart: 15 -> 15, of which waited for: 7 -> 6; matrix products, arithmetic and copies ran while one was open for 0% -> 0% of each run, Pallas kernels for 4% -> 8%
where the time goes in v3:
time: 94.9 us; the launch traced here: 94.4 us
  starting transfers between devices  28.6 us (30%)
  blocking collectives  28.4 us (30%)
  Pallas kernels  23.4 us (25%)
  waiting for transfers between devices  13 us (14%)
  between operations  0.95 us (1%)
    all_to_all x2, blocking collectives, gather_sum(): wide = lax.all_to_all(wide, axes, 0, 0, tiled=True)  28.4 us
    pallas_call x11, Pallas kernels, call(): pl.pallas_call(body, out_shape=[jax.ShapeDtypeStruct(s, t) for s, t in ou...  23.4 us
    ppermute x6, starting transfers between devices, exchange(): lax.ppermute(to_previous, axis, down)  13.4 us
    ppermute x6, starting transfers between devices, exchange(): lax.ppermute(to_next, axis, up)  7.67 us
    ppermute x6, waiting for transfers between devices, exchange(): lax.ppermute(to_next, axis, up)  6.33 us
    ppermute x2, starting transfers between devices, exchange_once(): return lax.ppermute(message, (axis, 'gz_1'), pairs)  4.52 us
    ppermute x6, waiting for transfers between devices, exchange(): lax.ppermute(to_previous, axis, down)  4.16 us
    ppermute x1, starting transfers between devices, exchange_once(): return lax.ppermute(message, GZ, shifts(GZ)[0])  2.99 us
  transfers between devices with their start and end apart: 15, of which 6 were waited for; matrix products, arithmetic and copies ran while one was open for 0% of the time, Pallas kernels for 8%

profile of v3, /device:TPU:1, one launch (start us, length us, event | category | flops | bytes accessed | tf_op | source)
XLA Modules:
  0.0 94.4 jit_solution(11387557008623605129)
XLA Ops:
  0.6 2.3 %shard_map.68 = (f32[256,384]{1,0:T(8,128)S(1)}, f32[256,384]{1,0:T(8,128)S(1)}, f32[256,384]{1,0:T(8,128)S(1)}, f32[256,384]{1,0:T(8,128)S(1)}, f32[256,384]{1,0:T(8,128)S(1)}, /*index=5*/f32[256,384]{1,0:T(8,128)S(1)}) custom-call(s32[2,6]{1,0:T(2,128)} %bitcast.18, bf16[2048,256]{1,0:T(8,128)(2,1)} %bitcast.16, f32[16,128,128]{2,1,0:T(8,128)} %bitcast.17), custom_call_target="tpu_custom_call" | custom-call | bytes 1048576 | tf_op jit(solution)/shard_map/pallas_call | solution.py:31
  3.0 2.6 %collective-permute-start.1 = (f32[256,384]{1,0:T(8,128)S(1)}, f32[256,384]{1,0:T(8,128)S(1)}, u32[]{:S(2)}, u32[]{:S(2)}) collective-permute-start(f32[256,384]{1,0:T(8,128)S(1)} %get-tuple-element.29.refs_0_), channel_id=1, source_target_pairs={{0,32},{32,64},{64,96},{96,128},{128,160},{160,192},{192,224},{224... | collective-permute-start | bytes 1179656 | tf_op jit(solution)/shard_map/ppermute | solution.py:52
  5.5 4.1 %collective-permute-start = (f32[256,384]{1,0:T(8,128)S(1)}, f32[256,384]{1,0:T(8,128)S(1)}, u32[]{:S(2)}, u32[]{:S(2)}) collective-permute-start(f32[256,384]{1,0:T(8,128)S(1)} %get-tuple-element.30.refs_1_), channel_id=1, source_target_pairs={{32,0},{64,32},{96,64},{128,96},{160,128},{192,160},{224,192},{0,2... | collective-permute-start | bytes 1179656 | tf_op jit(solution)/shard_map/ppermute | solution.py:52
  9.7 1.2 %collective-permute-start.3 = (f32[256,384]{1,0:T(8,128)S(1)}, f32[256,384]{1,0:T(8,128)S(1)}, u32[]{:S(2)}, u32[]{:S(2)}) collective-permute-start(f32[256,384]{1,0:T(8,128)S(1)} %get-tuple-element.31.refs_2_), channel_id=1, source_target_pairs={{0,8},{8,16},{16,24},{24,0},{1,9},{9,17},{17,25},{25,1},{2,10},{10... | collective-permute-start | bytes 1179656 | tf_op jit(solution)/shard_map/ppermute | solution.py:52
  10.8 1.7 %collective-permute-start.2 = (f32[256,384]{1,0:T(8,128)S(1)}, f32[256,384]{1,0:T(8,128)S(1)}, u32[]{:S(2)}, u32[]{:S(2)}) collective-permute-start(f32[256,384]{1,0:T(8,128)S(1)} %get-tuple-element.32.refs_3_), channel_id=1, source_target_pairs={{8,0},{16,8},{24,16},{0,24},{9,1},{17,9},{25,17},{1,25},{10,2},{18... | collective-permute-start | bytes 1179656 | tf_op jit(solution)/shard_map/ppermute | solution.py:52
  12.5 2.4 %collective-permute-start.5 = (f32[256,384]{1,0:T(8,128)S(1)}, f32[256,384]{1,0:T(8,128)S(1)}, u32[]{:S(2)}, u32[]{:S(2)}) collective-permute-start(f32[256,384]{1,0:T(8,128)S(1)} %get-tuple-element.33.refs_4_), channel_id=1, source_target_pairs={{0,1},{1,2},{2,3},{3,4},{4,5},{5,6},{6,7},{7,0},{8,9},{9,10},{10,1... | collective-permute-start | bytes 1179656 | tf_op jit(solution)/shard_map/ppermute | solution.py:52
  14.9 3.5 %collective-permute-done.1.refs_7_ = f32[256,384]{1,0:T(8,128)S(1)} collective-permute-done((f32[256,384]{1,0:T(8,128)S(1)}, f32[256,384]{1,0:T(8,128)S(1)}, u32[]{:S(2)}, u32[]{:S(2)}) %collective-permute-start.1) | collective-permute-done | bytes 393248 | tf_op jit(solution)/shard_map/ppermute | solution.py:52
  18.4 1.3 %collective-permute-start.4 = (f32[256,384]{1,0:T(8,128)S(1)}, f32[256,384]{1,0:T(8,128)S(1)}, u32[]{:S(2)}, u32[]{:S(2)}) collective-permute-start(f32[256,384]{1,0:T(8,128)S(1)} %get-tuple-element.34.refs_5_), channel_id=1, source_target_pairs={{1,0},{2,1},{3,2},{4,3},{5,4},{6,5},{7,6},{0,7},{9,8},{10,9},{11,1... | collective-permute-start | bytes 1179656 | tf_op jit(solution)/shard_map/ppermute | solution.py:52
  19.6 3.8 %shard_map.69.refs_13_.s_ref.refs_14_ = bf16[1536,2048]{1,0:T(8,128)(2,1)S(1)} custom-call(s32[2,6]{1,0:T(2,128)} %bitcast.19, bf16[2048,2048]{1,0:T(8,128)(2,1)} %bitcast.15), custom_call_target="tpu_custom_call" | custom-call | flops 2000000000 | bytes 1048576 | tf_op jit(solution)/shard_map/pallas_call | solution.py:31
  23.5 2.6 %collective-permute-done.4.refs_10_ = f32[256,384]{1,0:T(8,128)S(1)} collective-permute-done((f32[256,384]{1,0:T(8,128)S(1)}, f32[256,384]{1,0:T(8,128)S(1)}, u32[]{:S(2)}, u32[]{:S(2)}) %collective-permute-start.4) | collective-permute-done | bytes 393248 | tf_op jit(solution)/shard_map/ppermute | solution.py:52
  26.1 4.0 %shard_map.70 = (f32[1536,256]{1,0:T(8,128)S(1)}, f32[1536,256]{1,0:T(8,128)S(1)}, bf16[1536,256]{1,0:T(8,128)(2,1)S(1)}, bf16[2048,256]{1,0:T(8,128)(2,1)S(1)},...) custom-call(s32[2,6]{1,0:T(2,128)} %bitcast.20, f32[256,384]{1,0:T(8,128)S(1)} %get-tuple-element.29.refs_0_, ...), custom_call_target="tpu_custom_call" | custom-call | flops 2000000000 | bytes 1048576 | tf_op jit(solution)/shard_map/pallas_call | solution.py:31
  30.2 2.7 %collective-permute-start.6 = (f32[256,256]{1,0:T(8,128)S(1)}, f32[256,256]{1,0:T(8,128)S(1)}, u32[]{:S(2)}, u32[]{:S(2)}) collective-permute-start(f32[256,256]{1,0:T(8,128)S(1)} %get-tuple-element.37.refs_1_), channel_id=1, source_target_pairs={{32,0},{64,32},{96,64},{128,96},{160,128},{192,160},{224,192},{0,2... | collective-permute-start | bytes 786440 | tf_op jit(solution)/shard_map/ppermute | solution.py:52
  32.9 1.4 %shard_map.72 = (f32[256,256]{1,0:T(8,128)S(1)}, f32[256,256]{1,0:T(8,128)S(1)}) custom-call(s32[2,6]{1,0:T(2,128)} %bitcast.21, bf16[2048,256]{1,0:T(8,128)(2,1)S(1)} %get-tuple-element.38.zb_ref, f32[1536,256]{1,0:T(8,128)S(1)} %get-tuple-element.35.z_ref.z1_ref, f32[16,128]{1,0:T(8,128)S(1)} %bitcast.10, ...), custom_call_target="tpu_custom_call" | custom-call | flops 1000000000 | bytes 1048576 | tf_op jit(solution)/shard_map/pallas_call | solution.py:31
  34.3 0.4 collective-permute-start.11
  34.7 0.9 collective-permute-start.10
  35.6 1.4 %shard_map.71 = (f32[256,256]{1,0:T(8,128)S(1)}, f32[256,256]{1,0:T(8,128)S(1)}) custom-call(s32[2,6]{1,0:T(2,128)} %bitcast.22, bf16[2048,256]{1,0:T(8,128)(2,1)S(1)} %get-tuple-element.38.zb_ref, f32[1536,256]{1,0:T(8,128)S(1)} %get-tuple-element.35.z_ref.z1_ref, f32[16,128]{1,0:T(8,128)S(1)} %bitcast.11, ...), custom_call_target="tpu_custom_call" | custom-call | flops 1000000000 | bytes 1048576 | tf_op jit(solution)/shard_map/pallas_call | solution.py:31
  37.0 1.1 %collective-permute-start.9 = (f32[256,256]{1,0:T(8,128)S(1)}, f32[256,256]{1,0:T(8,128)S(1)}, u32[]{:S(2)}, u32[]{:S(2)}) collective-permute-start(f32[256,256]{1,0:T(8,128)S(1)} %get-tuple-element.39.refs_2_), channel_id=1, source_target_pairs={{0,8},{8,16},{16,24},{24,0},{1,9},{9,17},{17,25},{25,1},{2,10},{10... | collective-permute-start | bytes 786440 | tf_op jit(solution)/shard_map/ppermute | solution.py:52
  38.1 0.4 collective-permute-done.7.refs_7_
  38.5 2.7 %collective-permute-start.8 = (f32[256,256]{1,0:T(8,128)S(1)}, f32[256,256]{1,0:T(8,128)S(1)}, u32[]{:S(2)}, u32[]{:S(2)}) collective-permute-start(f32[256,256]{1,0:T(8,128)S(1)} %get-tuple-element.40.refs_3_), channel_id=1, source_target_pairs={{8,0},{16,8},{24,16},{0,24},{9,1},{17,9},{25,17},{1,25},{10,2},{18... | collective-permute-start | bytes 786440 | tf_op jit(solution)/shard_map/ppermute | solution.py:52
  41.3 2.4 %collective-permute-done.9.refs_9_ = f32[256,256]{1,0:T(8,128)S(1)} collective-permute-done((f32[256,256]{1,0:T(8,128)S(1)}, f32[256,256]{1,0:T(8,128)S(1)}, u32[]{:S(2)}, u32[]{:S(2)}) %collective-permute-start.9) | collective-permute-done | bytes 262176 | tf_op jit(solution)/shard_map/ppermute | solution.py:52
  43.7 1.5 %collective-permute-done.8.refs_8_ = f32[256,256]{1,0:T(8,128)S(1)} collective-permute-done((f32[256,256]{1,0:T(8,128)S(1)}, f32[256,256]{1,0:T(8,128)S(1)}, u32[]{:S(2)}, u32[]{:S(2)}) %collective-permute-start.8) | collective-permute-done | bytes 262176 | tf_op jit(solution)/shard_map/ppermute | solution.py:52
  45.2 4.0 %shard_map.73 = (f32[1536,256]{1,0:T(8,128)S(1)}, f32[1536,256]{1,0:T(8,128)S(1)}, bf16[2048,256]{1,0:T(8,128)(2,1)S(1)}, f32[256,256]{1,0:T(8,128)S(1)}, f32[256,256]{1,0:T(8,128)S(1)}) custom-call(s32[2,6]{1,0:T(2,128)} %bitcast.23, f32[256,256]{1,0:T(8,128)S(1)} %get-tuple-element.36.refs_0_, f32[256,256]{1,0:T(8,128)S(1)} %get-tuple-element.37.refs_1_, ...), custom_call_target="tpu_custom_call" | custom-call | flops 2000000000 | bytes 1048576 | tf_op jit(solution)/shard_map/pallas_call | solution.py:31
  49.2 1.4 %shard_map.75 = (f32[256,256]{1,0:T(8,128)S(1)}, f32[256,256]{1,0:T(8,128)S(1)}) custom-call(s32[2,6]{1,0:T(2,128)} %bitcast.24, bf16[2048,256]{1,0:T(8,128)(2,1)S(1)} %get-tuple-element.46.zb_ref, f32[1536,256]{1,0:T(8,128)S(1)} %get-tuple-element.44.z_ref.z2_ref, f32[16,128]{1,0:T(8,128)S(1)} %bitcast.13, ...), custom_call_target="tpu_custom_call" | custom-call | flops 1000000000 | bytes 1048576 | tf_op jit(solution)/shard_map/pallas_call | solution.py:31
  50.6 1.4 %shard_map.74 = (f32[256,256]{1,0:T(8,128)S(1)}, f32[256,256]{1,0:T(8,128)S(1)}) custom-call(s32[2,6]{1,0:T(2,128)} %bitcast.25, bf16[2048,256]{1,0:T(8,128)(2,1)S(1)} %get-tuple-element.46.zb_ref, f32[1536,256]{1,0:T(8,128)S(1)} %get-tuple-element.44.z_ref.z2_ref, f32[16,128]{1,0:T(8,128)S(1)} %bitcast.14, ...), custom_call_target="tpu_custom_call" | custom-call | flops 1000000000 | bytes 1048576 | tf_op jit(solution)/shard_map/pallas_call | solution.py:31
  52.0 1.1 %collective-permute-start.12 = (f32[256,256]{1,0:T(8,128)S(1)}, f32[256,256]{1,0:T(8,128)S(1)}, u32[]{:S(2)}, u32[]{:S(2)}) collective-permute-start(f32[256,256]{1,0:T(8,128)S(1)} %get-tuple-element.49.refs_6_), channel_id=1, source_target_pairs={{0,32},{1,225},{32,64},{33,1},{64,96},{65,33},{96,128},{97,65},{12... | collective-permute-start | bytes 786440 | tf_op jit(solution)/shard_map/ppermute | solution.py:62
  53.1 3.0 %collective-permute-start.14 = (f32[256,256]{1,0:T(8,128)S(1)}, f32[256,256]{1,0:T(8,128)S(1)}, u32[]{:S(2)}, u32[]{:S(2)}) collective-permute-start(f32[256,256]{1,0:T(8,128)S(1)} %get-tuple-element.51.refs_8_), channel_id=1, source_target_pairs={{0,1},{1,2},{2,3},{3,4},{4,5},{5,6},{6,7},{7,0},{8,9},{9,10},{10,1... | collective-permute-start | bytes 786440 | tf_op jit(solution)/shard_map/ppermute | solution.py:57
  56.1 3.4 %collective-permute-start.13 = (f32[256,256]{1,0:T(8,128)S(1)}, f32[256,256]{1,0:T(8,128)S(1)}, u32[]{:S(2)}, u32[]{:S(2)}) collective-permute-start(f32[256,256]{1,0:T(8,128)S(1)} %get-tuple-element.50.refs_7_), channel_id=1, source_target_pairs={{0,8},{1,25},{8,16},{9,1},{16,24},{17,9},{24,0},{25,17},{2,10},{3,... | collective-permute-start | bytes 786440 | tf_op jit(solution)/shard_map/ppermute | solution.py:62
  59.5 0.8 shard_map.76.refs_6_
  60.3 2.5 %collective-permute-done.13.refs_4_ = f32[256,256]{1,0:T(8,128)S(1)} collective-permute-done((f32[256,256]{1,0:T(8,128)S(1)}, f32[256,256]{1,0:T(8,128)S(1)}, u32[]{:S(2)}, u32[]{:S(2)}) %collective-permute-start.13) | collective-permute-done | bytes 262176 | tf_op jit(solution)/shard_map/ppermute | solution.py:62
  63.0 16.0 %all_to_all.12 = f32[32,8,256]{2,1,0:T(8,128)S(1)} all-to-all(f32[32,8,256]{2,1,0:T(8,128)S(1)} %broadcast_in_dim.4), channel_id=1, replica_groups=mesh['gx'=8,'gy'=4,'gz_0'=4,'gz_1'=2] {'gy','gz_0','gz_1'}, dimensions={0} | all-to-all | bytes 524288 | tf_op jit(solution)/shard_map/all_to_all | solution.py:68
  79.0 12.4 %all_to_all.13 = f32[8,8,256]{2,1,0:T(8,128)S(1)} all-to-all(f32[8,8,256]{2,1,0:T(8,128)S(1)} %broadcast_in_dim.5), channel_id=1, replica_groups=mesh['gx'=8,'gy'=4,'gz_0'=4,'gz_1'=2] {'gx'}, dimensions={0} | all-to-all | bytes 131072 | tf_op jit(solution)/shard_map/all_to_all | solution.py:68
  91.5 2.8 %shard_map.78 = (f32[2048,256]{1,0:T(8,128)}, f32[1,256]{1,0:T(1,128)}) custom-call(s32[2,6]{1,0:T(2,128)} %bitcast.26, f32[1536,256]{1,0:T(8,128)S(1)} %get-tuple-element.35.z_ref.z1_ref, f32[1536,256]{1,0:T(8,128)S(1)} %get-tuple-element.44.z_ref.z2_ref, f32[8,256]{1,0:T(8,128)S(1)} %reduce_sum.19.gram_ref), custom_call_target="tpu_custom_call" | custom-call | bytes 1048576 | tf_op jit(solution)/shard_map/pallas_call | solution.py:31
  (17 shorter events, 0.3 us)
Async XLA Ops:
  3.0 15.4 %collective-permute-start.1 = (f32[256,384]{1,0:T(8,128)S(1)}, f32[256,384]{1,0:T(8,128)S(1)}, u32[]{:S(2)}, u32[]{:S(2)}) collective-permute-start(f32[256,384]{1,0:T(8,128)S(1)} %get-tuple-element.29.refs_0_), channel_id=1, source_target_pairs={{0,32},{32,64},{64,96},{96,128},{128,160},{160,192},{192,224},{224... | collective-permute-start | bytes 1179656 | tf_op jit(solution)/shard_map/ppermute | solution.py:52
  5.5 17.9 %collective-permute-start = (f32[256,384]{1,0:T(8,128)S(1)}, f32[256,384]{1,0:T(8,128)S(1)}, u32[]{:S(2)}, u32[]{:S(2)}) collective-permute-start(f32[256,384]{1,0:T(8,128)S(1)} %get-tuple-element.30.refs_1_), channel_id=1, source_target_pairs={{32,0},{64,32},{96,64},{128,96},{160,128},{192,160},{224,192},{0,2... | collective-permute-start | bytes 1179656 | tf_op jit(solution)/shard_map/ppermute | solution.py:52
  9.7 13.8 %collective-permute-start.3 = (f32[256,384]{1,0:T(8,128)S(1)}, f32[256,384]{1,0:T(8,128)S(1)}, u32[]{:S(2)}, u32[]{:S(2)}) collective-permute-start(f32[256,384]{1,0:T(8,128)S(1)} %get-tuple-element.31.refs_2_), channel_id=1, source_target_pairs={{0,8},{8,16},{16,24},{24,0},{1,9},{9,17},{17,25},{25,1},{2,10},{10... | collective-permute-start | bytes 1179656 | tf_op jit(solution)/shard_map/ppermute | solution.py:52
  10.8 12.7 %collective-permute-start.2 = (f32[256,384]{1,0:T(8,128)S(1)}, f32[256,384]{1,0:T(8,128)S(1)}, u32[]{:S(2)}, u32[]{:S(2)}) collective-permute-start(f32[256,384]{1,0:T(8,128)S(1)} %get-tuple-element.32.refs_3_), channel_id=1, source_target_pairs={{8,0},{16,8},{24,16},{0,24},{9,1},{17,9},{25,17},{1,25},{10,2},{18... | collective-permute-start | bytes 1179656 | tf_op jit(solution)/shard_map/ppermute | solution.py:52
  12.5 11.0 %collective-permute-start.5 = (f32[256,384]{1,0:T(8,128)S(1)}, f32[256,384]{1,0:T(8,128)S(1)}, u32[]{:S(2)}, u32[]{:S(2)}) collective-permute-start(f32[256,384]{1,0:T(8,128)S(1)} %get-tuple-element.33.refs_4_), channel_id=1, source_target_pairs={{0,1},{1,2},{2,3},{3,4},{4,5},{5,6},{6,7},{7,0},{8,9},{9,10},{10,1... | collective-permute-start | bytes 1179656 | tf_op jit(solution)/shard_map/ppermute | solution.py:52
  18.4 7.8 %collective-permute-start.4 = (f32[256,384]{1,0:T(8,128)S(1)}, f32[256,384]{1,0:T(8,128)S(1)}, u32[]{:S(2)}, u32[]{:S(2)}) collective-permute-start(f32[256,384]{1,0:T(8,128)S(1)} %get-tuple-element.34.refs_5_), channel_id=1, source_target_pairs={{1,0},{2,1},{3,2},{4,3},{5,4},{6,5},{7,6},{0,7},{9,8},{10,9},{11,1... | collective-permute-start | bytes 1179656 | tf_op jit(solution)/shard_map/ppermute | solution.py:52
  19.6 6.5 %copy-start = (f32[1,1,1,2048]{3,2,1,0:T(1,128)S(1)}, f32[1,1,1,2048]{3,2,1,0:T(1,128)}, u32[]{:S(2)}) copy-start(f32[1,1,1,2048]{3,2,1,0:T(1,128)} %param.6) | copy-start | bytes 24580
  30.1 8.4 %collective-permute-start.7 = (f32[256,256]{1,0:T(8,128)S(1)}, f32[256,256]{1,0:T(8,128)S(1)}, u32[]{:S(2)}, u32[]{:S(2)}) collective-permute-start(f32[256,256]{1,0:T(8,128)S(1)} %get-tuple-element.36.refs_0_), channel_id=1, source_target_pairs={{0,32},{32,64},{64,96},{96,128},{128,160},{160,192},{192,224},{224... | collective-permute-start | bytes 786440 | tf_op jit(solution)/shard_map/ppermute | solution.py:52
  30.2 11.1 %collective-permute-start.6 = (f32[256,256]{1,0:T(8,128)S(1)}, f32[256,256]{1,0:T(8,128)S(1)}, u32[]{:S(2)}, u32[]{:S(2)}) collective-permute-start(f32[256,256]{1,0:T(8,128)S(1)} %get-tuple-element.37.refs_1_), channel_id=1, source_target_pairs={{32,0},{64,32},{96,64},{128,96},{160,128},{192,160},{224,192},{0,2... | collective-permute-start | bytes 786440 | tf_op jit(solution)/shard_map/ppermute | solution.py:52
  34.3 7.0 %collective-permute-start.11 = (f32[256,256]{1,0:T(8,128)S(1)}, f32[256,256]{1,0:T(8,128)S(1)}, u32[]{:S(2)}, u32[]{:S(2)}) collective-permute-start(f32[256,256]{1,0:T(8,128)S(1)} %get-tuple-element.41.refs_4_), channel_id=1, source_target_pairs={{0,1},{1,2},{2,3},{3,4},{4,5},{5,6},{6,7},{7,0},{8,9},{9,10},{10,1... | collective-permute-start | bytes 786440 | tf_op jit(solution)/shard_map/ppermute | solution.py:52
  34.7 6.6 %collective-permute-start.10 = (f32[256,256]{1,0:T(8,128)S(1)}, f32[256,256]{1,0:T(8,128)S(1)}, u32[]{:S(2)}, u32[]{:S(2)}) collective-permute-start(f32[256,256]{1,0:T(8,128)S(1)} %get-tuple-element.42.refs_5_), channel_id=1, source_target_pairs={{1,0},{2,1},{3,2},{4,3},{5,4},{6,5},{7,6},{0,7},{9,8},{10,9},{11,1... | collective-permute-start | bytes 786440 | tf_op jit(solution)/shard_map/ppermute | solution.py:52
  37.0 6.7 %collective-permute-start.9 = (f32[256,256]{1,0:T(8,128)S(1)}, f32[256,256]{1,0:T(8,128)S(1)}, u32[]{:S(2)}, u32[]{:S(2)}) collective-permute-start(f32[256,256]{1,0:T(8,128)S(1)} %get-tuple-element.39.refs_2_), channel_id=1, source_target_pairs={{0,8},{8,16},{16,24},{24,0},{1,9},{9,17},{17,25},{25,1},{2,10},{10... | collective-permute-start | bytes 786440 | tf_op jit(solution)/shard_map/ppermute | solution.py:52
  38.5 6.7 %collective-permute-start.8 = (f32[256,256]{1,0:T(8,128)S(1)}, f32[256,256]{1,0:T(8,128)S(1)}, u32[]{:S(2)}, u32[]{:S(2)}) collective-permute-start(f32[256,256]{1,0:T(8,128)S(1)} %get-tuple-element.40.refs_3_), channel_id=1, source_target_pairs={{8,0},{16,8},{24,16},{0,24},{9,1},{17,9},{25,17},{1,25},{10,2},{18... | collective-permute-start | bytes 786440 | tf_op jit(solution)/shard_map/ppermute | solution.py:52
  52.0 8.3 %collective-permute-start.12 = (f32[256,256]{1,0:T(8,128)S(1)}, f32[256,256]{1,0:T(8,128)S(1)}, u32[]{:S(2)}, u32[]{:S(2)}) collective-permute-start(f32[256,256]{1,0:T(8,128)S(1)} %get-tuple-element.49.refs_6_), channel_id=1, source_target_pairs={{0,32},{1,225},{32,64},{33,1},{64,96},{65,33},{96,128},{97,65},{12... | collective-permute-start | bytes 786440 | tf_op jit(solution)/shard_map/ppermute | solution.py:62
  53.1 7.2 %collective-permute-start.14 = (f32[256,256]{1,0:T(8,128)S(1)}, f32[256,256]{1,0:T(8,128)S(1)}, u32[]{:S(2)}, u32[]{:S(2)}) collective-permute-start(f32[256,256]{1,0:T(8,128)S(1)} %get-tuple-element.51.refs_8_), channel_id=1, source_target_pairs={{0,1},{1,2},{2,3},{3,4},{4,5},{5,6},{6,7},{7,0},{8,9},{9,10},{10,1... | collective-permute-start | bytes 786440 | tf_op jit(solution)/shard_map/ppermute | solution.py:57
  56.1 6.7 %collective-permute-start.13 = (f32[256,256]{1,0:T(8,128)S(1)}, f32[256,256]{1,0:T(8,128)S(1)}, u32[]{:S(2)}, u32[]{:S(2)}) collective-permute-start(f32[256,256]{1,0:T(8,128)S(1)} %get-tuple-element.50.refs_7_), channel_id=1, source_target_pairs={{0,8},{1,25},{8,16},{9,1},{16,24},{17,9},{24,0},{25,17},{2,10},{3,... | collective-permute-start | bytes 786440 | tf_op jit(solution)/shard_map/ppermute | solution.py:62

commit v4 on v3

v4 whole, which is shorter than its diff:
```python
import functools

import jax
import jax.numpy as jnp
from jax import lax
from jax.experimental import pallas as pl
from jax.experimental.pallas import tpu as pltpu
from jax.sharding import Mesh
from jax.sharding import PartitionSpec as P

GZ = ("gz_0", "gz_1")
GROUP = 2
AXES = ("gx", "gy", GZ)
INNER = ("gy", "gz_0", "gz_1")


epsilon = 1e-06
TRUST = 1e-3
F32 = jnp.float32
BF16 = jnp.bfloat16


def call(body, outs, operands, scratch=(), smem=1, raw=(), flops=0, mib=16, flag=False):
    specs = []
    operands = list(operands)
    for i in range(len(operands)):
        if i < smem:
            specs.append(pl.BlockSpec(memory_space=pltpu.SMEM))
            operands[i] = pltpu.with_memory_space_constraint(operands[i], pltpu.HBM)
        elif i in raw:
            specs.append(pl.BlockSpec(memory_space=pltpu.HBM))
            operands[i] = pltpu.with_memory_space_constraint(operands[i], pltpu.HBM)
        else:
            specs.append(pl.BlockSpec(memory_space=pltpu.VMEM))
    return pl.pallas_call(
        body,
        out_shape=[jax.ShapeDtypeStruct(s, t) for s, t in outs]
        + [jax.ShapeDtypeStruct((1,), jnp.int32)] * flag,
        in_specs=specs,
        out_specs=[pl.BlockSpec(memory_space=pltpu.VMEM) for _ in outs]
        + [pl.BlockSpec(memory_space=pltpu.SMEM)] * flag,
        scratch_shapes=list(scratch),
        compiler_params=pltpu.CompilerParams(vmem_limit_bytes=mib * 2**20),
        cost_estimate=pl.CostEstimate(flops=flops, transcendentals=0, bytes_accessed=2**20),
    )(*operands)


def shifts(axis):
    n = lax.axis_size(axis)
    up = [(i, (i + 1) % n) for i in range(n)]
    return up, [(j, i) for i, j in up]


def exchange(to_next, to_previous, axis):
    up, down = shifts(axis)
    return [lax.ppermute(to_previous, axis, down), lax.ppermute(to_next, axis, up)]


def exchange_once(message, axis):
    if axis == GZ:
        return lax.ppermute(message, GZ, shifts(GZ)[0])
    n = lax.axis_size(axis)
    pairs = []
    for i in range(n):
        pairs += [(2 * i, 2 * ((i + 1) % n)), (2 * i + 1, 2 * ((i - 1) % n) + 1)]
    return lax.ppermute(message, (axis, "gz_1"), pairs)


def gather_sum(rows, axes):
    n = lax.axis_size(axes)
    wide = jnp.broadcast_to(rows[None], (n,) + rows.shape).reshape(n * rows.shape[0], rows.shape[1])
    wide = lax.all_to_all(wide, axes, 0, 0, tiled=True)
    return jnp.sum(wide.reshape((n,) + rows.shape), axis=0)


def total(rows):
    return gather_sum(gather_sum(rows, INNER), ("gx",))


def split(x):
    hi = x.astype(BF16)
    return hi, (x - hi.astype(F32)).astype(BF16)


def apply_block(mcat, vec):
    blk = mcat.shape[0]
    hi, lo = split(vec)
    out = jnp.dot(mcat, jnp.concatenate([hi, hi], axis=0), preferred_element_type=F32)
    return out + jnp.dot(mcat[:, :blk], lo, preferred_element_type=F32)


def column(row, blk):
    r = lax.broadcasted_iota(jnp.int32, (blk, blk), 0)
    c = lax.broadcasted_iota(jnp.int32, (blk, blk), 1)
    return jnp.sum(jnp.where(r == c, jnp.broadcast_to(row, (blk, blk)), 0.0), axis=1, keepdims=True)


def colsum(x):
    return jnp.sum(x, axis=0, keepdims=True)


def on_device(schur, interface_diag, precond, load, face_blocks):
    nblk, blk = precond.shape[3], precond.shape[4]
    cols = load.shape[-1]
    order = nblk * blk
    cap = face_blocks.shape[-1]
    slots = 6 * cap
    rows = cap * blk
    table = face_blocks.reshape(6, cap).T
    matrix = schur.reshape(order, order)
    diag = interface_diag.reshape(nblk, blk)

    def pick(table_ref, i):
        b = table_ref[i % cap, i // cap]
        return jnp.minimum(b, nblk - 1), (b < nblk).astype(F32)

    def pack():
        def body(table_ref, load_ref, pre_ref, *refs):
            outs = refs[:6]
            load_buf, pre_buf, load_sems, pre_sems = refs[6:]
            copies = []
            for i in range(slots):
                b, _ = pick(table_ref, i)
                at = pl.multiple_of(b * blk, blk)
                copies.append(
                    (
                        pltpu.make_async_copy(load_ref.at[pl.ds(at, blk), :], load_buf.at[i], load_sems.at[i]),
                        pltpu.make_async_copy(pre_ref.at[b], pre_buf.at[i], pre_sems.at[i]),
                    )
                )
                for copy in copies[-1]:
                    copy.start()
            for i in range(slots):
                _, m = pick(table_ref, i)
                out, at = outs[i // cap], (i % cap) * blk
                for copy in copies[i]:
                    copy.wait()
                out[at : at + blk, :cols] = load_buf[i].astype(F32) * m
                out[at : at + blk, cols:] = pre_buf[i] * m

        return call(
            body,
            [((rows, cols + blk), F32)] * 6,
            (table, load.reshape(order, cols), precond.reshape(nblk, blk, blk)),
            scratch=(
                pltpu.VMEM((slots, blk, cols), BF16),
                pltpu.VMEM((slots, blk, blk), F32),
                pltpu.SemaphoreType.DMA((slots,)),
                pltpu.SemaphoreType.DMA((slots,)),
            ),
            raw=(1, 2),
            flops=10**8,
        )

    faces = pack()
    came = [x for a in range(3) for x in exchange(faces[2 * a], faces[2 * a + 1], AXES[a])]

    def fetch(table_ref, matrix_ref, s_ref, sems):
        copies = []
        for i in range(slots):
            b, _ = pick(table_ref, i)
            copy = pltpu.make_async_copy(
                matrix_ref.at[pl.ds(pl.multiple_of(b * blk, blk), blk), :],
                s_ref.at[pl.ds(i * blk, blk), :],
                sems.at[i],
            )
            copy.start()
            copies.append(copy)
        for copy in copies:
            copy.wait()

    def live_rows():
        return call(
            fetch,
            [((slots * blk, order), BF16)],
            (table, matrix),
            scratch=(pltpu.SemaphoreType.DMA((slots,)),),
            raw=(1,),
            flops=2 * 10**9,
        )[0]

    sel = live_rows()

    def spread(table_ref, zb_ref, i, value):
        b = table_ref[i % cap, i // cap]

        @pl.when(b < nblk)
        def _():
            zb_ref[pl.ds(pl.multiple_of(b * blk, blk), blk), :] = value.astype(BF16)

    def local_schur(table_ref, s_ref, zb_ref, z_ref, diag_ref, outs):
        for g in range(0, 6, GROUP):
            product = jnp.dot(
                s_ref[g * rows : (g + GROUP) * rows, :], zb_ref[...], preferred_element_type=F32
            )
            for d in range(g, g + GROUP):
                for k in range(cap):
                    i = d * cap + k
                    b, m = pick(table_ref, i)
                    dcol = column(diag_ref[pl.ds(b, 1), :], blk)
                    z = z_ref[i * blk : (i + 1) * blk, :]
                    at = i * blk - g * rows
                    outs[d][k * blk : (k + 1) * blk, :] = (product[at : at + blk] + dcol * z) * m

    long = slots * blk
    tall = (long, cols)
    flat = (rows, cols)

    def first(table_ref, *refs):
        own, got = refs[:6], refs[6:12]
        diag_ref, s_ref = refs[12:14]
        r_ref, z_ref, m_ref = refs[14:17]
        y_refs, zb_ref = refs[17:23], refs[23]
        zb_ref[...] = jnp.zeros_like(zb_ref)
        for i in range(slots):
            d, at = i // cap, (i % cap) * blk
            r = own[d][at : at + blk, :cols] + got[d][at : at + blk, :cols]
            m = own[d][at : at + blk, cols:] + got[d][at : at + blk, cols:]
            hi, lo = split(m)
            mcat = jnp.concatenate([hi, lo], axis=1)
            m_ref[i * blk : (i + 1) * blk, :] = mcat
            r_ref[i * blk : (i + 1) * blk, :] = r
            z = apply_block(mcat, r)
            z_ref[i * blk : (i + 1) * blk, :] = z
            spread(table_ref, zb_ref, i, z)
        local_schur(table_ref, s_ref, zb_ref, z_ref, diag_ref, y_refs)

    spread_z = (pltpu.VMEM((order, cols), BF16),)
    r, z1, mcat, *ys = call(
        first,
        [(tall, F32), (tall, F32), ((long, 2 * blk), BF16)] + [(flat, F32)] * 6,
        (table, *faces, *came, diag, sel),
        scratch=spread_z,
        flops=2 * 10**9,
    )
    came = [x for a in range(3) for x in exchange(ys[2 * a], ys[2 * a + 1], AXES[a])]

    def sides(axis):
        if axis == 2:
            return 4, 5
        low = lax.axis_index("gz_1") == 0
        return jnp.where(low, 2 * axis, 2 * axis + 1), jnp.where(low, 2 * axis + 1, 2 * axis)

    def second(table_ref, *refs, given=False):
        if given:
            raw_ref, r_ref, gram_ref = refs[:3]
            scale = 1.0 / jnp.sqrt(gram_ref[0:1, :] + epsilon)
            h11 = gram_ref[1:2, :] * scale * scale
            refs = refs[3:]
        else:
            own, got = refs[:6], refs[6:12]
            refs = refs[12:]
        m_ref, diag_ref, s_ref = refs[:3]
        w_ref, z_ref = refs[3:5]
        msg_refs, keep_refs = refs[5:8], refs[8:11]
        refs = refs[11:]
        if given:
            first_ref, *refs = refs
        zb_ref, y_refs = refs[0], refs[1:7]
        zb_ref[...] = jnp.zeros_like(zb_ref)
        for i in range(slots):
            d, at = i // cap, (i % cap) * blk
            if given:
                w = raw_ref[i * blk : (i + 1) * blk, :] - h11 * r_ref[i * blk : (i + 1) * blk, :]
                w = w * scale
                r = r_ref[i * blk : (i + 1) * blk, :]
                first_ref[i * blk : (i + 1) * blk, :] = apply_block(m_ref[i * blk : (i + 1) * blk, :], r)
            else:
                w = own[d][at : at + blk, :] + got[d][at : at + blk, :]
            w_ref[i * blk : (i + 1) * blk, :] = w
            z = apply_block(m_ref[i * blk : (i + 1) * blk, :], w)
            z_ref[i * blk : (i + 1) * blk, :] = z
            spread(table_ref, zb_ref, i, z)
        local_schur(table_ref, s_ref, zb_ref, z_ref, diag_ref, y_refs)
        low = lax.axis_index("gz_1") == 0
        for a in range(2):

            @pl.when(low)
            def _():
                msg_refs[a][...] = y_refs[2 * a][...]
                keep_refs[a][...] = y_refs[2 * a + 1][...]

            @pl.when(jnp.logical_not(low))
            def _():
                msg_refs[a][...] = y_refs[2 * a + 1][...]
                keep_refs[a][...] = y_refs[2 * a][...]

        msg_refs[2][...] = y_refs[4][...]
        keep_refs[2][...] = y_refs[5][...]

    def dots(*refs):
        y_refs, msg_refs, keep_refs = refs[:6], refs[6:9], refs[9:12]
        r_ref, w_ref, out_ref = refs[12:15]
        sums = [jnp.zeros((1, cols), F32) for _ in range(5)]
        for d in range(6):
            r = r_ref[d * rows : (d + 1) * rows, :]
            w = w_ref[d * rows : (d + 1) * rows, :]
            sums[0] += 0.5 * colsum(r * r)
            sums[1] += colsum(r * y_refs[d][...])
            sums[2] += 0.5 * colsum(w * w)
        for a in range(3):
            for d, ref in zip(sides(a), (msg_refs[a], keep_refs[a])):
                at = pl.ds(pl.multiple_of(d * rows, rows), rows)
                y = ref[...]
                sums[3] += colsum(y * r_ref[at, :])
                sums[4] += colsum(y * w_ref[at, :])
        out_ref[...] = jnp.zeros_like(out_ref)
        for i in range(5):
            out_ref[i : i + 1, :] = sums[i]

    def norms(*refs):
        keep_refs, got, in_ref, out_ref = refs[:3], refs[3:6], refs[6], refs[7]
        out_ref[...] = in_ref[...]
        square = jnp.zeros((1, cols), F32)
        for a in range(3):
            both = keep_refs[a][...] + got[a][...]
            square += colsum(both * both)
        out_ref[5:6, :] = square

    def second_step(ys, heads, mcat, sel, r, given=False):
        w, z, *rest = call(
            functools.partial(second, given=given),
            [(tall, F32), (tall, F32)] + [(flat, F32)] * 6 + [(tall, F32)] * given,
            (table, *heads, mcat, diag, sel),
            scratch=spread_z + (pltpu.VMEM(flat, F32),) * 6,
            flops=2 * 10**9,
        )
        msgs, keeps, z1 = rest[:3], rest[3:6], rest[6:]
        got = []
        for a in range(3):
            got.append(exchange_once(msgs[a], AXES[a]))
        (sums,) = call(dots, [((8, cols), F32)], (*ys, *msgs, *keeps, r, w), smem=0, flops=10**9)
        (sums,) = call(norms, [((8, cols), F32)], (*keeps, *got, sums), smem=0)
        return w, z, total(sums), z1

    w1, z2, sums, _ = second_step(ys, (*ys, *came), mcat, sel, r)

    def weights(initial, h11, h21, h12, h22, h32):
        r1 = jnp.sqrt(h11 * h11 + h21 * h21)
        c1, s1 = h11 / r1, h21 / r1
        top = c1 * h12 + s1 * h22
        bottom = c1 * h22 - s1 * h12
        r2 = jnp.sqrt(bottom * bottom + h32 * h32)
        c2, s2 = bottom / r2, h32 / r2
        y2 = -initial * s1 * c2 / r2
        y1 = (initial * c1 - top * y2) / r1
        return y1, y2, initial * s1 * s2

    def gram_rest(square, h12, dot22, g11, g12, g22):
        h22 = dot22 - h12 * g12
        left = square - h12 * h12 * (2.0 - g11) - h22 * (2.0 * dot22 - h22 * g22)
        return h22, left + 2.0 * h12 * h22 * g12

    def store(table_ref, z1_ref, z2_ref, a1, a2, out_ref):
        out_ref[...] = jnp.zeros_like(out_ref)
        for i in range(slots):
            b = table_ref[i % cap, i // cap]

            @pl.when(b < nblk)
            def _():
                z = a1 * z1_ref[i * blk : (i + 1) * blk, :] + a2 * z2_ref[i * blk : (i + 1) * blk, :]
                out_ref[pl.ds(pl.multiple_of(b * blk, blk), blk), :] = z

    def finish(table_ref, z1_ref, z2_ref, gram_ref, out_ref, res_ref, flag_ref):
        load_square = gram_ref[0:1, :]
        initial = jnp.sqrt(load_square + epsilon)
        rescale = 1.0 / initial
        scale2 = rescale * rescale
        h11 = gram_ref[1:2, :] * scale2
        b11 = gram_ref[2:3, :] * scale2
        c1v = gram_ref[3:4, :] * scale2
        c11 = gram_ref[4:5, :] * scale2
        e11 = gram_ref[5:6, :] * scale2
        g11 = load_square * scale2
        w_square = jnp.maximum(b11 - h11 * h11 * (2.0 - g11), 0.0)
        h21 = jnp.sqrt(w_square + epsilon)
        down = 1.0 / h21
        g22 = w_square * down * down
        g12 = h11 * (epsilon * scale2) * down
        h12 = (c1v - h11 * h11) * down
        dot22 = ((c11 - h11 * c1v) - h11 * (b11 - h11 * h11)) * down * down
        square = ((e11 - h11 * c11) - h11 * (c11 - h11 * b11)) * down * down
        h22, left = gram_rest(square, h12, dot22, g11, g12, g22)
        h32 = jnp.sqrt(jnp.maximum(left, 0.0) + epsilon)
        y1, y2, res = weights(initial, h11, h21, h12, h22, h32)
        a2 = y2 * down * rescale
        res_ref[...] = res
        store(table_ref, z1_ref, z2_ref, y1 * rescale - a2 * h11, a2, out_ref)
        kept = (w_square >= TRUST * b11) & (left * (w_square + epsilon) >= TRUST * e11)
        flag_ref[0] = 1 - jnp.min(kept.astype(F32)).astype(jnp.int32)

    def finish_again(table_ref, z1_ref, z2_ref, one_ref, two_ref, out_ref, res_ref):
        load_square = one_ref[0:1, :]
        initial = jnp.sqrt(load_square + epsilon)
        rescale = 1.0 / initial
        h11 = one_ref[1:2, :] * rescale * rescale
        w_square = two_ref[2:3, :]
        h21 = jnp.sqrt(w_square + epsilon)
        down = 1.0 / h21
        g11 = load_square * rescale * rescale
        g22 = w_square * down * down
        g12 = h11 * (epsilon * rescale * rescale) * down
        h12 = two_ref[3:4, :] * rescale * down
        dot22 = two_ref[4:5, :] * down * down
        square = two_ref[5:6, :] * down * down
        h22, left = gram_rest(square, h12, dot22, g11, g12, g22)
        h32 = jnp.sqrt(jnp.maximum(left, 0.0) + epsilon)
        y1, y2, res = weights(initial, h11, h21, h12, h22, h32)
        res_ref[...] = res
        store(table_ref, z1_ref, z2_ref, y1 * rescale, y2 * down, out_ref)

    results = [((order, cols), F32), ((1, cols), F32)]
    out, res, flag = call(finish, results, (table, z1, z2, sums), flag=True)

    def careful(state):
        r, w1, mcat = (pltpu.with_memory_space_constraint(x, pltpu.HBM) for x in state[3:6])
        sums = state[6]
        zeros = [jnp.zeros(flat, F32)] * 6
        _, z2, more, (z1,) = second_step(zeros, (w1, r, sums), mcat, live_rows(), r, given=True)
        out, res = call(finish_again, results, (table, z1, z2, sums, more))
        return jnp.zeros((1,), jnp.int32), out, res, *state[3:]

    _, out, res, *_ = lax.while_loop(
        lambda state: state[0][0] > 0, careful, (flag, out, res, r, w1, mcat, sums)
    )
    return out.reshape(1, 1, 1, order, cols), res.reshape(cols)


def solution(mesh):
    torus = Mesh(
        mesh.devices.reshape(mesh.shape["gx"], mesh.shape["gy"], 4, 2), ("gx", "gy", "gz_0", "gz_1")
    )
    in_specs = (
        P("gx", "gy", GZ, None, None),
        P("gx", "gy", GZ, None),
        P("gx", "gy", GZ, None, None, None),
        P("gx", "gy", GZ, None, None),
        P("gx", "gy", GZ, None, None),
    )
    out_specs = (P("gx", "gy", GZ, None, None), P())
    return jax.shard_map(
        on_device, mesh=torus, in_specs=in_specs, out_specs=out_specs, check_vma=False
    )
```

time: 94.9 us -> 90.5 us (0.954)
  starting transfers between devices: 28.6 us -> 24.7 us
  Pallas kernels: 23.4 us -> 19.5 us
  waiting for transfers between devices: 13 us -> 15 us
    pallas_call x11 -> x7, Pallas kernels: 23.4 us -> 19.5 us  [call(): pl.pallas_call(body, out_shape=[jax.ShapeDtypeStruct(s, t) for s, t in ou...]
    ppermute x1, starting transfers between devices: 2.99 us -> 0.01 us  [exchange_once(): return lax.ppermute(message, GZ, shifts(GZ)[0])]
    ppermute x6, waiting for transfers between devices: 4.16 us -> 6.05 us  [exchange(): lax.ppermute(to_previous, axis, down)]
    ppermute x2, starting transfers between devices: 4.52 us -> 3.51 us  [exchange_once(): return lax.ppermute(message, (axis, 'gz_1'), pairs)]
  transfers between devices with their start and end apart: 15 -> 15, of which waited for: 6 -> 7; matrix products, arithmetic and copies ran while one was open for 0% -> 0% of each run, Pallas kernels for 8% -> 5%
where the time goes in v4:
time: 90.5 us; the launch traced here: 90.2 us
  blocking collectives  29.3 us (32%)
  starting transfers between devices  24.7 us (27%)
  Pallas kernels  19.5 us (22%)
  waiting for transfers between devices  15 us (17%)
  between operations  0.95 us (1%)
    all_to_all x2, blocking collectives, gather_sum(): wide = lax.all_to_all(wide, axes, 0, 0, tiled=True)  29.3 us
    pallas_call x7, Pallas kernels, call(): pl.pallas_call(body, out_shape=[jax.ShapeDtypeStruct(s, t) for s, t in ou...  19.5 us
    ppermute x6, starting transfers between devices, exchange(): lax.ppermute(to_previous, axis, down)  12.9 us
    ppermute x6, starting transfers between devices, exchange(): lax.ppermute(to_next, axis, up)  8.27 us
    ppermute x6, waiting for transfers between devices, exchange(): lax.ppermute(to_next, axis, up)  6.26 us
    ppermute x6, waiting for transfers between devices, exchange(): lax.ppermute(to_previous, axis, down)  6.05 us
    ppermute x2, starting transfers between devices, exchange_once(): return lax.ppermute(message, (axis, 'gz_1'), pairs)  3.51 us
    ppermute x2, waiting for transfers between devices, exchange_once(): return lax.ppermute(message, (axis, 'gz_1'), pairs)  2.65 us
  transfers between devices with their start and end apart: 15, of which 7 were waited for; matrix products, arithmetic and copies ran while one was open for 0% of the time, Pallas kernels for 5%

profile of v4, /device:TPU:1, one launch (start us, length us, event | category | flops | bytes accessed | tf_op | source)
XLA Modules:
  0.0 90.2 jit_solution(12498635360091109999)
XLA Ops:
  0.6 2.3 %shard_map.68 = (f32[256,384]{1,0:T(8,128)S(1)}, f32[256,384]{1,0:T(8,128)S(1)}, f32[256,384]{1,0:T(8,128)S(1)}, f32[256,384]{1,0:T(8,128)S(1)}, f32[256,384]{1,0:T(8,128)S(1)}, /*index=5*/f32[256,384]{1,0:T(8,128)S(1)}) custom-call(s32[2,6]{1,0:T(2,128)} %bitcast.14, bf16[2048,256]{1,0:T(8,128)(2,1)} %bitcast.12, f32[16,128,128]{2,1,0:T(8,128)} %bitcast.13), custom_call_target="tpu_custom_call" | custom-call | flops 100000000 | bytes 1048576 | tf_op jit(solution)/shard_map/pallas_call | solution.py:35
  3.0 2.6 %collective-permute-start.4 = (f32[256,384]{1,0:T(8,128)S(1)}, f32[256,384]{1,0:T(8,128)S(1)}, u32[]{:S(2)}, u32[]{:S(2)}) collective-permute-start(f32[256,384]{1,0:T(8,128)S(1)} %get-tuple-element.89.refs_0_), channel_id=1, source_target_pairs={{0,32},{32,64},{64,96},{96,128},{128,160},{160,192},{192,224},{224... | collective-permute-start | bytes 1179656 | tf_op jit(solution)/shard_map/ppermute | solution.py:56
  5.5 4.1 %collective-permute-start.3 = (f32[256,384]{1,0:T(8,128)S(1)}, f32[256,384]{1,0:T(8,128)S(1)}, u32[]{:S(2)}, u32[]{:S(2)}) collective-permute-start(f32[256,384]{1,0:T(8,128)S(1)} %get-tuple-element.90.refs_1_), channel_id=1, source_target_pairs={{32,0},{64,32},{96,64},{128,96},{160,128},{192,160},{224,192},{0,2... | collective-permute-start | bytes 1179656 | tf_op jit(solution)/shard_map/ppermute | solution.py:56
  9.7 1.2 %collective-permute-start.6 = (f32[256,384]{1,0:T(8,128)S(1)}, f32[256,384]{1,0:T(8,128)S(1)}, u32[]{:S(2)}, u32[]{:S(2)}) collective-permute-start(f32[256,384]{1,0:T(8,128)S(1)} %get-tuple-element.91.refs_2_), channel_id=1, source_target_pairs={{0,8},{8,16},{16,24},{24,0},{1,9},{9,17},{17,25},{25,1},{2,10},{10... | collective-permute-start | bytes 1179656 | tf_op jit(solution)/shard_map/ppermute | solution.py:56
  10.8 1.7 %collective-permute-start.5 = (f32[256,384]{1,0:T(8,128)S(1)}, f32[256,384]{1,0:T(8,128)S(1)}, u32[]{:S(2)}, u32[]{:S(2)}) collective-permute-start(f32[256,384]{1,0:T(8,128)S(1)} %get-tuple-element.92.refs_3_), channel_id=1, source_target_pairs={{8,0},{16,8},{24,16},{0,24},{9,1},{17,9},{25,17},{1,25},{10,2},{18... | collective-permute-start | bytes 1179656 | tf_op jit(solution)/shard_map/ppermute | solution.py:56
  12.5 2.4 %collective-permute-start.8 = (f32[256,384]{1,0:T(8,128)S(1)}, f32[256,384]{1,0:T(8,128)S(1)}, u32[]{:S(2)}, u32[]{:S(2)}) collective-permute-start(f32[256,384]{1,0:T(8,128)S(1)} %get-tuple-element.93.refs_4_), channel_id=1, source_target_pairs={{0,1},{1,2},{2,3},{3,4},{4,5},{5,6},{6,7},{7,0},{8,9},{9,10},{10,1... | collective-permute-start | bytes 1179656 | tf_op jit(solution)/shard_map/ppermute | solution.py:56
  14.9 3.5 %collective-permute-done.4.refs_7_ = f32[256,384]{1,0:T(8,128)S(1)} collective-permute-done((f32[256,384]{1,0:T(8,128)S(1)}, f32[256,384]{1,0:T(8,128)S(1)}, u32[]{:S(2)}, u32[]{:S(2)}) %collective-permute-start.4) | collective-permute-done | bytes 393248 | tf_op jit(solution)/shard_map/ppermute | solution.py:56
  18.4 1.3 %collective-permute-start.7 = (f32[256,384]{1,0:T(8,128)S(1)}, f32[256,384]{1,0:T(8,128)S(1)}, u32[]{:S(2)}, u32[]{:S(2)}) collective-permute-start(f32[256,384]{1,0:T(8,128)S(1)} %get-tuple-element.94.refs_5_), channel_id=1, source_target_pairs={{1,0},{2,1},{3,2},{4,3},{5,4},{6,5},{7,6},{0,7},{9,8},{10,9},{11,1... | collective-permute-start | bytes 1179656 | tf_op jit(solution)/shard_map/ppermute | solution.py:56
  19.6 3.8 %shard_map.69.refs_13_.refs_14_ = bf16[1536,2048]{1,0:T(8,128)(2,1)S(1)} custom-call(s32[2,6]{1,0:T(2,128)} %bitcast.15, bf16[2048,2048]{1,0:T(8,128)(2,1)} %bitcast.10), custom_call_target="tpu_custom_call" | custom-call | flops 2000000000 | bytes 1048576 | tf_op jit(solution)/shard_map/pallas_call | solution.py:35
  23.5 0.0 collective-permute-done.5.refs_8_
  23.5 2.6 %collective-permute-done.7.refs_10_ = f32[256,384]{1,0:T(8,128)S(1)} collective-permute-done((f32[256,384]{1,0:T(8,128)S(1)}, f32[256,384]{1,0:T(8,128)S(1)}, u32[]{:S(2)}, u32[]{:S(2)}) %collective-permute-start.7) | collective-permute-done | bytes 393248 | tf_op jit(solution)/shard_map/ppermute | solution.py:56
  26.1 5.0 %shard_map.70 = (f32[1536,256]{1,0:T(8,128)S(1)}, f32[1536,256]{1,0:T(8,128)S(1)}, bf16[1536,256]{1,0:T(8,128)(2,1)S(1)}, f32[256,256]{1,0:T(8,128)S(1)}, f32[25...) custom-call(s32[2,6]{1,0:T(2,128)} %bitcast.16, ...), custom_call_target="tpu_custom_call" | custom-call | flops 2000000000 | bytes 1048576 | tf_op jit(solution)/shard_map/pallas_call | solution.py:35
  31.2 0.1 collective-permute-start.10
  31.3 2.7 %collective-permute-start.9 = (f32[256,256]{1,0:T(8,128)S(1)}, f32[256,256]{1,0:T(8,128)S(1)}, u32[]{:S(2)}, u32[]{:S(2)}) collective-permute-start(f32[256,256]{1,0:T(8,128)S(1)} %get-tuple-element.97.refs_1_), channel_id=1, source_target_pairs={{32,0},{64,32},{96,64},{128,96},{160,128},{192,160},{224,192},{0,2... | collective-permute-start | bytes 786440 | tf_op jit(solution)/shard_map/ppermute | solution.py:56
  34.0 1.2 %collective-permute-start.12 = (f32[256,256]{1,0:T(8,128)S(1)}, f32[256,256]{1,0:T(8,128)S(1)}, u32[]{:S(2)}, u32[]{:S(2)}) collective-permute-start(f32[256,256]{1,0:T(8,128)S(1)} %get-tuple-element.98.refs_2_), channel_id=1, source_target_pairs={{0,8},{8,16},{16,24},{24,0},{1,9},{9,17},{17,25},{25,1},{2,10},{10... | collective-permute-start | bytes 786440 | tf_op jit(solution)/shard_map/ppermute | solution.py:56
  35.2 1.5 %collective-permute-start.11 = (f32[256,256]{1,0:T(8,128)S(1)}, f32[256,256]{1,0:T(8,128)S(1)}, u32[]{:S(2)}, u32[]{:S(2)}) collective-permute-start(f32[256,256]{1,0:T(8,128)S(1)} %get-tuple-element.99.refs_3_), channel_id=1, source_target_pairs={{8,0},{16,8},{24,16},{0,24},{9,1},{17,9},{25,17},{1,25},{10,2},{18... | collective-permute-start | bytes 786440 | tf_op jit(solution)/shard_map/ppermute | solution.py:56
  36.8 0.8 collective-permute-start.14
  37.6 2.0 %collective-permute-done.10.refs_7_ = f32[256,256]{1,0:T(8,128)S(1)} collective-permute-done((f32[256,256]{1,0:T(8,128)S(1)}, f32[256,256]{1,0:T(8,128)S(1)}, u32[]{:S(2)}, u32[]{:S(2)}) %collective-permute-start.10) | collective-permute-done | bytes 262176 | tf_op jit(solution)/shard_map/ppermute | solution.py:56
  39.6 1.6 %collective-permute-start.13 = (f32[256,256]{1,0:T(8,128)S(1)}, f32[256,256]{1,0:T(8,128)S(1)}, u32[]{:S(2)}, u32[]{:S(2)}) collective-permute-start(f32[256,256]{1,0:T(8,128)S(1)} %get-tuple-element.101.refs_5_), channel_id=1, source_target_pairs={{1,0},{2,1},{3,2},{4,3},{5,4},{6,5},{7,6},{0,7},{9,8},{10,9},{11,1... | collective-permute-start | bytes 786440 | tf_op jit(solution)/shard_map/ppermute | solution.py:56
  41.2 0.7 collective-permute-done.12.refs_9_
  42.0 3.4 %collective-permute-done.13.refs_10_ = f32[256,256]{1,0:T(8,128)S(1)} collective-permute-done((f32[256,256]{1,0:T(8,128)S(1)}, f32[256,256]{1,0:T(8,128)S(1)}, u32[]{:S(2)}, u32[]{:S(2)}) %collective-permute-start.13) | collective-permute-done | bytes 262176 | tf_op jit(solution)/shard_map/ppermute | solution.py:56
  45.4 5.2 %shard_map.71 = (f32[1536,256]{1,0:T(8,128)S(1)}, f32[1536,256]{1,0:T(8,128)S(1)}, f32[256,256]{1,0:T(8,128)S(1)}, f32[256,256]{1,0:T(8,128)S(1)}, f32[256,256]{...) custom-call(s32[2,6]{1,0:T(2,128)} %bitcast.17, ...), custom_call_target="tpu_custom_call" | custom-call | flops 2000000000 | bytes 1048576 | tf_op jit(solution)/shard_map/pallas_call | solution.py:35
  50.6 0.8 collective-permute-start.15
  51.4 2.7 %collective-permute-start.16 = (f32[256,256]{1,0:T(8,128)S(1)}, f32[256,256]{1,0:T(8,128)S(1)}, u32[]{:S(2)}, u32[]{:S(2)}) collective-permute-start(f32[256,256]{1,0:T(8,128)S(1)} %get-tuple-element.108.refs_7_), channel_id=1, source_target_pairs={{0,8},{1,25},{8,16},{9,1},{16,24},{17,9},{24,0},{25,17},{2,10},{3,... | collective-permute-start | bytes 786440 | tf_op jit(solution)/shard_map/ppermute | solution.py:66
  54.1 0.7 shard_map.72.refs_6_
  54.8 1.3 %collective-permute-done.15.refs_3_ = f32[256,256]{1,0:T(8,128)S(1)} collective-permute-done((f32[256,256]{1,0:T(8,128)S(1)}, f32[256,256]{1,0:T(8,128)S(1)}, u32[]{:S(2)}, u32[]{:S(2)}) %collective-permute-start.15) | collective-permute-done | bytes 262176 | tf_op jit(solution)/shard_map/ppermute | solution.py:66
  56.1 1.4 %collective-permute-done.16.refs_4_ = f32[256,256]{1,0:T(8,128)S(1)} collective-permute-done((f32[256,256]{1,0:T(8,128)S(1)}, f32[256,256]{1,0:T(8,128)S(1)}, u32[]{:S(2)}, u32[]{:S(2)}) %collective-permute-start.16) | collective-permute-done | bytes 262176 | tf_op jit(solution)/shard_map/ppermute | solution.py:66
  57.4 0.1 shard_map.73
  57.6 17.4 %all_to_all.23 = f32[32,8,256]{2,1,0:T(8,128)S(1)} all-to-all(f32[32,8,256]{2,1,0:T(8,128)S(1)} %broadcast_in_dim.8), channel_id=1, replica_groups=mesh['gx'=8,'gy'=4,'gz_0'=4,'gz_1'=2] {'gy','gz_0','gz_1'}, dimensions={0} | all-to-all | bytes 524288 | tf_op jit(solution)/shard_map/all_to_all | solution.py:72
  75.1 11.9 %all_to_all.24 = f32[8,8,256]{2,1,0:T(8,128)S(1)} all-to-all(f32[8,8,256]{2,1,0:T(8,128)S(1)} %broadcast_in_dim.9), channel_id=1, replica_groups=mesh['gx'=8,'gy'=4,'gz_0'=4,'gz_1'=2] {'gx'}, dimensions={0} | all-to-all | bytes 131072 | tf_op jit(solution)/shard_map/all_to_all | solution.py:72
  87.0 2.3 %shard_map.74 = (f32[2048,256]{1,0:T(8,128)}, f32[1,256]{1,0:T(1,128)}, s32[1]{0:T(128)}) custom-call(s32[2,6]{1,0:T(2,128)} %bitcast.18, f32[1536,256]{1,0:T(8,128)S(1)} %get-tuple-element.95.z1_ref, f32[1536,256]{1,0:T(8,128)S(1)} %get-tuple-element.103.z2_ref, f32[8,256]{1,0:T(8,128)S(1)} %reduce_sum.37.gram_ref), custom_call_target="tpu_custom_call" | custom-call | bytes 1048576 | tf_op jit(solution)/shard_map/pallas_call | solution.py:35
  89.3 0.7 while.11
  (20 shorter events, 0.1 us)
Async XLA Ops:
  3.0 15.4 %collective-permute-start.4 = (f32[256,384]{1,0:T(8,128)S(1)}, f32[256,384]{1,0:T(8,128)S(1)}, u32[]{:S(2)}, u32[]{:S(2)}) collective-permute-start(f32[256,384]{1,0:T(8,128)S(1)} %get-tuple-element.89.refs_0_), channel_id=1, source_target_pairs={{0,32},{32,64},{64,96},{96,128},{128,160},{160,192},{192,224},{224... | collective-permute-start | bytes 1179656 | tf_op jit(solution)/shard_map/ppermute | solution.py:56
  5.5 17.9 %collective-permute-start.3 = (f32[256,384]{1,0:T(8,128)S(1)}, f32[256,384]{1,0:T(8,128)S(1)}, u32[]{:S(2)}, u32[]{:S(2)}) collective-permute-start(f32[256,384]{1,0:T(8,128)S(1)} %get-tuple-element.90.refs_1_), channel_id=1, source_target_pairs={{32,0},{64,32},{96,64},{128,96},{160,128},{192,160},{224,192},{0,2... | collective-permute-start | bytes 1179656 | tf_op jit(solution)/shard_map/ppermute | solution.py:56
  9.7 13.8 %collective-permute-start.6 = (f32[256,384]{1,0:T(8,128)S(1)}, f32[256,384]{1,0:T(8,128)S(1)}, u32[]{:S(2)}, u32[]{:S(2)}) collective-permute-start(f32[256,384]{1,0:T(8,128)S(1)} %get-tuple-element.91.refs_2_), channel_id=1, source_target_pairs={{0,8},{8,16},{16,24},{24,0},{1,9},{9,17},{17,25},{25,1},{2,10},{10... | collective-permute-start | bytes 1179656 | tf_op jit(solution)/shard_map/ppermute | solution.py:56
  10.8 12.7 %collective-permute-start.5 = (f32[256,384]{1,0:T(8,128)S(1)}, f32[256,384]{1,0:T(8,128)S(1)}, u32[]{:S(2)}, u32[]{:S(2)}) collective-permute-start(f32[256,384]{1,0:T(8,128)S(1)} %get-tuple-element.92.refs_3_), channel_id=1, source_target_pairs={{8,0},{16,8},{24,16},{0,24},{9,1},{17,9},{25,17},{1,25},{10,2},{18... | collective-permute-start | bytes 1179656 | tf_op jit(solution)/shard_map/ppermute | solution.py:56
  12.5 11.0 %collective-permute-start.8 = (f32[256,384]{1,0:T(8,128)S(1)}, f32[256,384]{1,0:T(8,128)S(1)}, u32[]{:S(2)}, u32[]{:S(2)}) collective-permute-start(f32[256,384]{1,0:T(8,128)S(1)} %get-tuple-element.93.refs_4_), channel_id=1, source_target_pairs={{0,1},{1,2},{2,3},{3,4},{4,5},{5,6},{6,7},{7,0},{8,9},{9,10},{10,1... | collective-permute-start | bytes 1179656 | tf_op jit(solution)/shard_map/ppermute | solution.py:56
  18.4 7.8 %collective-permute-start.7 = (f32[256,384]{1,0:T(8,128)S(1)}, f32[256,384]{1,0:T(8,128)S(1)}, u32[]{:S(2)}, u32[]{:S(2)}) collective-permute-start(f32[256,384]{1,0:T(8,128)S(1)} %get-tuple-element.94.refs_5_), channel_id=1, source_target_pairs={{1,0},{2,1},{3,2},{4,3},{5,4},{6,5},{7,6},{0,7},{9,8},{10,9},{11,1... | collective-permute-start | bytes 1179656 | tf_op jit(solution)/shard_map/ppermute | solution.py:56
  19.6 6.5 %copy-start.3 = (f32[1,1,1,2048]{3,2,1,0:T(1,128)S(1)}, f32[1,1,1,2048]{3,2,1,0:T(1,128)}, u32[]{:S(2)}) copy-start(f32[1,1,1,2048]{3,2,1,0:T(1,128)} %param.8) | copy-start | bytes 24580
  31.2 19.4 %copy-start.2 = (bf16[1536,256]{1,0:T(8,128)(2,1)}, bf16[1536,256]{1,0:T(8,128)(2,1)S(1)}, u32[]{:S(2)}) copy-start(bf16[1536,256]{1,0:T(8,128)(2,1)S(1)} %get-tuple-element.155.refs_12_) | copy-start | bytes 2359300
  31.2 22.9 %copy-start = (f32[1536,256]{1,0:T(8,128)}, f32[1536,256]{1,0:T(8,128)S(1)}, u32[]{:S(2)}) copy-start(f32[1536,256]{1,0:T(8,128)S(1)} %get-tuple-element.153.refs_12_) | copy-start | bytes 4718596
  31.2 8.4 %collective-permute-start.10 = (f32[256,256]{1,0:T(8,128)S(1)}, f32[256,256]{1,0:T(8,128)S(1)}, u32[]{:S(2)}, u32[]{:S(2)}) collective-permute-start(f32[256,256]{1,0:T(8,128)S(1)} %get-tuple-element.96.refs_0_), channel_id=1, source_target_pairs={{0,32},{32,64},{64,96},{96,128},{128,160},{160,192},{192,224},{224... | collective-permute-start | bytes 786440 | tf_op jit(solution)/shard_map/ppermute | solution.py:56
  31.3 9.9 %collective-permute-start.9 = (f32[256,256]{1,0:T(8,128)S(1)}, f32[256,256]{1,0:T(8,128)S(1)}, u32[]{:S(2)}, u32[]{:S(2)}) collective-permute-start(f32[256,256]{1,0:T(8,128)S(1)} %get-tuple-element.97.refs_1_), channel_id=1, source_target_pairs={{32,0},{64,32},{96,64},{128,96},{160,128},{192,160},{224,192},{0,2... | collective-permute-start | bytes 786440 | tf_op jit(solution)/shard_map/ppermute | solution.py:56
  34.0 8.0 %collective-permute-start.12 = (f32[256,256]{1,0:T(8,128)S(1)}, f32[256,256]{1,0:T(8,128)S(1)}, u32[]{:S(2)}, u32[]{:S(2)}) collective-permute-start(f32[256,256]{1,0:T(8,128)S(1)} %get-tuple-element.98.refs_2_), channel_id=1, source_target_pairs={{0,8},{8,16},{16,24},{24,0},{1,9},{9,17},{17,25},{25,1},{2,10},{10... | collective-permute-start | bytes 786440 | tf_op jit(solution)/shard_map/ppermute | solution.py:56
  35.2 6.8 %collective-permute-start.11 = (f32[256,256]{1,0:T(8,128)S(1)}, f32[256,256]{1,0:T(8,128)S(1)}, u32[]{:S(2)}, u32[]{:S(2)}) collective-permute-start(f32[256,256]{1,0:T(8,128)S(1)} %get-tuple-element.99.refs_3_), channel_id=1, source_target_pairs={{8,0},{16,8},{24,16},{0,24},{9,1},{17,9},{25,17},{1,25},{10,2},{18... | collective-permute-start | bytes 786440 | tf_op jit(solution)/shard_map/ppermute | solution.py:56
  36.8 5.2 %collective-permute-start.14 = (f32[256,256]{1,0:T(8,128)S(1)}, f32[256,256]{1,0:T(8,128)S(1)}, u32[]{:S(2)}, u32[]{:S(2)}) collective-permute-start(f32[256,256]{1,0:T(8,128)S(1)} %get-tuple-element.100.refs_4_), channel_id=1, source_target_pairs={{0,1},{1,2},{2,3},{3,4},{4,5},{5,6},{6,7},{7,0},{8,9},{9,10},{10,1... | collective-permute-start | bytes 786440 | tf_op jit(solution)/shard_map/ppermute | solution.py:56
  39.6 5.8 %collective-permute-start.13 = (f32[256,256]{1,0:T(8,128)S(1)}, f32[256,256]{1,0:T(8,128)S(1)}, u32[]{:S(2)}, u32[]{:S(2)}) collective-permute-start(f32[256,256]{1,0:T(8,128)S(1)} %get-tuple-element.101.refs_5_), channel_id=1, source_target_pairs={{1,0},{2,1},{3,2},{4,3},{5,4},{6,5},{7,6},{0,7},{9,8},{10,9},{11,1... | collective-permute-start | bytes 786440 | tf_op jit(solution)/shard_map/ppermute | solution.py:56
  50.6 4.2 %copy-start.1 = (f32[1536,256]{1,0:T(8,128)}, f32[1536,256]{1,0:T(8,128)S(1)}, u32[]{:S(2)}) copy-start(f32[1536,256]{1,0:T(8,128)S(1)} %get-tuple-element.152.refs_13_) | copy-start | bytes 4718596
  50.6 5.5 %collective-permute-start.15 = (f32[256,256]{1,0:T(8,128)S(1)}, f32[256,256]{1,0:T(8,128)S(1)}, u32[]{:S(2)}, u32[]{:S(2)}) collective-permute-start(f32[256,256]{1,0:T(8,128)S(1)} %get-tuple-element.107.refs_6_), channel_id=1, source_target_pairs={{0,32},{1,225},{32,64},{33,1},{64,96},{65,33},{96,128},{97,65},{12... | collective-permute-start | bytes 786440 | tf_op jit(solution)/shard_map/ppermute | solution.py:66
  51.4 6.1 %collective-permute-start.16 = (f32[256,256]{1,0:T(8,128)S(1)}, f32[256,256]{1,0:T(8,128)S(1)}, u32[]{:S(2)}, u32[]{:S(2)}) collective-permute-start(f32[256,256]{1,0:T(8,128)S(1)} %get-tuple-element.108.refs_7_), channel_id=1, source_target_pairs={{0,8},{1,25},{8,16},{9,1},{16,24},{17,9},{24,0},{25,17},{2,10},{3,... | collective-permute-start | bytes 786440 | tf_op jit(solution)/shard_map/ppermute | solution.py:66
  54.1 3.3 %collective-permute-start.17 = (f32[256,256]{1,0:T(8,128)S(1)}, f32[256,256]{1,0:T(8,128)S(1)}, u32[]{:S(2)}, u32[]{:S(2)}) collective-permute-start(f32[256,256]{1,0:T(8,128)S(1)} %get-tuple-element.109.refs_8_), channel_id=1, source_target_pairs={{0,1},{1,2},{2,3},{3,4},{4,5},{5,6},{6,7},{7,0},{8,9},{9,10},{10,1... | collective-permute-start | bytes 786440 | tf_op jit(solution)/shard_map/ppermute | solution.py:61

commit v5 on v4

--- a/solution.py
+++ b/solution.py
@@ -9,7 +9,7 @@
 from jax.sharding import PartitionSpec as P
 
 GZ = ("gz_0", "gz_1")
-GROUP = 2
+STEPS = 4
 AXES = ("gx", "gy", GZ)
 INNER = ("gy", "gz_0", "gz_1")
 
@@ -20,13 +20,14 @@
 BF16 = jnp.bfloat16
 
 
-def call(body, outs, operands, scratch=(), smem=1, raw=(), flops=0, mib=16, flag=False):
+def call(body, outs, operands, scratch=(), smem=1, raw=(), flops=0, mib=16, hbm_table=False):
     specs = []
     operands = list(operands)
     for i in range(len(operands)):
         if i < smem:
             specs.append(pl.BlockSpec(memory_space=pltpu.SMEM))
-            operands[i] = pltpu.with_memory_space_constraint(operands[i], pltpu.HBM)
+            if hbm_table:
+                operands[i] = pltpu.with_memory_space_constraint(operands[i], pltpu.HBM)
         elif i in raw:
             specs.append(pl.BlockSpec(memory_space=pltpu.HBM))
             operands[i] = pltpu.with_memory_space_constraint(operands[i], pltpu.HBM)
@@ -34,11 +35,9 @@
             specs.append(pl.BlockSpec(memory_space=pltpu.VMEM))
     return pl.pallas_call(
         body,
-        out_shape=[jax.ShapeDtypeStruct(s, t) for s, t in outs]
-        + [jax.ShapeDtypeStruct((1,), jnp.int32)] * flag,
+        out_shape=[jax.ShapeDtypeStruct(s, t) for s, t in outs],
         in_specs=specs,
-        out_specs=[pl.BlockSpec(memory_space=pltpu.VMEM) for _ in outs]
-        + [pl.BlockSpec(memory_space=pltpu.SMEM)] * flag,
+        out_specs=[pl.BlockSpec(memory_space=pltpu.VMEM) for _ in outs],
         scratch_shapes=list(scratch),
         compiler_params=pltpu.CompilerParams(vmem_limit_bytes=mib * 2**20),
         cost_estimate=pl.CostEstimate(flops=flops, transcendentals=0, bytes_accessed=2**20),
@@ -150,57 +149,52 @@
             ),
             raw=(1, 2),
             flops=10**8,
+            hbm_table=True,
         )
 
     faces = pack()
     came = [x for a in range(3) for x in exchange(faces[2 * a], faces[2 * a + 1], AXES[a])]
 
-    def fetch(table_ref, matrix_ref, s_ref, sems):
+    def fetch(table_ref, matrix_ref, s_ref, row_buf, sems):
         copies = []
         for i in range(slots):
             b, _ = pick(table_ref, i)
             copy = pltpu.make_async_copy(
                 matrix_ref.at[pl.ds(pl.multiple_of(b * blk, blk), blk), :],
-                s_ref.at[pl.ds(i * blk, blk), :],
+                row_buf.at[pl.ds(i * blk, blk), :],
                 sems.at[i],
             )
             copy.start()
             copies.append(copy)
-        for copy in copies:
-            copy.wait()
-
-    def live_rows():
+        for i in range(slots):
+            copies[i].wait()
+            for j in range(slots):
+                b, _ = pick(table_ref, j)
+                s_ref[i * blk : (i + 1) * blk, j * blk : (j + 1) * blk] = row_buf[
+                    i * blk : (i + 1) * blk, pl.ds(pl.multiple_of(b * blk, blk), blk)
+                ]
+
+    def live_part():
         return call(
             fetch,
-            [((slots * blk, order), BF16)],
+            [((slots * blk, slots * blk), BF16)],
             (table, matrix),
-            scratch=(pltpu.SemaphoreType.DMA((slots,)),),
+            scratch=(pltpu.VMEM((slots * blk, order), BF16), pltpu.SemaphoreType.DMA((slots,))),
             raw=(1,),
             flops=2 * 10**9,
         )[0]
 
-    sel = live_rows()
-
-    def spread(table_ref, zb_ref, i, value):
-        b = table_ref[i % cap, i // cap]
-
-        @pl.when(b < nblk)
-        def _():
-            zb_ref[pl.ds(pl.multiple_of(b * blk, blk), blk), :] = value.astype(BF16)
-
-    def local_schur(table_ref, s_ref, zb_ref, z_ref, diag_ref, outs):
-        for g in range(0, 6, GROUP):
-            product = jnp.dot(
-                s_ref[g * rows : (g + GROUP) * rows, :], zb_ref[...], preferred_element_type=F32
-            )
-            for d in range(g, g + GROUP):
-                for k in range(cap):
-                    i = d * cap + k
-                    b, m = pick(table_ref, i)
-                    dcol = column(diag_ref[pl.ds(b, 1), :], blk)
-                    z = z_ref[i * blk : (i + 1) * blk, :]
-                    at = i * blk - g * rows
-                    outs[d][k * blk : (k + 1) * blk, :] = (product[at : at + blk] + dcol * z) * m
+    sel = live_part()
+
+    def local_schur(table_ref, d, s_ref, zb_ref, z_ref, diag_ref, out_ref):
+        base = d * rows if isinstance(d, int) else pl.multiple_of(d * rows, rows)
+        product = jnp.dot(s_ref[pl.ds(base, rows), :], zb_ref[...], preferred_element_type=F32)
+        for k in range(cap):
+            b = table_ref[k, d]
+            m = (b < nblk).astype(F32)
+            dcol = column(diag_ref[pl.ds(jnp.minimum(b, nblk - 1), 1), :], blk)
+            z = z_ref[pl.ds(base + k * blk, blk), :]
+            out_ref[k * blk : (k + 1) * blk, :] = (product[k * blk : (k + 1) * blk] + dcol * z) * m
 
     long = slots * blk
     tall = (long, cols)
@@ -211,7 +205,6 @@
         diag_ref, s_ref = refs[12:14]
         r_ref, z_ref, m_ref = refs[14:17]
         y_refs, zb_ref = refs[17:23], refs[23]
-        zb_ref[...] = jnp.zeros_like(zb_ref)
         for i in range(slots):
             d, at = i // cap, (i % cap) * blk
             r = own[d][at : at + blk, :cols] + got[d][at : at + blk, :cols]
@@ -222,15 +215,15 @@
             r_ref[i * blk : (i + 1) * blk, :] = r
             z = apply_block(mcat, r)
             z_ref[i * blk : (i + 1) * blk, :] = z
-            spread(table_ref, zb_ref, i, z)
-        local_schur(table_ref, s_ref, zb_ref, z_ref, diag_ref, y_refs)
-
-    spread_z = (pltpu.VMEM((order, cols), BF16),)
+            zb_ref[i * blk : (i + 1) * blk, :] = z.astype(BF16)
+        for d in range(6):
+            local_schur(table_ref, d, s_ref, zb_ref, z_ref, diag_ref, y_refs[d])
+
     r, z1, mcat, *ys = call(
         first,
         [(tall, F32), (tall, F32), ((long, 2 * blk), BF16)] + [(flat, F32)] * 6,
         (table, *faces, *came, diag, sel),
-        scratch=spread_z,
+        scratch=(pltpu.VMEM(tall, BF16),),
         flops=2 * 10**9,
     )
     came = [x for a in range(3) for x in exchange(ys[2 * a], ys[2 * a + 1], AXES[a])]
@@ -251,42 +244,27 @@
             own, got = refs[:6], refs[6:12]
             refs = refs[12:]
         m_ref, diag_ref, s_ref = refs[:3]
-        w_ref, z_ref = refs[3:5]
-        msg_refs, keep_refs = refs[5:8], refs[8:11]
-        refs = refs[11:]
-        if given:
-            first_ref, *refs = refs
-        zb_ref, y_refs = refs[0], refs[1:7]
-        zb_ref[...] = jnp.zeros_like(zb_ref)
+        w_ref, z_ref, zb_ref = refs[3:6]
+        msg_refs = refs[6:9]
         for i in range(slots):
             d, at = i // cap, (i % cap) * blk
             if given:
                 w = raw_ref[i * blk : (i + 1) * blk, :] - h11 * r_ref[i * blk : (i + 1) * blk, :]
                 w = w * scale
                 r = r_ref[i * blk : (i + 1) * blk, :]
-                first_ref[i * blk : (i + 1) * blk, :] = apply_block(m_ref[i * blk : (i + 1) * blk, :], r)
+                refs[9][i * blk : (i + 1) * blk, :] = apply_block(m_ref[i * blk : (i + 1) * blk, :], r)
             else:
                 w = own[d][at : at + blk, :] + got[d][at : at + blk, :]
             w_ref[i * blk : (i + 1) * blk, :] = w
             z = apply_block(m_ref[i * blk : (i + 1) * blk, :], w)
             z_ref[i * blk : (i + 1) * blk, :] = z
-            spread(table_ref, zb_ref, i, z)
-        local_schur(table_ref, s_ref, zb_ref, z_ref, diag_ref, y_refs)
-        low = lax.axis_index("gz_1") == 0
-        for a in range(2):
-
-            @pl.when(low)
-            def _():
-                msg_refs[a][...] = y_refs[2 * a][...]
-                keep_refs[a][...] = y_refs[2 * a + 1][...]
-
-            @pl.when(jnp.logical_not(low))
-            def _():
-                msg_refs[a][...] = y_refs[2 * a + 1][...]
-                keep_refs[a][...] = y_refs[2 * a][...]
-
-        msg_refs[2][...] = y_refs[4][...]
-        keep_refs[2][...] = y_refs[5][...]
+            zb_ref[i * blk : (i + 1) * blk, :] = z.astype(BF16)
+        for a in range(3):
+            local_schur(table_ref, sides(a)[0], s_ref, zb_ref, z_ref, diag_ref, msg_refs[a])
+
+    def rest_of_second(table_ref, zb_ref, z_ref, diag_ref, s_ref, *keep_refs):
+        for a in range(3):
+            local_schur(table_ref, sides(a)[1], s_ref, zb_ref, z_ref, diag_ref, keep_refs[a])
 
     def dots(*refs):
         y_refs, msg_refs, keep_refs = refs[:6], refs[6:9], refs[9:12]
@@ -318,17 +296,19 @@
         out_ref[5:6, :] = square
 
     def second_step(ys, heads, mcat, sel, r, given=False):
-        w, z, *rest = call(
+        w, z, zb, *rest = call(
             functools.partial(second, given=given),
-            [(tall, F32), (tall, F32)] + [(flat, F32)] * 6 + [(tall, F32)] * given,
+            [(tall, F32), (tall, F32), (tall, BF16)] + [(flat, F32)] * 3 + [(tall, F32)] * given,
             (table, *heads, mcat, diag, sel),
-            scratch=spread_z + (pltpu.VMEM(flat, F32),) * 6,
             flops=2 * 10**9,
         )
-        msgs, keeps, z1 = rest[:3], rest[3:6], rest[6:]
+        msgs, z1 = rest[:3], rest[3:]
         got = []
         for a in range(3):
             got.append(exchange_once(msgs[a], AXES[a]))
+        keeps = call(
+            rest_of_second, [(flat, F32)] * 3, (table, zb, z, diag, sel), flops=10**9
+        )
         (sums,) = call(dots, [((8, cols), F32)], (*ys, *msgs, *keeps, r, w), smem=0, flops=10**9)
         (sums,) = call(norms, [((8, cols), F32)], (*keeps, *got, sums), smem=0)
         return w, z, total(sums), z1
@@ -361,7 +341,11 @@
                 z = a1 * z1_ref[i * blk : (i + 1) * blk, :] + a2 * z2_ref[i * blk : (i + 1) * blk, :]
                 out_ref[pl.ds(pl.multiple_of(b * blk, blk), blk), :] = z
 
-    def finish(table_ref, z1_ref, z2_ref, gram_ref, out_ref, res_ref, flag_ref):
+    def finish(table_ref, z1_ref, z2_ref, gram_ref, out_ref, res_ref, flag_ref, slot_ref, buf_ref, sems):
+        for b in range(nblk):
+            slot_ref[b] = jnp.int32(-1)
+        for i in range(slots):
+            slot_ref[table_ref[i % cap, i // cap]] = jnp.int32(i)
         load_square = gram_ref[0:1, :]
         initial = jnp.sqrt(load_square + epsilon)
         rescale = 1.0 / initial
@@ -385,9 +369,22 @@
         y1, y2, res = weights(initial, h11, h21, h12, h22, h32)
         a2 = y2 * down * rescale
         res_ref[...] = res
-        store(table_ref, z1_ref, z2_ref, y1 * rescale - a2 * h11, a2, out_ref)
+        a1 = y1 * rescale - a2 * h11
+        copies = []
+        for g in range(STEPS):
+            for b in range(g * nblk // STEPS, (g + 1) * nblk // STEPS):
+                slot = slot_ref[b]
+                m = (slot >= 0).astype(F32)
+                at = pl.ds(pl.multiple_of(jnp.maximum(slot, 0) * blk, blk), blk)
+                z = (a1 * m) * z1_ref[at, :] + (a2 * m) * z2_ref[at, :]
+                buf_ref[b * blk : (b + 1) * blk, :] = z
+            part = pl.ds(g * (order // STEPS), order // STEPS)
+            copies.append(pltpu.make_async_copy(buf_ref.at[part, :], out_ref.at[part, :], sems.at[g]))
+            copies[-1].start()
         kept = (w_square >= TRUST * b11) & (left * (w_square + epsilon) >= TRUST * e11)
         flag_ref[0] = 1 - jnp.min(kept.astype(F32)).astype(jnp.int32)
+        for copy in copies:
+            copy.wait()
 
     def finish_again(table_ref, z1_ref, z2_ref, one_ref, two_ref, out_ref, res_ref):
         load_square = one_ref[0:1, :]
@@ -410,13 +407,29 @@
         store(table_ref, z1_ref, z2_ref, y1 * rescale, y2 * down, out_ref)
 
     results = [((order, cols), F32), ((1, cols), F32)]
-    out, res, flag = call(finish, results, (table, z1, z2, sums), flag=True)
+    out, res, flag = pl.pallas_call(
+        finish,
+        out_shape=[jax.ShapeDtypeStruct(shape, t) for shape, t in results]
+        + [jax.ShapeDtypeStruct((1,), jnp.int32)],
+        in_specs=[pl.BlockSpec(memory_space=pltpu.SMEM)] + [pl.BlockSpec(memory_space=pltpu.VMEM)] * 3,
+        out_specs=[
+            pl.BlockSpec(memory_space=pltpu.HBM),
+            pl.BlockSpec(memory_space=pltpu.VMEM),
+            pl.BlockSpec(memory_space=pltpu.SMEM),
+        ],
+        scratch_shapes=[
+            pltpu.SMEM((nblk + 1,), jnp.int32),
+            pltpu.VMEM((order, cols), F32),
+            pltpu.SemaphoreType.DMA((STEPS,)),
+        ],
+        compiler_params=pltpu.CompilerParams(vmem_limit_bytes=16 * 2**20),
+    )(table, z1, z2, sums)
 
     def careful(state):
         r, w1, mcat = (pltpu.with_memory_space_constraint(x, pltpu.HBM) for x in state[3:6])
         sums = state[6]
         zeros = [jnp.zeros(flat, F32)] * 6
-        _, z2, more, (z1,) = second_step(zeros, (w1, r, sums), mcat, live_rows(), r, given=True)
+        _, z2, more, (z1,) = second_step(zeros, (w1, r, sums), mcat, live_part(), r, given=True)
         out, res = call(finish_again, results, (table, z1, z2, sums, more))
         return jnp.zeros((1,), jnp.int32), out, res, *state[3:]
 

time: 90.5 us -> 84.8 us (0.937)
  Pallas kernels: 19.5 us -> 15.5 us
  waiting for transfers between devices: 15 us -> 13.6 us
    pallas_call x7, Pallas kernels: 19.5 us -> 12.9 us  [call(): pl.pallas_call(body, out_shape=[jax.ShapeDtypeStruct(s, t) for s, t in ou...]
    pallas_call x0 -> x1, Pallas kernels: none -> 2.63 us  [on_device(): pl.pallas_call(finish, out_shape=[jax.ShapeDtypeStruct(shape, t) for shap...]
    ppermute x2, waiting for transfers between devices: 2.65 us -> 1.28 us  [exchange_once(): return lax.ppermute(message, (axis, 'gz_1'), pairs)]
  transfers between devices with their start and end apart: 15 -> 15, of which waited for: 7 -> 6; matrix products, arithmetic and copies ran while one was open for 0% -> 0% of each run, Pallas kernels for 5% -> 7%
where the time goes in v5:
time: 84.8 us; the launch traced here: 84.6 us
  blocking collectives  29.3 us (35%)
  starting transfers between devices  24.5 us (29%)
  Pallas kernels  15.5 us (18%)
  waiting for transfers between devices  13.6 us (16%)
  between operations  0.98 us (1%)
    all_to_all x2, blocking collectives, gather_sum(): wide = lax.all_to_all(wide, axes, 0, 0, tiled=True)  29.3 us
    ppermute x6, starting transfers between devices, exchange(): lax.ppermute(to_previous, axis, down)  12.9 us
    pallas_call x7, Pallas kernels, call(): pl.pallas_call(body, out_shape=[jax.ShapeDtypeStruct(s, t) for s, t in ou...  12.9 us
    ppermute x6, starting transfers between devices, exchange(): lax.ppermute(to_next, axis, up)  8.27 us
    ppermute x6, waiting for transfers between devices, exchange(): lax.ppermute(to_next, axis, up)  6.26 us
    ppermute x6, waiting for transfers between devices, exchange(): lax.ppermute(to_previous, axis, down)  6.01 us
    ppermute x2, starting transfers between devices, exchange_once(): return lax.ppermute(message, (axis, 'gz_1'), pairs)  3.34 us
    pallas_call x1, Pallas kernels, on_device(): pl.pallas_call(finish, out_shape=[jax.ShapeDtypeStruct(shape, t) for shap...  2.63 us
  transfers between devices with their start and end apart: 15, of which 6 were waited for; matrix products, arithmetic and copies ran while one was open for 0% of the time, Pallas kernels for 7%

profile of v5, /device:TPU:1, one launch (start us, length us, event | category | flops | bytes accessed | tf_op | source)
XLA Modules:
  0.0 84.6 jit_solution(14274910151821724659)
XLA Ops:
  0.6 2.5 %shard_map.68 = (f32[256,384]{1,0:T(8,128)S(1)}, f32[256,384]{1,0:T(8,128)S(1)}, f32[256,384]{1,0:T(8,128)S(1)}, f32[256,384]{1,0:T(8,128)S(1)}, f32[256,384]{1,0:T(8,128)S(1)}, /*index=5*/f32[256,384]{1,0:T(8,128)S(1)}) custom-call(s32[2,6]{1,0:T(2,128)} %bitcast.18, bf16[2048,256]{1,0:T(8,128)(2,1)} %bitcast.16, f32[16,128,128]{2,1,0:T(8,128)} %bitcast.17), custom_call_target="tpu_custom_call" | custom-call | flops 100000000 | bytes 1048576 | tf_op jit(solution)/shard_map/pallas_call | solution.py:36
  3.1 2.6 %collective-permute-start.4 = (f32[256,384]{1,0:T(8,128)S(1)}, f32[256,384]{1,0:T(8,128)S(1)}, u32[]{:S(2)}, u32[]{:S(2)}) collective-permute-start(f32[256,384]{1,0:T(8,128)S(1)} %get-tuple-element.91.refs_0_), channel_id=1, source_target_pairs={{0,32},{32,64},{64,96},{96,128},{128,160},{160,192},{192,224},{224... | collective-permute-start | bytes 1179656 | tf_op jit(solution)/shard_map/ppermute | solution.py:55
  5.7 4.1 %collective-permute-start.3 = (f32[256,384]{1,0:T(8,128)S(1)}, f32[256,384]{1,0:T(8,128)S(1)}, u32[]{:S(2)}, u32[]{:S(2)}) collective-permute-start(f32[256,384]{1,0:T(8,128)S(1)} %get-tuple-element.92.refs_1_), channel_id=1, source_target_pairs={{32,0},{64,32},{96,64},{128,96},{160,128},{192,160},{224,192},{0,2... | collective-permute-start | bytes 1179656 | tf_op jit(solution)/shard_map/ppermute | solution.py:55
  9.8 1.2 %collective-permute-start.6 = (f32[256,384]{1,0:T(8,128)S(1)}, f32[256,384]{1,0:T(8,128)S(1)}, u32[]{:S(2)}, u32[]{:S(2)}) collective-permute-start(f32[256,384]{1,0:T(8,128)S(1)} %get-tuple-element.93.refs_2_), channel_id=1, source_target_pairs={{0,8},{8,16},{16,24},{24,0},{1,9},{9,17},{17,25},{25,1},{2,10},{10... | collective-permute-start | bytes 1179656 | tf_op jit(solution)/shard_map/ppermute | solution.py:55
  11.0 1.7 %collective-permute-start.5 = (f32[256,384]{1,0:T(8,128)S(1)}, f32[256,384]{1,0:T(8,128)S(1)}, u32[]{:S(2)}, u32[]{:S(2)}) collective-permute-start(f32[256,384]{1,0:T(8,128)S(1)} %get-tuple-element.94.refs_3_), channel_id=1, source_target_pairs={{8,0},{16,8},{24,16},{0,24},{9,1},{17,9},{25,17},{1,25},{10,2},{18... | collective-permute-start | bytes 1179656 | tf_op jit(solution)/shard_map/ppermute | solution.py:55
  12.7 2.4 %collective-permute-start.8 = (f32[256,384]{1,0:T(8,128)S(1)}, f32[256,384]{1,0:T(8,128)S(1)}, u32[]{:S(2)}, u32[]{:S(2)}) collective-permute-start(f32[256,384]{1,0:T(8,128)S(1)} %get-tuple-element.95.refs_4_), channel_id=1, source_target_pairs={{0,1},{1,2},{2,3},{3,4},{4,5},{5,6},{6,7},{7,0},{8,9},{9,10},{10,1... | collective-permute-start | bytes 1179656 | tf_op jit(solution)/shard_map/ppermute | solution.py:55
  15.0 3.5 %collective-permute-done.4.refs_7_ = f32[256,384]{1,0:T(8,128)S(1)} collective-permute-done((f32[256,384]{1,0:T(8,128)S(1)}, f32[256,384]{1,0:T(8,128)S(1)}, u32[]{:S(2)}, u32[]{:S(2)}) %collective-permute-start.4) | collective-permute-done | bytes 393248 | tf_op jit(solution)/shard_map/ppermute | solution.py:55
  18.5 1.3 %collective-permute-start.7 = (f32[256,384]{1,0:T(8,128)S(1)}, f32[256,384]{1,0:T(8,128)S(1)}, u32[]{:S(2)}, u32[]{:S(2)}) collective-permute-start(f32[256,384]{1,0:T(8,128)S(1)} %get-tuple-element.96.refs_5_), channel_id=1, source_target_pairs={{1,0},{2,1},{3,2},{4,3},{5,4},{6,5},{7,6},{0,7},{9,8},{10,9},{11,1... | collective-permute-start | bytes 1179656 | tf_op jit(solution)/shard_map/ppermute | solution.py:55
  19.8 3.9 %shard_map.69.refs_13_.refs_14_.s_ref = bf16[1536,1536]{1,0:T(8,128)(2,1)S(1)} custom-call(s32[2,6]{1,0:T(2,128)S(1)} %bitcast.19, bf16[2048,2048]{1,0:T(8,128)(2,1)} %bitcast.10), custom_call_target="tpu_custom_call" | custom-call | flops 2000000000 | bytes 1048576 | tf_op jit(solution)/shard_map/pallas_call | solution.py:36
  23.7 0.0 collective-permute-done.3.refs_6_
  23.7 2.6 %collective-permute-done.7.refs_10_ = f32[256,384]{1,0:T(8,128)S(1)} collective-permute-done((f32[256,384]{1,0:T(8,128)S(1)}, f32[256,384]{1,0:T(8,128)S(1)}, u32[]{:S(2)}, u32[]{:S(2)}) %collective-permute-start.7) | collective-permute-done | bytes 393248 | tf_op jit(solution)/shard_map/ppermute | solution.py:55
  26.3 2.6 %shard_map.70 = (f32[1536,256]{1,0:T(8,128)S(1)}, f32[1536,256]{1,0:T(8,128)S(1)}, bf16[1536,256]{1,0:T(8,128)(2,1)S(1)}, f32[256,256]{1,0:T(8,128)S(1)}, f32[25...) custom-call(s32[2,6]{1,0:T(2,128)S(1)} %bitcast.20, ...), custom_call_target="tpu_custom_call" | custom-call | flops 2000000000 | bytes 1048576 | tf_op jit(solution)/shard_map/pallas_call | solution.py:36
  28.9 0.1 collective-permute-start.10
  29.0 2.7 %collective-permute-start.9 = (f32[256,256]{1,0:T(8,128)S(1)}, f32[256,256]{1,0:T(8,128)S(1)}, u32[]{:S(2)}, u32[]{:S(2)}) collective-permute-start(f32[256,256]{1,0:T(8,128)S(1)} %get-tuple-element.99.refs_1_), channel_id=1, source_target_pairs={{32,0},{64,32},{96,64},{128,96},{160,128},{192,160},{224,192},{0,2... | collective-permute-start | bytes 786440 | tf_op jit(solution)/shard_map/ppermute | solution.py:55
  31.6 1.2 %collective-permute-start.12 = (f32[256,256]{1,0:T(8,128)S(1)}, f32[256,256]{1,0:T(8,128)S(1)}, u32[]{:S(2)}, u32[]{:S(2)}) collective-permute-start(f32[256,256]{1,0:T(8,128)S(1)} %get-tuple-element.100.refs_2_), channel_id=1, source_target_pairs={{0,8},{8,16},{16,24},{24,0},{1,9},{9,17},{17,25},{25,1},{2,10},{10... | collective-permute-start | bytes 786440 | tf_op jit(solution)/shard_map/ppermute | solution.py:55
  32.9 1.5 %collective-permute-start.11 = (f32[256,256]{1,0:T(8,128)S(1)}, f32[256,256]{1,0:T(8,128)S(1)}, u32[]{:S(2)}, u32[]{:S(2)}) collective-permute-start(f32[256,256]{1,0:T(8,128)S(1)} %get-tuple-element.101.refs_3_), channel_id=1, source_target_pairs={{8,0},{16,8},{24,16},{0,24},{9,1},{17,9},{25,17},{1,25},{10,2},{18... | collective-permute-start | bytes 786440 | tf_op jit(solution)/shard_map/ppermute | solution.py:55
  34.4 0.8 collective-permute-start.14
  35.3 2.0 %collective-permute-done.10.refs_7_ = f32[256,256]{1,0:T(8,128)S(1)} collective-permute-done((f32[256,256]{1,0:T(8,128)S(1)}, f32[256,256]{1,0:T(8,128)S(1)}, u32[]{:S(2)}, u32[]{:S(2)}) %collective-permute-start.10) | collective-permute-done | bytes 262176 | tf_op jit(solution)/shard_map/ppermute | solution.py:55
  37.3 1.6 %collective-permute-start.13 = (f32[256,256]{1,0:T(8,128)S(1)}, f32[256,256]{1,0:T(8,128)S(1)}, u32[]{:S(2)}, u32[]{:S(2)}) collective-permute-start(f32[256,256]{1,0:T(8,128)S(1)} %get-tuple-element.103.refs_5_), channel_id=1, source_target_pairs={{1,0},{2,1},{3,2},{4,3},{5,4},{6,5},{7,6},{0,7},{9,8},{10,9},{11,1... | collective-permute-start | bytes 786440 | tf_op jit(solution)/shard_map/ppermute | solution.py:55
  38.9 0.8 collective-permute-done.12.refs_9_
  39.6 3.4 %collective-permute-done.13.refs_10_ = f32[256,256]{1,0:T(8,128)S(1)} collective-permute-done((f32[256,256]{1,0:T(8,128)S(1)}, f32[256,256]{1,0:T(8,128)S(1)}, u32[]{:S(2)}, u32[]{:S(2)}) %collective-permute-start.13) | collective-permute-done | bytes 262176 | tf_op jit(solution)/shard_map/ppermute | solution.py:55
  43.1 1.8 %shard_map.71 = (f32[1536,256]{1,0:T(8,128)S(1)}, f32[1536,256]{1,0:T(8,128)S(1)}, bf16[1536,256]{1,0:T(8,128)(2,1)S(1)}, f32[256,256]{1,0:T(8,128)S(1)}, f32[25...) custom-call(s32[2,6]{1,0:T(2,128)S(1)} %bitcast.21, f32[256,256]{1,0:T(8,128)S(1)} %get-tuple-element.98.refs_0_, ...), custom_call_target="tpu_custom_call" | custom-call | flops 2000000000 | bytes 1048576 | tf_op jit(solution)/shard_map/pallas_call | solution.py:36
  45.0 0.6 collective-permute-start.15
  45.6 2.7 %collective-permute-start.16 = (f32[256,256]{1,0:T(8,128)S(1)}, f32[256,256]{1,0:T(8,128)S(1)}, u32[]{:S(2)}, u32[]{:S(2)}) collective-permute-start(f32[256,256]{1,0:T(8,128)S(1)} %get-tuple-element.111.refs_7_), channel_id=1, source_target_pairs={{0,8},{1,25},{8,16},{9,1},{16,24},{17,9},{24,0},{25,17},{2,10},{3,... | collective-permute-start | bytes 786440 | tf_op jit(solution)/shard_map/ppermute | solution.py:65
  48.3 1.3 %shard_map.72 = (f32[256,256]{1,0:T(8,128)S(1)}, f32[256,256]{1,0:T(8,128)S(1)}, f32[256,256]{1,0:T(8,128)S(1)}) custom-call(s32[2,6]{1,0:T(2,128)S(1)} %bitcast.22, bf16[1536,256]{1,0:T(8,128)(2,1)S(1)} %get-tuple-element.106.zb_ref, f32[1536,256]{1,0:T(8,128)S(1)} %get-tuple-element.105.z_ref.z2_ref, f32[16,128]{1,0:T(8,128)S(1)} %bitcast.14, ...), custom_call_target="tpu_custom_call" | custom-call | flops 1000000000 | bytes 1048576 | tf_op jit(solution)/shard_map/pallas_call | solution.py:36
  49.7 0.7 shard_map.73.refs_6_
  50.3 1.3 %collective-permute-done.16.refs_4_ = f32[256,256]{1,0:T(8,128)S(1)} collective-permute-done((f32[256,256]{1,0:T(8,128)S(1)}, f32[256,256]{1,0:T(8,128)S(1)}, u32[]{:S(2)}, u32[]{:S(2)}) %collective-permute-start.16) | collective-permute-done | bytes 262176 | tf_op jit(solution)/shard_map/ppermute | solution.py:65
  51.6 0.1 shard_map.74
  51.7 17.5 %all_to_all.23 = f32[32,8,256]{2,1,0:T(8,128)S(1)} all-to-all(f32[32,8,256]{2,1,0:T(8,128)S(1)} %broadcast_in_dim.8), channel_id=1, replica_groups=mesh['gx'=8,'gy'=4,'gz_0'=4,'gz_1'=2] {'gy','gz_0','gz_1'}, dimensions={0} | all-to-all | bytes 524288 | tf_op jit(solution)/shard_map/all_to_all | solution.py:71
  69.3 11.8 %all_to_all.24 = f32[8,8,256]{2,1,0:T(8,128)S(1)} all-to-all(f32[8,8,256]{2,1,0:T(8,128)S(1)} %broadcast_in_dim.9), channel_id=1, replica_groups=mesh['gx'=8,'gy'=4,'gz_0'=4,'gz_1'=2] {'gx'}, dimensions={0} | all-to-all | bytes 131072 | tf_op jit(solution)/shard_map/all_to_all | solution.py:71
  81.1 2.6 %shard_map.75 = (f32[2048,256]{1,0:T(8,128)}, f32[1,256]{1,0:T(1,128)}, s32[1]{0:T(128)}) custom-call(s32[2,6]{1,0:T(2,128)S(1)} %bitcast.23, f32[1536,256]{1,0:T(8,128)S(1)} %get-tuple-element.97.z1_ref, f32[1536,256]{1,0:T(8,128)S(1)} %get-tuple-element.105.z_ref.z2_ref, f32[8,256]{1,0:T(8,128)S(1)} %reduce_sum.37.gram_ref), custom_call_target="tpu_custom_call" | custom-call | tf_op jit(solution)/shard_map/pallas_call | solution.py:410
  83.8 0.6 while.11
  (23 shorter events, 0.1 us)
Async XLA Ops:
  0.6 19.2 %copy-start.4 = (s32[1,1,1,6,2]{3,4,2,1,0:T(2,128)S(1)}, s32[1,1,1,6,2]{3,4,2,1,0:T(2,128)}, u32[]{:S(2)}) copy-start(s32[1,1,1,6,2]{3,4,2,1,0:T(2,128)} %param.11) | copy-start | bytes 148
  3.1 15.4 %collective-permute-start.4 = (f32[256,384]{1,0:T(8,128)S(1)}, f32[256,384]{1,0:T(8,128)S(1)}, u32[]{:S(2)}, u32[]{:S(2)}) collective-permute-start(f32[256,384]{1,0:T(8,128)S(1)} %get-tuple-element.91.refs_0_), channel_id=1, source_target_pairs={{0,32},{32,64},{64,96},{96,128},{128,160},{160,192},{192,224},{224... | collective-permute-start | bytes 1179656 | tf_op jit(solution)/shard_map/ppermute | solution.py:55
  5.7 18.0 %collective-permute-start.3 = (f32[256,384]{1,0:T(8,128)S(1)}, f32[256,384]{1,0:T(8,128)S(1)}, u32[]{:S(2)}, u32[]{:S(2)}) collective-permute-start(f32[256,384]{1,0:T(8,128)S(1)} %get-tuple-element.92.refs_1_), channel_id=1, source_target_pairs={{32,0},{64,32},{96,64},{128,96},{160,128},{192,160},{224,192},{0,2... | collective-permute-start | bytes 1179656 | tf_op jit(solution)/shard_map/ppermute | solution.py:55
  9.8 13.9 %collective-permute-start.6 = (f32[256,384]{1,0:T(8,128)S(1)}, f32[256,384]{1,0:T(8,128)S(1)}, u32[]{:S(2)}, u32[]{:S(2)}) collective-permute-start(f32[256,384]{1,0:T(8,128)S(1)} %get-tuple-element.93.refs_2_), channel_id=1, source_target_pairs={{0,8},{8,16},{16,24},{24,0},{1,9},{9,17},{17,25},{25,1},{2,10},{10... | collective-permute-start | bytes 1179656 | tf_op jit(solution)/shard_map/ppermute | solution.py:55
  11.0 12.7 %collective-permute-start.5 = (f32[256,384]{1,0:T(8,128)S(1)}, f32[256,384]{1,0:T(8,128)S(1)}, u32[]{:S(2)}, u32[]{:S(2)}) collective-permute-start(f32[256,384]{1,0:T(8,128)S(1)} %get-tuple-element.94.refs_3_), channel_id=1, source_target_pairs={{8,0},{16,8},{24,16},{0,24},{9,1},{17,9},{25,17},{1,25},{10,2},{18... | collective-permute-start | bytes 1179656 | tf_op jit(solution)/shard_map/ppermute | solution.py:55
  12.7 11.0 %collective-permute-start.8 = (f32[256,384]{1,0:T(8,128)S(1)}, f32[256,384]{1,0:T(8,128)S(1)}, u32[]{:S(2)}, u32[]{:S(2)}) collective-permute-start(f32[256,384]{1,0:T(8,128)S(1)} %get-tuple-element.95.refs_4_), channel_id=1, source_target_pairs={{0,1},{1,2},{2,3},{3,4},{4,5},{5,6},{6,7},{7,0},{8,9},{9,10},{10,1... | collective-permute-start | bytes 1179656 | tf_op jit(solution)/shard_map/ppermute | solution.py:55
  18.5 7.8 %collective-permute-start.7 = (f32[256,384]{1,0:T(8,128)S(1)}, f32[256,384]{1,0:T(8,128)S(1)}, u32[]{:S(2)}, u32[]{:S(2)}) collective-permute-start(f32[256,384]{1,0:T(8,128)S(1)} %get-tuple-element.96.refs_5_), channel_id=1, source_target_pairs={{1,0},{2,1},{3,2},{4,3},{5,4},{6,5},{7,6},{0,7},{9,8},{10,9},{11,1... | collective-permute-start | bytes 1179656 | tf_op jit(solution)/shard_map/ppermute | solution.py:55
  19.8 6.5 %copy-start.3 = (f32[1,1,1,2048]{3,2,1,0:T(1,128)S(1)}, f32[1,1,1,2048]{3,2,1,0:T(1,128)}, u32[]{:S(2)}) copy-start(f32[1,1,1,2048]{3,2,1,0:T(1,128)} %param.8) | copy-start | bytes 24580
  28.9 16.1 %copy-start.2 = (bf16[1536,256]{1,0:T(8,128)(2,1)}, bf16[1536,256]{1,0:T(8,128)(2,1)S(1)}, u32[]{:S(2)}) copy-start(bf16[1536,256]{1,0:T(8,128)(2,1)S(1)} %get-tuple-element.158.refs_12_) | copy-start | bytes 2359300
  28.9 20.8 %copy-start = (f32[1536,256]{1,0:T(8,128)}, f32[1536,256]{1,0:T(8,128)S(1)}, u32[]{:S(2)}) copy-start(f32[1536,256]{1,0:T(8,128)S(1)} %get-tuple-element.156.refs_12_) | copy-start | bytes 4718596
  28.9 8.4 %collective-permute-start.10 = (f32[256,256]{1,0:T(8,128)S(1)}, f32[256,256]{1,0:T(8,128)S(1)}, u32[]{:S(2)}, u32[]{:S(2)}) collective-permute-start(f32[256,256]{1,0:T(8,128)S(1)} %get-tuple-element.98.refs_0_), channel_id=1, source_target_pairs={{0,32},{32,64},{64,96},{96,128},{128,160},{160,192},{192,224},{224... | collective-permute-start | bytes 786440 | tf_op jit(solution)/shard_map/ppermute | solution.py:55
  29.0 9.9 %collective-permute-start.9 = (f32[256,256]{1,0:T(8,128)S(1)}, f32[256,256]{1,0:T(8,128)S(1)}, u32[]{:S(2)}, u32[]{:S(2)}) collective-permute-start(f32[256,256]{1,0:T(8,128)S(1)} %get-tuple-element.99.refs_1_), channel_id=1, source_target_pairs={{32,0},{64,32},{96,64},{128,96},{160,128},{192,160},{224,192},{0,2... | collective-permute-start | bytes 786440 | tf_op jit(solution)/shard_map/ppermute | solution.py:55
  31.6 8.0 %collective-permute-start.12 = (f32[256,256]{1,0:T(8,128)S(1)}, f32[256,256]{1,0:T(8,128)S(1)}, u32[]{:S(2)}, u32[]{:S(2)}) collective-permute-start(f32[256,256]{1,0:T(8,128)S(1)} %get-tuple-element.100.refs_2_), channel_id=1, source_target_pairs={{0,8},{8,16},{16,24},{24,0},{1,9},{9,17},{17,25},{25,1},{2,10},{10... | collective-permute-start | bytes 786440 | tf_op jit(solution)/shard_map/ppermute | solution.py:55
  32.9 6.8 %collective-permute-start.11 = (f32[256,256]{1,0:T(8,128)S(1)}, f32[256,256]{1,0:T(8,128)S(1)}, u32[]{:S(2)}, u32[]{:S(2)}) collective-permute-start(f32[256,256]{1,0:T(8,128)S(1)} %get-tuple-element.101.refs_3_), channel_id=1, source_target_pairs={{8,0},{16,8},{24,16},{0,24},{9,1},{17,9},{25,17},{1,25},{10,2},{18... | collective-permute-start | bytes 786440 | tf_op jit(solution)/shard_map/ppermute | solution.py:55
  34.4 5.2 %collective-permute-start.14 = (f32[256,256]{1,0:T(8,128)S(1)}, f32[256,256]{1,0:T(8,128)S(1)}, u32[]{:S(2)}, u32[]{:S(2)}) collective-permute-start(f32[256,256]{1,0:T(8,128)S(1)} %get-tuple-element.102.refs_4_), channel_id=1, source_target_pairs={{0,1},{1,2},{2,3},{3,4},{4,5},{5,6},{6,7},{7,0},{8,9},{9,10},{10,1... | collective-permute-start | bytes 786440 | tf_op jit(solution)/shard_map/ppermute | solution.py:55
  37.3 5.8 %collective-permute-start.13 = (f32[256,256]{1,0:T(8,128)S(1)}, f32[256,256]{1,0:T(8,128)S(1)}, u32[]{:S(2)}, u32[]{:S(2)}) collective-permute-start(f32[256,256]{1,0:T(8,128)S(1)} %get-tuple-element.103.refs_5_), channel_id=1, source_target_pairs={{1,0},{2,1},{3,2},{4,3},{5,4},{6,5},{7,6},{0,7},{9,8},{10,9},{11,1... | collective-permute-start | bytes 786440 | tf_op jit(solution)/shard_map/ppermute | solution.py:55
  44.9 4.7 %copy-start.1 = (f32[1536,256]{1,0:T(8,128)}, f32[1536,256]{1,0:T(8,128)S(1)}, u32[]{:S(2)}) copy-start(f32[1536,256]{1,0:T(8,128)S(1)} %get-tuple-element.155.refs_13_) | copy-start | bytes 4718596
  45.0 5.4 %collective-permute-start.15 = (f32[256,256]{1,0:T(8,128)S(1)}, f32[256,256]{1,0:T(8,128)S(1)}, u32[]{:S(2)}, u32[]{:S(2)}) collective-permute-start(f32[256,256]{1,0:T(8,128)S(1)} %get-tuple-element.110.refs_6_), channel_id=1, source_target_pairs={{0,32},{1,225},{32,64},{33,1},{64,96},{65,33},{96,128},{97,65},{12... | collective-permute-start | bytes 786440 | tf_op jit(solution)/shard_map/ppermute | solution.py:65
  45.6 6.1 %collective-permute-start.16 = (f32[256,256]{1,0:T(8,128)S(1)}, f32[256,256]{1,0:T(8,128)S(1)}, u32[]{:S(2)}, u32[]{:S(2)}) collective-permute-start(f32[256,256]{1,0:T(8,128)S(1)} %get-tuple-element.111.refs_7_), channel_id=1, source_target_pairs={{0,8},{1,25},{8,16},{9,1},{16,24},{17,9},{24,0},{25,17},{2,10},{3,... | collective-permute-start | bytes 786440 | tf_op jit(solution)/shard_map/ppermute | solution.py:65
  48.3 3.3 %collective-permute-start.17 = (f32[256,256]{1,0:T(8,128)S(1)}, f32[256,256]{1,0:T(8,128)S(1)}, u32[]{:S(2)}, u32[]{:S(2)}) collective-permute-start(f32[256,256]{1,0:T(8,128)S(1)} %get-tuple-element.112.refs_8_), channel_id=1, source_target_pairs={{0,1},{1,2},{2,3},{3,4},{4,5},{5,6},{6,7},{7,0},{8,9},{9,10},{10,1... | collective-permute-start | bytes 786440 | tf_op jit(solution)/shard_map/ppermute | solution.py:60

commit v6 on v5

--- a/solution.py
+++ b/solution.py
@@ -51,6 +51,10 @@
 
 
 def exchange(to_next, to_previous, axis):
+    if axis == GZ:
+        n = lax.axis_size(GZ)
+        across = lax.ppermute(to_previous, GZ, [(i, (i - 1 + 2 * (i % 2)) % n) for i in range(n)])
+        return [lax.ppermute(to_next, GZ, [(i, i ^ 1) for i in range(n)]), across]
     up, down = shifts(axis)
     return [lax.ppermute(to_previous, axis, down), lax.ppermute(to_next, axis, up)]
 
@@ -109,45 +113,32 @@
     matrix = schur.reshape(order, order)
     diag = interface_diag.reshape(nblk, blk)
 
+    def entry(table_ref, k, d):
+        if isinstance(d, int) and d < 4:
+            return table_ref[k, d]
+        kept = (lax.axis_index("gz_1") == 0) | (d < 4)
+        return table_ref[k, jnp.where(kept, d, 9 - d)]
+
     def pick(table_ref, i):
-        b = table_ref[i % cap, i // cap]
+        b = entry(table_ref, i % cap, i // cap)
         return jnp.minimum(b, nblk - 1), (b < nblk).astype(F32)
 
     def pack():
-        def body(table_ref, load_ref, pre_ref, *refs):
-            outs = refs[:6]
-            load_buf, pre_buf, load_sems, pre_sems = refs[6:]
-            copies = []
+        def body(table_ref, load_ref, pre_ref, *outs):
             for i in range(slots):
-                b, _ = pick(table_ref, i)
-                at = pl.multiple_of(b * blk, blk)
-                copies.append(
-                    (
-                        pltpu.make_async_copy(load_ref.at[pl.ds(at, blk), :], load_buf.at[i], load_sems.at[i]),
-                        pltpu.make_async_copy(pre_ref.at[b], pre_buf.at[i], pre_sems.at[i]),
-                    )
-                )
-                for copy in copies[-1]:
-                    copy.start()
-            for i in range(slots):
-                _, m = pick(table_ref, i)
+                b, m = pick(table_ref, i)
                 out, at = outs[i // cap], (i % cap) * blk
-                for copy in copies[i]:
-                    copy.wait()
-                out[at : at + blk, :cols] = load_buf[i].astype(F32) * m
-                out[at : at + blk, cols:] = pre_buf[i] * m
+                out[at : at + blk, :cols] = load_ref[pl.ds(pl.multiple_of(b * blk, blk), blk), :].astype(F32) * m
+                out[at : at + blk, cols:] = pre_ref[b] * m
 
         return call(
             body,
             [((rows, cols + blk), F32)] * 6,
-            (table, load.reshape(order, cols), precond.reshape(nblk, blk, blk)),
-            scratch=(
-                pltpu.VMEM((slots, blk, cols), BF16),
-                pltpu.VMEM((slots, blk, blk), F32),
-                pltpu.SemaphoreType.DMA((slots,)),
-                pltpu.SemaphoreType.DMA((slots,)),
+            (
+                table,
+                pltpu.with_memory_space_constraint(load.reshape(order, cols), pltpu.HBM),
+                pltpu.with_memory_space_constraint(precond.reshape(nblk, blk, blk), pltpu.HBM),
             ),
-            raw=(1, 2),
             flops=10**8,
             hbm_table=True,
         )
@@ -190,7 +181,7 @@
         base = d * rows if isinstance(d, int) else pl.multiple_of(d * rows, rows)
         product = jnp.dot(s_ref[pl.ds(base, rows), :], zb_ref[...], preferred_element_type=F32)
         for k in range(cap):
-            b = table_ref[k, d]
+            b = entry(table_ref, k, d)
             m = (b < nblk).astype(F32)
             dcol = column(diag_ref[pl.ds(jnp.minimum(b, nblk - 1), 1), :], blk)
             z = z_ref[pl.ds(base + k * blk, blk), :]
@@ -229,8 +220,6 @@
     came = [x for a in range(3) for x in exchange(ys[2 * a], ys[2 * a + 1], AXES[a])]
 
     def sides(axis):
-        if axis == 2:
-            return 4, 5
         low = lax.axis_index("gz_1") == 0
         return jnp.where(low, 2 * axis, 2 * axis + 1), jnp.where(low, 2 * axis + 1, 2 * axis)
 
@@ -334,7 +323,7 @@
     def store(table_ref, z1_ref, z2_ref, a1, a2, out_ref):
         out_ref[...] = jnp.zeros_like(out_ref)
         for i in range(slots):
-            b = table_ref[i % cap, i // cap]
+            b = entry(table_ref, i % cap, i // cap)
 
             @pl.when(b < nblk)
             def _():
@@ -345,7 +334,7 @@
         for b in range(nblk):
             slot_ref[b] = jnp.int32(-1)
         for i in range(slots):
-            slot_ref[table_ref[i % cap, i // cap]] = jnp.int32(i)
+            slot_ref[entry(table_ref, i % cap, i // cap)] = jnp.int32(i)
         load_square = gram_ref[0:1, :]
         initial = jnp.sqrt(load_square + epsilon)
         rescale = 1.0 / initial

time: 84.8 us -> 85.5 us (level)
  starting transfers between devices: 24.5 us -> 27.3 us
  waiting for transfers between devices: 13.6 us -> 12.1 us
    ppermute x0 -> x4, starting transfers between devices: none -> 9.37 us  [the longest x2 5.29 us: exchange(): lax.ppermute(to_previous, GZ, [(i, (i - 1 + 2 * (i % 2)) % n) for i in ra...]
    ppermute x0 -> x4, waiting for transfers between devices: none -> 6.22 us  [the longest x2 6.22 us: exchange(): lax.ppermute(to_previous, GZ, [(i, (i - 1 + 2 * (i % 2)) % n) for i in ra...]
    ppermute x6 -> x4, waiting for transfers between devices: 6.01 us -> 0.01 us  [exchange(): lax.ppermute(to_previous, axis, down)]
    ppermute x6 -> x4, starting transfers between devices: 12.9 us -> 9.57 us  [exchange(): lax.ppermute(to_previous, axis, down)]
    ppermute x6 -> x4, starting transfers between devices: 8.27 us -> 5.21 us  [exchange(): lax.ppermute(to_next, axis, up)]
    ppermute x6 -> x4, waiting for transfers between devices: 6.26 us -> 4.54 us  [exchange(): lax.ppermute(to_next, axis, up)]
where the time goes in v6:
time: 85.5 us; the launch traced here: 85.3 us
  blocking collectives  29.5 us (35%)
  starting transfers between devices  27.3 us (32%)
  Pallas kernels  14.7 us (17%)
  waiting for transfers between devices  12.1 us (14%)
  between operations  0.98 us (1%)
    all_to_all x2, blocking collectives, gather_sum(): wide = lax.all_to_all(wide, axes, 0, 0, tiled=True)  29.5 us
    pallas_call x7, Pallas kernels, call(): pl.pallas_call(body, out_shape=[jax.ShapeDtypeStruct(s, t) for s, t in ou...  12 us
    ppermute x4, starting transfers between devices, exchange(): lax.ppermute(to_previous, axis, down)  9.57 us
    ppermute x2, waiting for transfers between devices, exchange(): lax.ppermute(to_previous, GZ, [(i, (i - 1 + 2 * (i % 2)) % n) for i in ra...  6.22 us
    ppermute x2, starting transfers between devices, exchange(): lax.ppermute(to_previous, GZ, [(i, (i - 1 + 2 * (i % 2)) % n) for i in ra...  5.29 us
    ppermute x4, starting transfers between devices, exchange(): lax.ppermute(to_next, axis, up)  5.21 us
    ppermute x4, waiting for transfers between devices, exchange(): lax.ppermute(to_next, axis, up)  4.54 us
    ppermute x2, starting transfers between devices, exchange(): return [lax.ppermute(to_next, GZ, [(i, i ^ 1) for i in range(n)]), across]  4.07 us
  transfers between devices with their start and end apart: 15, of which 6 were waited for; matrix products, arithmetic and copies ran while one was open for 0% of the time, Pallas kernels for 7%

profile of v6, /device:TPU:1, one launch (start us, length us, event | category | flops | bytes accessed | tf_op | source)
XLA Modules:
  0.0 85.3 jit_solution(14067347964932775143)
XLA Ops:
  0.6 1.7 %shard_map.68 = (f32[256,384]{1,0:T(8,128)S(1)}, f32[256,384]{1,0:T(8,128)S(1)}, f32[256,384]{1,0:T(8,128)S(1)}, f32[256,384]{1,0:T(8,128)S(1)}, f32[256,384]{1,0:T(8,128)S(1)}, /*index=5*/f32[256,384]{1,0:T(8,128)S(1)}) custom-call(s32[2,6]{1,0:T(2,128)} %bitcast.18, bf16[2048,256]{1,0:T(8,128)(2,1)} %bitcast.16, f32[16,128,128]{2,1,0:T(8,128)} %bitcast.17), custom_call_target="tpu_custom_call" | custom-call | flops 100000000 | bytes 1048576 | tf_op jit(solution)/shard_map/pallas_call | solution.py:36
  2.4 2.5 %collective-permute-start.4 = (f32[256,384]{1,0:T(8,128)S(1)}, f32[256,384]{1,0:T(8,128)S(1)}, u32[]{:S(2)}, u32[]{:S(2)}) collective-permute-start(f32[256,384]{1,0:T(8,128)S(1)} %get-tuple-element.91.refs_0_), channel_id=1, source_target_pairs={{0,32},{32,64},{64,96},{96,128},{128,160},{160,192},{192,224},{224... | collective-permute-start | bytes 1179656 | tf_op jit(solution)/shard_map/ppermute | solution.py:59
  4.9 4.0 %collective-permute-start.3 = (f32[256,384]{1,0:T(8,128)S(1)}, f32[256,384]{1,0:T(8,128)S(1)}, u32[]{:S(2)}, u32[]{:S(2)}) collective-permute-start(f32[256,384]{1,0:T(8,128)S(1)} %get-tuple-element.92.refs_1_), channel_id=1, source_target_pairs={{32,0},{64,32},{96,64},{128,96},{160,128},{192,160},{224,192},{0,2... | collective-permute-start | bytes 1179656 | tf_op jit(solution)/shard_map/ppermute | solution.py:59
  8.9 1.3 %collective-permute-start.6 = (f32[256,384]{1,0:T(8,128)S(1)}, f32[256,384]{1,0:T(8,128)S(1)}, u32[]{:S(2)}, u32[]{:S(2)}) collective-permute-start(f32[256,384]{1,0:T(8,128)S(1)} %get-tuple-element.93.refs_2_), channel_id=1, source_target_pairs={{0,8},{8,16},{16,24},{24,0},{1,9},{9,17},{17,25},{25,1},{2,10},{10... | collective-permute-start | bytes 1179656 | tf_op jit(solution)/shard_map/ppermute | solution.py:59
  10.2 1.4 %collective-permute-start.5 = (f32[256,384]{1,0:T(8,128)S(1)}, f32[256,384]{1,0:T(8,128)S(1)}, u32[]{:S(2)}, u32[]{:S(2)}) collective-permute-start(f32[256,384]{1,0:T(8,128)S(1)} %get-tuple-element.94.refs_3_), channel_id=1, source_target_pairs={{8,0},{16,8},{24,16},{0,24},{9,1},{17,9},{25,17},{1,25},{10,2},{18... | collective-permute-start | bytes 1179656 | tf_op jit(solution)/shard_map/ppermute | solution.py:59
  11.7 1.5 %collective-permute-start.7 = (f32[256,384]{1,0:T(8,128)S(1)}, f32[256,384]{1,0:T(8,128)S(1)}, u32[]{:S(2)}, u32[]{:S(2)}) collective-permute-start(f32[256,384]{1,0:T(8,128)S(1)} %get-tuple-element.95.refs_4_), channel_id=1, source_target_pairs={{0,1},{1,0},{2,3},{3,2},{4,5},{5,4},{6,7},{7,6},{8,9},{9,8},{10,11... | collective-permute-start | bytes 1179656 | tf_op jit(solution)/shard_map/ppermute | solution.py:57
  13.1 4.5 %collective-permute-done.4.refs_7_ = f32[256,384]{1,0:T(8,128)S(1)} collective-permute-done((f32[256,384]{1,0:T(8,128)S(1)}, f32[256,384]{1,0:T(8,128)S(1)}, u32[]{:S(2)}, u32[]{:S(2)}) %collective-permute-start.4) | collective-permute-done | bytes 393248 | tf_op jit(solution)/shard_map/ppermute | solution.py:59
  17.7 2.3 %collective-permute-start.8 = (f32[256,384]{1,0:T(8,128)S(1)}, f32[256,384]{1,0:T(8,128)S(1)}, u32[]{:S(2)}, u32[]{:S(2)}) collective-permute-start(f32[256,384]{1,0:T(8,128)S(1)} %get-tuple-element.96.refs_5_), channel_id=1, source_target_pairs={{0,7},{1,2},{2,1},{3,4},{4,3},{5,6},{6,5},{7,0},{8,15},{9,10},{10,... | collective-permute-start | bytes 1179656 | tf_op jit(solution)/shard_map/ppermute | solution.py:56
  20.0 3.8 %shard_map.69.refs_13_.refs_14_.s_ref = bf16[1536,1536]{1,0:T(8,128)(2,1)S(1)} custom-call(s32[2,6]{1,0:T(2,128)S(1)} %bitcast.19, bf16[2048,2048]{1,0:T(8,128)(2,1)} %bitcast.10), custom_call_target="tpu_custom_call" | custom-call | flops 2000000000 | bytes 1048576 | tf_op jit(solution)/shard_map/pallas_call | solution.py:36
  23.9 1.9 %collective-permute-done.8.refs_11_ = f32[256,384]{1,0:T(8,128)S(1)} collective-permute-done((f32[256,384]{1,0:T(8,128)S(1)}, f32[256,384]{1,0:T(8,128)S(1)}, u32[]{:S(2)}, u32[]{:S(2)}) %collective-permute-start.8) | collective-permute-done | bytes 393248 | tf_op jit(solution)/shard_map/ppermute | solution.py:56
  25.8 2.6 %shard_map.70 = (f32[1536,256]{1,0:T(8,128)S(1)}, f32[1536,256]{1,0:T(8,128)S(1)}, bf16[1536,256]{1,0:T(8,128)(2,1)S(1)}, f32[256,256]{1,0:T(8,128)S(1)}, f32[25...) custom-call(s32[2,6]{1,0:T(2,128)S(1)} %bitcast.20, ...), custom_call_target="tpu_custom_call" | custom-call | flops 2000000000 | bytes 1048576 | tf_op jit(solution)/shard_map/pallas_call | solution.py:36
  28.4 0.1 collective-permute-start.10
  28.5 2.7 %collective-permute-start.9 = (f32[256,256]{1,0:T(8,128)S(1)}, f32[256,256]{1,0:T(8,128)S(1)}, u32[]{:S(2)}, u32[]{:S(2)}) collective-permute-start(f32[256,256]{1,0:T(8,128)S(1)} %get-tuple-element.99.refs_1_), channel_id=1, source_target_pairs={{32,0},{64,32},{96,64},{128,96},{160,128},{192,160},{224,192},{0,2... | collective-permute-start | bytes 786440 | tf_op jit(solution)/shard_map/ppermute | solution.py:59
  31.1 1.3 %collective-permute-start.12 = (f32[256,256]{1,0:T(8,128)S(1)}, f32[256,256]{1,0:T(8,128)S(1)}, u32[]{:S(2)}, u32[]{:S(2)}) collective-permute-start(f32[256,256]{1,0:T(8,128)S(1)} %get-tuple-element.100.refs_2_), channel_id=1, source_target_pairs={{0,8},{8,16},{16,24},{24,0},{1,9},{9,17},{17,25},{25,1},{2,10},{10... | collective-permute-start | bytes 786440 | tf_op jit(solution)/shard_map/ppermute | solution.py:59
  32.4 1.4 %collective-permute-start.11 = (f32[256,256]{1,0:T(8,128)S(1)}, f32[256,256]{1,0:T(8,128)S(1)}, u32[]{:S(2)}, u32[]{:S(2)}) collective-permute-start(f32[256,256]{1,0:T(8,128)S(1)} %get-tuple-element.101.refs_3_), channel_id=1, source_target_pairs={{8,0},{16,8},{24,16},{0,24},{9,1},{17,9},{25,17},{1,25},{10,2},{18... | collective-permute-start | bytes 786440 | tf_op jit(solution)/shard_map/ppermute | solution.py:59
  33.9 2.6 %collective-permute-start.13 = (f32[256,256]{1,0:T(8,128)S(1)}, f32[256,256]{1,0:T(8,128)S(1)}, u32[]{:S(2)}, u32[]{:S(2)}) collective-permute-start(f32[256,256]{1,0:T(8,128)S(1)} %get-tuple-element.102.refs_4_), channel_id=1, source_target_pairs={{0,1},{1,0},{2,3},{3,2},{4,5},{5,4},{6,7},{7,6},{8,9},{9,8},{10,11... | collective-permute-start | bytes 786440 | tf_op jit(solution)/shard_map/ppermute | solution.py:57
  36.5 2.9 %collective-permute-start.14 = (f32[256,256]{1,0:T(8,128)S(1)}, f32[256,256]{1,0:T(8,128)S(1)}, u32[]{:S(2)}, u32[]{:S(2)}) collective-permute-start(f32[256,256]{1,0:T(8,128)S(1)} %get-tuple-element.103.refs_5_), channel_id=1, source_target_pairs={{0,7},{1,2},{2,1},{3,4},{4,3},{5,6},{6,5},{7,0},{8,15},{9,10},{10,... | collective-permute-start | bytes 786440 | tf_op jit(solution)/shard_map/ppermute | solution.py:56
  39.5 4.3 %collective-permute-done.14.refs_11_ = f32[256,256]{1,0:T(8,128)S(1)} collective-permute-done((f32[256,256]{1,0:T(8,128)S(1)}, f32[256,256]{1,0:T(8,128)S(1)}, u32[]{:S(2)}, u32[]{:S(2)}) %collective-permute-start.14) | collective-permute-done | bytes 262176 | tf_op jit(solution)/shard_map/ppermute | solution.py:56
  43.8 1.8 %shard_map.71 = (f32[1536,256]{1,0:T(8,128)S(1)}, f32[1536,256]{1,0:T(8,128)S(1)}, bf16[1536,256]{1,0:T(8,128)(2,1)S(1)}, f32[256,256]{1,0:T(8,128)S(1)}, f32[25...) custom-call(s32[2,6]{1,0:T(2,128)S(1)} %bitcast.21, f32[256,256]{1,0:T(8,128)S(1)} %get-tuple-element.98.refs_0_, ...), custom_call_target="tpu_custom_call" | custom-call | flops 2000000000 | bytes 1048576 | tf_op jit(solution)/shard_map/pallas_call | solution.py:36
  45.6 0.3 collective-permute-start.15
  46.0 2.7 %collective-permute-start.16 = (f32[256,256]{1,0:T(8,128)S(1)}, f32[256,256]{1,0:T(8,128)S(1)}, u32[]{:S(2)}, u32[]{:S(2)}) collective-permute-start(f32[256,256]{1,0:T(8,128)S(1)} %get-tuple-element.111.refs_7_), channel_id=1, source_target_pairs={{0,8},{1,25},{8,16},{9,1},{16,24},{17,9},{24,0},{25,17},{2,10},{3,... | collective-permute-start | bytes 786440 | tf_op jit(solution)/shard_map/ppermute | solution.py:69
  48.7 0.1 collective-permute-start.17
  48.8 1.3 %shard_map.72 = (f32[256,256]{1,0:T(8,128)S(1)}, f32[256,256]{1,0:T(8,128)S(1)}, f32[256,256]{1,0:T(8,128)S(1)}) custom-call(s32[2,6]{1,0:T(2,128)S(1)} %bitcast.22, bf16[1536,256]{1,0:T(8,128)(2,1)S(1)} %get-tuple-element.106.zb_ref, f32[1536,256]{1,0:T(8,128)S(1)} %get-tuple-element.105.z_ref.z2_ref, f32[16,128]{1,0:T(8,128)S(1)} %bitcast.14, ...), custom_call_target="tpu_custom_call" | custom-call | flops 1000000000 | bytes 1048576 | tf_op jit(solution)/shard_map/pallas_call | solution.py:36
  50.2 0.7 shard_map.73.refs_6_
  50.9 0.1 collective-permute-done.15.refs_3_
  50.9 1.1 %collective-permute-done.16.refs_4_ = f32[256,256]{1,0:T(8,128)S(1)} collective-permute-done((f32[256,256]{1,0:T(8,128)S(1)}, f32[256,256]{1,0:T(8,128)S(1)}, u32[]{:S(2)}, u32[]{:S(2)}) %collective-permute-start.16) | collective-permute-done | bytes 262176 | tf_op jit(solution)/shard_map/ppermute | solution.py:69
  52.0 0.1 collective-permute-done.17.refs_5_
  52.1 0.1 shard_map.74
  52.3 17.4 %all_to_all.23 = f32[32,8,256]{2,1,0:T(8,128)S(1)} all-to-all(f32[32,8,256]{2,1,0:T(8,128)S(1)} %broadcast_in_dim.8), channel_id=1, replica_groups=mesh['gx'=8,'gy'=4,'gz_0'=4,'gz_1'=2] {'gy','gz_0','gz_1'}, dimensions={0} | all-to-all | bytes 524288 | tf_op jit(solution)/shard_map/all_to_all | solution.py:75
  69.7 12.2 %all_to_all.24 = f32[8,8,256]{2,1,0:T(8,128)S(1)} all-to-all(f32[8,8,256]{2,1,0:T(8,128)S(1)} %broadcast_in_dim.9), channel_id=1, replica_groups=mesh['gx'=8,'gy'=4,'gz_0'=4,'gz_1'=2] {'gx'}, dimensions={0} | all-to-all | bytes 131072 | tf_op jit(solution)/shard_map/all_to_all | solution.py:75
  81.9 2.6 %shard_map.75 = (f32[2048,256]{1,0:T(8,128)}, f32[1,256]{1,0:T(1,128)}, s32[1]{0:T(128)}) custom-call(s32[2,6]{1,0:T(2,128)S(1)} %bitcast.23, f32[1536,256]{1,0:T(8,128)S(1)} %get-tuple-element.97.z1_ref, f32[1536,256]{1,0:T(8,128)S(1)} %get-tuple-element.105.z_ref.z2_ref, f32[8,256]{1,0:T(8,128)S(1)} %reduce_sum.37.gram_ref), custom_call_target="tpu_custom_call" | custom-call | tf_op jit(solution)/shard_map/pallas_call | solution.py:399
  84.5 0.6 while.11
  (23 shorter events, 0.1 us)
Async XLA Ops:
  0.6 19.4 %copy-start.4 = (s32[1,1,1,6,2]{3,4,2,1,0:T(2,128)S(1)}, s32[1,1,1,6,2]{3,4,2,1,0:T(2,128)}, u32[]{:S(2)}) copy-start(s32[1,1,1,6,2]{3,4,2,1,0:T(2,128)} %param.11) | copy-start | bytes 148
  2.4 15.3 %collective-permute-start.4 = (f32[256,384]{1,0:T(8,128)S(1)}, f32[256,384]{1,0:T(8,128)S(1)}, u32[]{:S(2)}, u32[]{:S(2)}) collective-permute-start(f32[256,384]{1,0:T(8,128)S(1)} %get-tuple-element.91.refs_0_), channel_id=1, source_target_pairs={{0,32},{32,64},{64,96},{96,128},{128,160},{160,192},{192,224},{224... | collective-permute-start | bytes 1179656 | tf_op jit(solution)/shard_map/ppermute | solution.py:59
  4.9 18.9 %collective-permute-start.3 = (f32[256,384]{1,0:T(8,128)S(1)}, f32[256,384]{1,0:T(8,128)S(1)}, u32[]{:S(2)}, u32[]{:S(2)}) collective-permute-start(f32[256,384]{1,0:T(8,128)S(1)} %get-tuple-element.92.refs_1_), channel_id=1, source_target_pairs={{32,0},{64,32},{96,64},{128,96},{160,128},{192,160},{224,192},{0,2... | collective-permute-start | bytes 1179656 | tf_op jit(solution)/shard_map/ppermute | solution.py:59
  8.9 14.9 %collective-permute-start.6 = (f32[256,384]{1,0:T(8,128)S(1)}, f32[256,384]{1,0:T(8,128)S(1)}, u32[]{:S(2)}, u32[]{:S(2)}) collective-permute-start(f32[256,384]{1,0:T(8,128)S(1)} %get-tuple-element.93.refs_2_), channel_id=1, source_target_pairs={{0,8},{8,16},{16,24},{24,0},{1,9},{9,17},{17,25},{25,1},{2,10},{10... | collective-permute-start | bytes 1179656 | tf_op jit(solution)/shard_map/ppermute | solution.py:59
  10.2 13.6 %collective-permute-start.5 = (f32[256,384]{1,0:T(8,128)S(1)}, f32[256,384]{1,0:T(8,128)S(1)}, u32[]{:S(2)}, u32[]{:S(2)}) collective-permute-start(f32[256,384]{1,0:T(8,128)S(1)} %get-tuple-element.94.refs_3_), channel_id=1, source_target_pairs={{8,0},{16,8},{24,16},{0,24},{9,1},{17,9},{25,17},{1,25},{10,2},{18... | collective-permute-start | bytes 1179656 | tf_op jit(solution)/shard_map/ppermute | solution.py:59
  11.7 12.2 %collective-permute-start.7 = (f32[256,384]{1,0:T(8,128)S(1)}, f32[256,384]{1,0:T(8,128)S(1)}, u32[]{:S(2)}, u32[]{:S(2)}) collective-permute-start(f32[256,384]{1,0:T(8,128)S(1)} %get-tuple-element.95.refs_4_), channel_id=1, source_target_pairs={{0,1},{1,0},{2,3},{3,2},{4,5},{5,4},{6,7},{7,6},{8,9},{9,8},{10,11... | collective-permute-start | bytes 1179656 | tf_op jit(solution)/shard_map/ppermute | solution.py:57
  17.7 8.1 %collective-permute-start.8 = (f32[256,384]{1,0:T(8,128)S(1)}, f32[256,384]{1,0:T(8,128)S(1)}, u32[]{:S(2)}, u32[]{:S(2)}) collective-permute-start(f32[256,384]{1,0:T(8,128)S(1)} %get-tuple-element.96.refs_5_), channel_id=1, source_target_pairs={{0,7},{1,2},{2,1},{3,4},{4,3},{5,6},{6,5},{7,0},{8,15},{9,10},{10,... | collective-permute-start | bytes 1179656 | tf_op jit(solution)/shard_map/ppermute | solution.py:56
  20.0 5.8 %copy-start.3 = (f32[1,1,1,2048]{3,2,1,0:T(1,128)S(1)}, f32[1,1,1,2048]{3,2,1,0:T(1,128)}, u32[]{:S(2)}) copy-start(f32[1,1,1,2048]{3,2,1,0:T(1,128)} %param.8) | copy-start | bytes 24580
  28.3 17.3 %copy-start.2 = (bf16[1536,256]{1,0:T(8,128)(2,1)}, bf16[1536,256]{1,0:T(8,128)(2,1)S(1)}, u32[]{:S(2)}) copy-start(bf16[1536,256]{1,0:T(8,128)(2,1)S(1)} %get-tuple-element.158.refs_12_) | copy-start | bytes 2359300
  28.4 21.8 %copy-start = (f32[1536,256]{1,0:T(8,128)}, f32[1536,256]{1,0:T(8,128)S(1)}, u32[]{:S(2)}) copy-start(f32[1536,256]{1,0:T(8,128)S(1)} %get-tuple-element.156.refs_12_) | copy-start | bytes 4718596
  28.4 8.1 %collective-permute-start.10 = (f32[256,256]{1,0:T(8,128)S(1)}, f32[256,256]{1,0:T(8,128)S(1)}, u32[]{:S(2)}, u32[]{:S(2)}) collective-permute-start(f32[256,256]{1,0:T(8,128)S(1)} %get-tuple-element.98.refs_0_), channel_id=1, source_target_pairs={{0,32},{32,64},{64,96},{96,128},{128,160},{160,192},{192,224},{224... | collective-permute-start | bytes 786440 | tf_op jit(solution)/shard_map/ppermute | solution.py:59
  28.5 11.0 %collective-permute-start.9 = (f32[256,256]{1,0:T(8,128)S(1)}, f32[256,256]{1,0:T(8,128)S(1)}, u32[]{:S(2)}, u32[]{:S(2)}) collective-permute-start(f32[256,256]{1,0:T(8,128)S(1)} %get-tuple-element.99.refs_1_), channel_id=1, source_target_pairs={{32,0},{64,32},{96,64},{128,96},{160,128},{192,160},{224,192},{0,2... | collective-permute-start | bytes 786440 | tf_op jit(solution)/shard_map/ppermute | solution.py:59
  31.1 8.3 %collective-permute-start.12 = (f32[256,256]{1,0:T(8,128)S(1)}, f32[256,256]{1,0:T(8,128)S(1)}, u32[]{:S(2)}, u32[]{:S(2)}) collective-permute-start(f32[256,256]{1,0:T(8,128)S(1)} %get-tuple-element.100.refs_2_), channel_id=1, source_target_pairs={{0,8},{8,16},{16,24},{24,0},{1,9},{9,17},{17,25},{25,1},{2,10},{10... | collective-permute-start | bytes 786440 | tf_op jit(solution)/shard_map/ppermute | solution.py:59
  32.4 7.0 %collective-permute-start.11 = (f32[256,256]{1,0:T(8,128)S(1)}, f32[256,256]{1,0:T(8,128)S(1)}, u32[]{:S(2)}, u32[]{:S(2)}) collective-permute-start(f32[256,256]{1,0:T(8,128)S(1)} %get-tuple-element.101.refs_3_), channel_id=1, source_target_pairs={{8,0},{16,8},{24,16},{0,24},{9,1},{17,9},{25,17},{1,25},{10,2},{18... | collective-permute-start | bytes 786440 | tf_op jit(solution)/shard_map/ppermute | solution.py:59
  33.9 5.6 %collective-permute-start.13 = (f32[256,256]{1,0:T(8,128)S(1)}, f32[256,256]{1,0:T(8,128)S(1)}, u32[]{:S(2)}, u32[]{:S(2)}) collective-permute-start(f32[256,256]{1,0:T(8,128)S(1)} %get-tuple-element.102.refs_4_), channel_id=1, source_target_pairs={{0,1},{1,0},{2,3},{3,2},{4,5},{5,4},{6,7},{7,6},{8,9},{9,8},{10,11... | collective-permute-start | bytes 786440 | tf_op jit(solution)/shard_map/ppermute | solution.py:57
  36.5 7.3 %collective-permute-start.14 = (f32[256,256]{1,0:T(8,128)S(1)}, f32[256,256]{1,0:T(8,128)S(1)}, u32[]{:S(2)}, u32[]{:S(2)}) collective-permute-start(f32[256,256]{1,0:T(8,128)S(1)} %get-tuple-element.103.refs_5_), channel_id=1, source_target_pairs={{0,7},{1,2},{2,1},{3,4},{4,3},{5,6},{6,5},{7,0},{8,15},{9,10},{10,... | collective-permute-start | bytes 786440 | tf_op jit(solution)/shard_map/ppermute | solution.py:56
  45.6 4.5 %copy-start.1 = (f32[1536,256]{1,0:T(8,128)}, f32[1536,256]{1,0:T(8,128)S(1)}, u32[]{:S(2)}) copy-start(f32[1536,256]{1,0:T(8,128)S(1)} %get-tuple-element.155.refs_13_) | copy-start | bytes 4718596
  45.6 5.3 %collective-permute-start.15 = (f32[256,256]{1,0:T(8,128)S(1)}, f32[256,256]{1,0:T(8,128)S(1)}, u32[]{:S(2)}, u32[]{:S(2)}) collective-permute-start(f32[256,256]{1,0:T(8,128)S(1)} %get-tuple-element.110.refs_6_), channel_id=1, source_target_pairs={{0,32},{1,225},{32,64},{33,1},{64,96},{65,33},{96,128},{97,65},{12... | collective-permute-start | bytes 786440 | tf_op jit(solution)/shard_map/ppermute | solution.py:69
  46.0 6.1 %collective-permute-start.16 = (f32[256,256]{1,0:T(8,128)S(1)}, f32[256,256]{1,0:T(8,128)S(1)}, u32[]{:S(2)}, u32[]{:S(2)}) collective-permute-start(f32[256,256]{1,0:T(8,128)S(1)} %get-tuple-element.111.refs_7_), channel_id=1, source_target_pairs={{0,8},{1,25},{8,16},{9,1},{16,24},{17,9},{24,0},{25,17},{2,10},{3,... | collective-permute-start | bytes 786440 | tf_op jit(solution)/shard_map/ppermute | solution.py:69
  48.7 3.5 %collective-permute-start.17 = (f32[256,256]{1,0:T(8,128)S(1)}, f32[256,256]{1,0:T(8,128)S(1)}, u32[]{:S(2)}, u32[]{:S(2)}) collective-permute-start(f32[256,256]{1,0:T(8,128)S(1)} %get-tuple-element.112.refs_8_), channel_id=1, source_target_pairs={{0,1},{1,2},{2,3},{3,4},{4,5},{5,6},{6,7},{7,0},{8,9},{9,10},{10,1... | collective-permute-start | bytes 786440 | tf_op jit(solution)/shard_map/ppermute | solution.py:64

commit v7 on v6

--- a/solution.py
+++ b/solution.py
@@ -50,13 +50,16 @@
     return up, [(j, i) for i, j in up]
 
 
-def exchange(to_next, to_previous, axis):
-    if axis == GZ:
-        n = lax.axis_size(GZ)
-        across = lax.ppermute(to_previous, GZ, [(i, (i - 1 + 2 * (i % 2)) % n) for i in range(n)])
-        return [lax.ppermute(to_next, GZ, [(i, i ^ 1) for i in range(n)]), across]
-    up, down = shifts(axis)
-    return [lax.ppermute(to_previous, axis, down), lax.ppermute(to_next, axis, up)]
+def exchange(first, second, axis):
+    n = lax.axis_size(axis)
+    return [
+        lax.ppermute(first, axis, [(i, i ^ 1) for i in range(n)]),
+        lax.ppermute(second, axis, [(i, (i - 1 + 2 * (i % 2)) % n) for i in range(n)]),
+    ]
+
+
+def even(axis):
+    return lax.axis_index(("gx", "gy", "gz_1")[axis]) % 2 == 0
 
 
 def exchange_once(message, axis):
@@ -114,10 +117,11 @@
     diag = interface_diag.reshape(nblk, blk)
 
     def entry(table_ref, k, d):
-        if isinstance(d, int) and d < 4:
-            return table_ref[k, d]
-        kept = (lax.axis_index("gz_1") == 0) | (d < 4)
-        return table_ref[k, jnp.where(kept, d, 9 - d)]
+        if isinstance(d, int):
+            return table_ref[k, jnp.where(even(d // 2), d, d ^ 1)]
+        flips = [jnp.where(even(a), 0, 1) for a in range(3)]
+        flip = jnp.where(d < 2, flips[0], jnp.where(d < 4, flips[1], flips[2]))
+        return table_ref[k, d + flip * (1 - 2 * (d % 2))]
 
     def pick(table_ref, i):
         b = entry(table_ref, i % cap, i // cap)
@@ -220,8 +224,9 @@
     came = [x for a in range(3) for x in exchange(ys[2 * a], ys[2 * a + 1], AXES[a])]
 
     def sides(axis):
-        low = lax.axis_index("gz_1") == 0
-        return jnp.where(low, 2 * axis, 2 * axis + 1), jnp.where(low, 2 * axis + 1, 2 * axis)
+        up = lax.axis_index("gz_1") == 0
+        partner = even(axis) == up if axis < 2 else up
+        return jnp.where(partner, 2 * axis, 2 * axis + 1), jnp.where(partner, 2 * axis + 1, 2 * axis)
 
     def second(table_ref, *refs, given=False):
         if given:

time: 85.5 us -> 83.6 us (0.978)
  waiting for transfers between devices: 12.1 us -> 9.5 us
  starting transfers between devices: 27.3 us -> 29.8 us
  blocking collectives: 29.5 us -> 27.7 us
    ppermute x12, waiting for transfers between devices: 10.8 us -> 8.22 us  [the longest x6 8.2 us: exchange(): lax.ppermute(second, axis, [(i, (i - 1 + 2 * (i % 2)) % n) for i in range...]
    all_to_all x2, blocking collectives: 29.5 us -> 27.7 us  [gather_sum(): wide = lax.all_to_all(wide, axes, 0, 0, tiled=True)]
    ppermute x12, starting transfers between devices: 24.1 us -> 25.6 us  [the longest x6 14.6 us: exchange(): lax.ppermute(second, axis, [(i, (i - 1 + 2 * (i % 2)) % n) for i in range...]
    ppermute x2, starting transfers between devices: 3.06 us -> 4.23 us  [exchange_once(): return lax.ppermute(message, (axis, 'gz_1'), pairs)]
  transfers between devices with their start and end apart: 15 -> 15, of which waited for: 6 -> 5; matrix products, arithmetic and copies ran while one was open for 0% -> 0% of each run, Pallas kernels for 7% -> 7%
where the time goes in v7:
time: 83.6 us; the launch traced here: 83.4 us
  starting transfers between devices  29.8 us (36%)
  blocking collectives  27.7 us (33%)
  Pallas kernels  14.7 us (18%)
  waiting for transfers between devices  9.5 us (11%)
  between operations  0.97 us (1%)
    all_to_all x2, blocking collectives, gather_sum(): wide = lax.all_to_all(wide, axes, 0, 0, tiled=True)  27.7 us
    ppermute x6, starting transfers between devices, exchange(): lax.ppermute(second, axis, [(i, (i - 1 + 2 * (i % 2)) % n) for i in range...  14.6 us
    pallas_call x7, Pallas kernels, call(): pl.pallas_call(body, out_shape=[jax.ShapeDtypeStruct(s, t) for s, t in ou...  12.1 us
    ppermute x6, starting transfers between devices, exchange(): lax.ppermute(first, axis, [(i, i ^ 1) for i in range(n)])  10.9 us
    ppermute x6, waiting for transfers between devices, exchange(): lax.ppermute(second, axis, [(i, (i - 1 + 2 * (i % 2)) % n) for i in range...  8.2 us
    ppermute x2, starting transfers between devices, exchange_once(): return lax.ppermute(message, (axis, 'gz_1'), pairs)  4.23 us
    pallas_call x1, Pallas kernels, on_device(): pl.pallas_call(finish, out_shape=[jax.ShapeDtypeStruct(shape, t) for shap...  2.65 us
  transfers between devices with their start and end apart: 15, of which 5 were waited for; matrix products, arithmetic and copies ran while one was open for 0% of the time, Pallas kernels for 7%

profile of v7, /device:TPU:1, one launch (start us, length us, event | category | flops | bytes accessed | tf_op | source)
XLA Modules:
  0.0 83.4 jit_solution(152068689987017943)
XLA Ops:
  0.6 1.7 %shard_map.68 = (f32[256,384]{1,0:T(8,128)S(1)}, f32[256,384]{1,0:T(8,128)S(1)}, f32[256,384]{1,0:T(8,128)S(1)}, f32[256,384]{1,0:T(8,128)S(1)}, f32[256,384]{1,0:T(8,128)S(1)}, /*index=5*/f32[256,384]{1,0:T(8,128)S(1)}) custom-call(s32[2,6]{1,0:T(2,128)} %bitcast.18, bf16[2048,256]{1,0:T(8,128)(2,1)} %bitcast.16, f32[16,128,128]{2,1,0:T(8,128)} %bitcast.17), custom_call_target="tpu_custom_call" | custom-call | flops 100000000 | bytes 1048576 | tf_op jit(solution)/shard_map/pallas_call | solution.py:36
  2.4 2.5 %collective-permute-start.3 = (f32[256,384]{1,0:T(8,128)S(1)}, f32[256,384]{1,0:T(8,128)S(1)}, u32[]{:S(2)}, u32[]{:S(2)}) collective-permute-start(f32[256,384]{1,0:T(8,128)S(1)} %get-tuple-element.91.refs_0_), channel_id=1, source_target_pairs={{0,32},{32,0},{64,96},{96,64},{128,160},{160,128},{192,224},{224,1... | collective-permute-start | bytes 1179656 | tf_op jit(solution)/shard_map/ppermute | solution.py:56
  4.9 4.7 %collective-permute-start.4 = (f32[256,384]{1,0:T(8,128)S(1)}, f32[256,384]{1,0:T(8,128)S(1)}, u32[]{:S(2)}, u32[]{:S(2)}) collective-permute-start(f32[256,384]{1,0:T(8,128)S(1)} %get-tuple-element.92.refs_1_), channel_id=1, source_target_pairs={{0,224},{32,64},{64,32},{96,128},{128,96},{160,192},{192,160},{224... | collective-permute-start | bytes 1179656 | tf_op jit(solution)/shard_map/ppermute | solution.py:57
  9.6 1.3 %collective-permute-start.5 = (f32[256,384]{1,0:T(8,128)S(1)}, f32[256,384]{1,0:T(8,128)S(1)}, u32[]{:S(2)}, u32[]{:S(2)}) collective-permute-start(f32[256,384]{1,0:T(8,128)S(1)} %get-tuple-element.93.refs_2_), channel_id=1, source_target_pairs={{0,8},{8,0},{16,24},{24,16},{1,9},{9,1},{17,25},{25,17},{2,10},{10... | collective-permute-start | bytes 1179656 | tf_op jit(solution)/shard_map/ppermute | solution.py:56
  10.9 1.9 %collective-permute-start.6 = (f32[256,384]{1,0:T(8,128)S(1)}, f32[256,384]{1,0:T(8,128)S(1)}, u32[]{:S(2)}, u32[]{:S(2)}) collective-permute-start(f32[256,384]{1,0:T(8,128)S(1)} %get-tuple-element.94.refs_3_), channel_id=1, source_target_pairs={{0,24},{8,16},{16,8},{24,0},{1,25},{9,17},{17,9},{25,1},{2,26},{10... | collective-permute-start | bytes 1179656 | tf_op jit(solution)/shard_map/ppermute | solution.py:57
  12.8 1.8 %collective-permute-start.7 = (f32[256,384]{1,0:T(8,128)S(1)}, f32[256,384]{1,0:T(8,128)S(1)}, u32[]{:S(2)}, u32[]{:S(2)}) collective-permute-start(f32[256,384]{1,0:T(8,128)S(1)} %get-tuple-element.95.refs_4_), channel_id=1, source_target_pairs={{0,1},{1,0},{2,3},{3,2},{4,5},{5,4},{6,7},{7,6},{8,9},{9,8},{10,11... | collective-permute-start | bytes 1179656 | tf_op jit(solution)/shard_map/ppermute | solution.py:56
  14.6 1.5 %collective-permute-start.8 = (f32[256,384]{1,0:T(8,128)S(1)}, f32[256,384]{1,0:T(8,128)S(1)}, u32[]{:S(2)}, u32[]{:S(2)}) collective-permute-start(f32[256,384]{1,0:T(8,128)S(1)} %get-tuple-element.96.refs_5_), channel_id=1, source_target_pairs={{0,7},{1,2},{2,1},{3,4},{4,3},{5,6},{6,5},{7,0},{8,15},{9,10},{10,... | collective-permute-start | bytes 1179656 | tf_op jit(solution)/shard_map/ppermute | solution.py:57
  16.1 3.8 %shard_map.69.refs_13_.refs_14_.s_ref = bf16[1536,1536]{1,0:T(8,128)(2,1)S(1)} custom-call(s32[2,6]{1,0:T(2,128)S(1)} %bitcast.19, bf16[2048,2048]{1,0:T(8,128)(2,1)} %bitcast.10), custom_call_target="tpu_custom_call" | custom-call | flops 2000000000 | bytes 1048576 | tf_op jit(solution)/shard_map/pallas_call | solution.py:36
  19.9 0.0 collective-permute-done.4.refs_7_
  20.0 1.3 %collective-permute-done.6.refs_9_ = f32[256,384]{1,0:T(8,128)S(1)} collective-permute-done((f32[256,384]{1,0:T(8,128)S(1)}, f32[256,384]{1,0:T(8,128)S(1)}, u32[]{:S(2)}, u32[]{:S(2)}) %collective-permute-start.6) | collective-permute-done | bytes 393248 | tf_op jit(solution)/shard_map/ppermute | solution.py:57
  21.3 0.8 collective-permute-done.8.refs_11_
  22.1 2.6 %shard_map.70 = (f32[1536,256]{1,0:T(8,128)S(1)}, f32[1536,256]{1,0:T(8,128)S(1)}, bf16[1536,256]{1,0:T(8,128)(2,1)S(1)}, f32[256,256]{1,0:T(8,128)S(1)}, f32[25...) custom-call(s32[2,6]{1,0:T(2,128)S(1)} %bitcast.20, ...), custom_call_target="tpu_custom_call" | custom-call | flops 2000000000 | bytes 1048576 | tf_op jit(solution)/shard_map/pallas_call | solution.py:36
  24.7 1.3 %collective-permute-start.9 = (f32[256,256]{1,0:T(8,128)S(1)}, f32[256,256]{1,0:T(8,128)S(1)}, u32[]{:S(2)}, u32[]{:S(2)}) collective-permute-start(f32[256,256]{1,0:T(8,128)S(1)} %get-tuple-element.98.refs_0_), channel_id=1, source_target_pairs={{0,32},{32,0},{64,96},{96,64},{128,160},{160,128},{192,224},{224,1... | collective-permute-start | bytes 786440 | tf_op jit(solution)/shard_map/ppermute | solution.py:56
  26.0 4.7 %collective-permute-start.10 = (f32[256,256]{1,0:T(8,128)S(1)}, f32[256,256]{1,0:T(8,128)S(1)}, u32[]{:S(2)}, u32[]{:S(2)}) collective-permute-start(f32[256,256]{1,0:T(8,128)S(1)} %get-tuple-element.99.refs_1_), channel_id=1, source_target_pairs={{0,224},{32,64},{64,32},{96,128},{128,96},{160,192},{192,160},{224... | collective-permute-start | bytes 786440 | tf_op jit(solution)/shard_map/ppermute | solution.py:57
  30.7 1.3 %collective-permute-start.11 = (f32[256,256]{1,0:T(8,128)S(1)}, f32[256,256]{1,0:T(8,128)S(1)}, u32[]{:S(2)}, u32[]{:S(2)}) collective-permute-start(f32[256,256]{1,0:T(8,128)S(1)} %get-tuple-element.100.refs_2_), channel_id=1, source_target_pairs={{0,8},{8,0},{16,24},{24,16},{1,9},{9,1},{17,25},{25,17},{2,10},{10... | collective-permute-start | bytes 786440 | tf_op jit(solution)/shard_map/ppermute | solution.py:56
  32.0 1.9 %collective-permute-start.12 = (f32[256,256]{1,0:T(8,128)S(1)}, f32[256,256]{1,0:T(8,128)S(1)}, u32[]{:S(2)}, u32[]{:S(2)}) collective-permute-start(f32[256,256]{1,0:T(8,128)S(1)} %get-tuple-element.101.refs_3_), channel_id=1, source_target_pairs={{0,24},{8,16},{16,8},{24,0},{1,25},{9,17},{17,9},{25,1},{2,26},{10... | collective-permute-start | bytes 786440 | tf_op jit(solution)/shard_map/ppermute | solution.py:57
  33.9 2.7 %collective-permute-start.13 = (f32[256,256]{1,0:T(8,128)S(1)}, f32[256,256]{1,0:T(8,128)S(1)}, u32[]{:S(2)}, u32[]{:S(2)}) collective-permute-start(f32[256,256]{1,0:T(8,128)S(1)} %get-tuple-element.102.refs_4_), channel_id=1, source_target_pairs={{0,1},{1,0},{2,3},{3,2},{4,5},{5,4},{6,7},{7,6},{8,9},{9,8},{10,11... | collective-permute-start | bytes 786440 | tf_op jit(solution)/shard_map/ppermute | solution.py:56
  36.5 0.0 collective-permute-start.14
  36.5 0.0 collective-permute-done.10.refs_7_
  36.6 1.8 %collective-permute-done.12.refs_9_ = f32[256,256]{1,0:T(8,128)S(1)} collective-permute-done((f32[256,256]{1,0:T(8,128)S(1)}, f32[256,256]{1,0:T(8,128)S(1)}, u32[]{:S(2)}, u32[]{:S(2)}) %collective-permute-start.12) | collective-permute-done | bytes 262176 | tf_op jit(solution)/shard_map/ppermute | solution.py:57
  38.4 4.2 %collective-permute-done.14.refs_11_ = f32[256,256]{1,0:T(8,128)S(1)} collective-permute-done((f32[256,256]{1,0:T(8,128)S(1)}, f32[256,256]{1,0:T(8,128)S(1)}, u32[]{:S(2)}, u32[]{:S(2)}) %collective-permute-start.14) | collective-permute-done | bytes 262176 | tf_op jit(solution)/shard_map/ppermute | solution.py:57
  42.6 1.8 %shard_map.71 = (f32[1536,256]{1,0:T(8,128)S(1)}, f32[1536,256]{1,0:T(8,128)S(1)}, bf16[1536,256]{1,0:T(8,128)(2,1)S(1)}, f32[256,256]{1,0:T(8,128)S(1)}, f32[25...) custom-call(s32[2,6]{1,0:T(2,128)S(1)} %bitcast.21, f32[256,256]{1,0:T(8,128)S(1)} %get-tuple-element.98.refs_0_, ...), custom_call_target="tpu_custom_call" | custom-call | flops 2000000000 | bytes 1048576 | tf_op jit(solution)/shard_map/pallas_call | solution.py:36
  44.5 1.5 %collective-permute-start.15 = (f32[256,256]{1,0:T(8,128)S(1)}, f32[256,256]{1,0:T(8,128)S(1)}, u32[]{:S(2)}, u32[]{:S(2)}) collective-permute-start(f32[256,256]{1,0:T(8,128)S(1)} %get-tuple-element.110.refs_6_), channel_id=1, source_target_pairs={{0,32},{1,225},{32,64},{33,1},{64,96},{65,33},{96,128},{97,65},{12... | collective-permute-start | bytes 786440 | tf_op jit(solution)/shard_map/ppermute | solution.py:72
  46.0 2.7 %collective-permute-start.16 = (f32[256,256]{1,0:T(8,128)S(1)}, f32[256,256]{1,0:T(8,128)S(1)}, u32[]{:S(2)}, u32[]{:S(2)}) collective-permute-start(f32[256,256]{1,0:T(8,128)S(1)} %get-tuple-element.111.refs_7_), channel_id=1, source_target_pairs={{0,8},{1,25},{8,16},{9,1},{16,24},{17,9},{24,0},{25,17},{2,10},{3,... | collective-permute-start | bytes 786440 | tf_op jit(solution)/shard_map/ppermute | solution.py:72
  48.7 1.3 %shard_map.72 = (f32[256,256]{1,0:T(8,128)S(1)}, f32[256,256]{1,0:T(8,128)S(1)}, f32[256,256]{1,0:T(8,128)S(1)}) custom-call(s32[2,6]{1,0:T(2,128)S(1)} %bitcast.22, bf16[1536,256]{1,0:T(8,128)(2,1)S(1)} %get-tuple-element.106.zb_ref, f32[1536,256]{1,0:T(8,128)S(1)} %get-tuple-element.105.z_ref.z2_ref, f32[16,128]{1,0:T(8,128)S(1)} %bitcast.14, ...), custom_call_target="tpu_custom_call" | custom-call | flops 1000000000 | bytes 1048576 | tf_op jit(solution)/shard_map/pallas_call | solution.py:36
  50.1 0.7 shard_map.73.refs_6_
  50.8 1.3 %collective-permute-done.16.refs_4_ = f32[256,256]{1,0:T(8,128)S(1)} collective-permute-done((f32[256,256]{1,0:T(8,128)S(1)}, f32[256,256]{1,0:T(8,128)S(1)}, u32[]{:S(2)}, u32[]{:S(2)}) %collective-permute-start.16) | collective-permute-done | bytes 262176 | tf_op jit(solution)/shard_map/ppermute | solution.py:72
  52.0 0.1 shard_map.74
  52.2 16.3 %all_to_all.23 = f32[32,8,256]{2,1,0:T(8,128)S(1)} all-to-all(f32[32,8,256]{2,1,0:T(8,128)S(1)} %broadcast_in_dim.8), channel_id=1, replica_groups=mesh['gx'=8,'gy'=4,'gz_0'=4,'gz_1'=2] {'gy','gz_0','gz_1'}, dimensions={0} | all-to-all | bytes 524288 | tf_op jit(solution)/shard_map/all_to_all | solution.py:78
  68.5 11.4 %all_to_all.24 = f32[8,8,256]{2,1,0:T(8,128)S(1)} all-to-all(f32[8,8,256]{2,1,0:T(8,128)S(1)} %broadcast_in_dim.9), channel_id=1, replica_groups=mesh['gx'=8,'gy'=4,'gz_0'=4,'gz_1'=2] {'gx'}, dimensions={0} | all-to-all | bytes 131072 | tf_op jit(solution)/shard_map/all_to_all | solution.py:78
  79.9 2.7 %shard_map.75 = (f32[2048,256]{1,0:T(8,128)}, f32[1,256]{1,0:T(1,128)}, s32[1]{0:T(128)}) custom-call(s32[2,6]{1,0:T(2,128)S(1)} %bitcast.23, f32[1536,256]{1,0:T(8,128)S(1)} %get-tuple-element.97.z1_ref, f32[1536,256]{1,0:T(8,128)S(1)} %get-tuple-element.105.z_ref.z2_ref, f32[8,256]{1,0:T(8,128)S(1)} %reduce_sum.37.gram_ref), custom_call_target="tpu_custom_call" | custom-call | tf_op jit(solution)/shard_map/pallas_call | solution.py:404
  82.6 0.6 while.11
  (23 shorter events, 0.1 us)
Async XLA Ops:
  0.6 15.5 %copy-start.4 = (s32[1,1,1,6,2]{3,4,2,1,0:T(2,128)S(1)}, s32[1,1,1,6,2]{3,4,2,1,0:T(2,128)}, u32[]{:S(2)}) copy-start(s32[1,1,1,6,2]{3,4,2,1,0:T(2,128)} %param.11) | copy-start | bytes 148
  2.4 12.2 %collective-permute-start.3 = (f32[256,384]{1,0:T(8,128)S(1)}, f32[256,384]{1,0:T(8,128)S(1)}, u32[]{:S(2)}, u32[]{:S(2)}) collective-permute-start(f32[256,384]{1,0:T(8,128)S(1)} %get-tuple-element.91.refs_0_), channel_id=1, source_target_pairs={{0,32},{32,0},{64,96},{96,64},{128,160},{160,128},{192,224},{224,1... | collective-permute-start | bytes 1179656 | tf_op jit(solution)/shard_map/ppermute | solution.py:56
  4.9 15.0 %collective-permute-start.4 = (f32[256,384]{1,0:T(8,128)S(1)}, f32[256,384]{1,0:T(8,128)S(1)}, u32[]{:S(2)}, u32[]{:S(2)}) collective-permute-start(f32[256,384]{1,0:T(8,128)S(1)} %get-tuple-element.92.refs_1_), channel_id=1, source_target_pairs={{0,224},{32,64},{64,32},{96,128},{128,96},{160,192},{192,160},{224... | collective-permute-start | bytes 1179656 | tf_op jit(solution)/shard_map/ppermute | solution.py:57
  9.6 10.4 %collective-permute-start.5 = (f32[256,384]{1,0:T(8,128)S(1)}, f32[256,384]{1,0:T(8,128)S(1)}, u32[]{:S(2)}, u32[]{:S(2)}) collective-permute-start(f32[256,384]{1,0:T(8,128)S(1)} %get-tuple-element.93.refs_2_), channel_id=1, source_target_pairs={{0,8},{8,0},{16,24},{24,16},{1,9},{9,1},{17,25},{25,17},{2,10},{10... | collective-permute-start | bytes 1179656 | tf_op jit(solution)/shard_map/ppermute | solution.py:56
  10.9 10.4 %collective-permute-start.6 = (f32[256,384]{1,0:T(8,128)S(1)}, f32[256,384]{1,0:T(8,128)S(1)}, u32[]{:S(2)}, u32[]{:S(2)}) collective-permute-start(f32[256,384]{1,0:T(8,128)S(1)} %get-tuple-element.94.refs_3_), channel_id=1, source_target_pairs={{0,24},{8,16},{16,8},{24,0},{1,25},{9,17},{17,9},{25,1},{2,26},{10... | collective-permute-start | bytes 1179656 | tf_op jit(solution)/shard_map/ppermute | solution.py:57
  12.8 8.5 %collective-permute-start.7 = (f32[256,384]{1,0:T(8,128)S(1)}, f32[256,384]{1,0:T(8,128)S(1)}, u32[]{:S(2)}, u32[]{:S(2)}) collective-permute-start(f32[256,384]{1,0:T(8,128)S(1)} %get-tuple-element.95.refs_4_), channel_id=1, source_target_pairs={{0,1},{1,0},{2,3},{3,2},{4,5},{5,4},{6,7},{7,6},{8,9},{9,8},{10,11... | collective-permute-start | bytes 1179656 | tf_op jit(solution)/shard_map/ppermute | solution.py:56
  14.6 7.5 %collective-permute-start.8 = (f32[256,384]{1,0:T(8,128)S(1)}, f32[256,384]{1,0:T(8,128)S(1)}, u32[]{:S(2)}, u32[]{:S(2)}) collective-permute-start(f32[256,384]{1,0:T(8,128)S(1)} %get-tuple-element.96.refs_5_), channel_id=1, source_target_pairs={{0,7},{1,2},{2,1},{3,4},{4,3},{5,6},{6,5},{7,0},{8,15},{9,10},{10,... | collective-permute-start | bytes 1179656 | tf_op jit(solution)/shard_map/ppermute | solution.py:57
  16.1 6.0 %copy-start.3 = (f32[1,1,1,2048]{3,2,1,0:T(1,128)S(1)}, f32[1,1,1,2048]{3,2,1,0:T(1,128)}, u32[]{:S(2)}) copy-start(f32[1,1,1,2048]{3,2,1,0:T(1,128)} %param.8) | copy-start | bytes 24580
  24.7 19.8 %copy-start.2 = (bf16[1536,256]{1,0:T(8,128)(2,1)}, bf16[1536,256]{1,0:T(8,128)(2,1)S(1)}, u32[]{:S(2)}) copy-start(bf16[1536,256]{1,0:T(8,128)(2,1)S(1)} %get-tuple-element.158.refs_12_) | copy-start | bytes 2359300
  24.7 25.4 %copy-start = (f32[1536,256]{1,0:T(8,128)}, f32[1536,256]{1,0:T(8,128)S(1)}, u32[]{:S(2)}) copy-start(f32[1536,256]{1,0:T(8,128)S(1)} %get-tuple-element.156.refs_12_) | copy-start | bytes 4718596
  24.7 11.9 %collective-permute-start.9 = (f32[256,256]{1,0:T(8,128)S(1)}, f32[256,256]{1,0:T(8,128)S(1)}, u32[]{:S(2)}, u32[]{:S(2)}) collective-permute-start(f32[256,256]{1,0:T(8,128)S(1)} %get-tuple-element.98.refs_0_), channel_id=1, source_target_pairs={{0,32},{32,0},{64,96},{96,64},{128,160},{160,128},{192,224},{224,1... | collective-permute-start | bytes 786440 | tf_op jit(solution)/shard_map/ppermute | solution.py:56
  26.0 10.6 %collective-permute-start.10 = (f32[256,256]{1,0:T(8,128)S(1)}, f32[256,256]{1,0:T(8,128)S(1)}, u32[]{:S(2)}, u32[]{:S(2)}) collective-permute-start(f32[256,256]{1,0:T(8,128)S(1)} %get-tuple-element.99.refs_1_), channel_id=1, source_target_pairs={{0,224},{32,64},{64,32},{96,128},{128,96},{160,192},{192,160},{224... | collective-permute-start | bytes 786440 | tf_op jit(solution)/shard_map/ppermute | solution.py:57
  30.7 5.9 %collective-permute-start.11 = (f32[256,256]{1,0:T(8,128)S(1)}, f32[256,256]{1,0:T(8,128)S(1)}, u32[]{:S(2)}, u32[]{:S(2)}) collective-permute-start(f32[256,256]{1,0:T(8,128)S(1)} %get-tuple-element.100.refs_2_), channel_id=1, source_target_pairs={{0,8},{8,0},{16,24},{24,16},{1,9},{9,1},{17,25},{25,17},{2,10},{10... | collective-permute-start | bytes 786440 | tf_op jit(solution)/shard_map/ppermute | solution.py:56
  32.0 6.4 %collective-permute-start.12 = (f32[256,256]{1,0:T(8,128)S(1)}, f32[256,256]{1,0:T(8,128)S(1)}, u32[]{:S(2)}, u32[]{:S(2)}) collective-permute-start(f32[256,256]{1,0:T(8,128)S(1)} %get-tuple-element.101.refs_3_), channel_id=1, source_target_pairs={{0,24},{8,16},{16,8},{24,0},{1,25},{9,17},{17,9},{25,1},{2,26},{10... | collective-permute-start | bytes 786440 | tf_op jit(solution)/shard_map/ppermute | solution.py:57
  33.9 4.5 %collective-permute-start.13 = (f32[256,256]{1,0:T(8,128)S(1)}, f32[256,256]{1,0:T(8,128)S(1)}, u32[]{:S(2)}, u32[]{:S(2)}) collective-permute-start(f32[256,256]{1,0:T(8,128)S(1)} %get-tuple-element.102.refs_4_), channel_id=1, source_target_pairs={{0,1},{1,0},{2,3},{3,2},{4,5},{5,4},{6,7},{7,6},{8,9},{9,8},{10,11... | collective-permute-start | bytes 786440 | tf_op jit(solution)/shard_map/ppermute | solution.py:56
  36.5 6.1 %collective-permute-start.14 = (f32[256,256]{1,0:T(8,128)S(1)}, f32[256,256]{1,0:T(8,128)S(1)}, u32[]{:S(2)}, u32[]{:S(2)}) collective-permute-start(f32[256,256]{1,0:T(8,128)S(1)} %get-tuple-element.103.refs_5_), channel_id=1, source_target_pairs={{0,7},{1,2},{2,1},{3,4},{4,3},{5,6},{6,5},{7,0},{8,15},{9,10},{10,... | collective-permute-start | bytes 786440 | tf_op jit(solution)/shard_map/ppermute | solution.py:57
  44.5 5.6 %copy-start.1 = (f32[1536,256]{1,0:T(8,128)}, f32[1536,256]{1,0:T(8,128)S(1)}, u32[]{:S(2)}) copy-start(f32[1536,256]{1,0:T(8,128)S(1)} %get-tuple-element.155.refs_13_) | copy-start | bytes 4718596
  44.5 6.3 %collective-permute-start.15 = (f32[256,256]{1,0:T(8,128)S(1)}, f32[256,256]{1,0:T(8,128)S(1)}, u32[]{:S(2)}, u32[]{:S(2)}) collective-permute-start(f32[256,256]{1,0:T(8,128)S(1)} %get-tuple-element.110.refs_6_), channel_id=1, source_target_pairs={{0,32},{1,225},{32,64},{33,1},{64,96},{65,33},{96,128},{97,65},{12... | collective-permute-start | bytes 786440 | tf_op jit(solution)/shard_map/ppermute | solution.py:72
  46.0 6.1 %collective-permute-start.16 = (f32[256,256]{1,0:T(8,128)S(1)}, f32[256,256]{1,0:T(8,128)S(1)}, u32[]{:S(2)}, u32[]{:S(2)}) collective-permute-start(f32[256,256]{1,0:T(8,128)S(1)} %get-tuple-element.111.refs_7_), channel_id=1, source_target_pairs={{0,8},{1,25},{8,16},{9,1},{16,24},{17,9},{24,0},{25,17},{2,10},{3,... | collective-permute-start | bytes 786440 | tf_op jit(solution)/shard_map/ppermute | solution.py:72
  48.7 3.3 %collective-permute-start.17 = (f32[256,256]{1,0:T(8,128)S(1)}, f32[256,256]{1,0:T(8,128)S(1)}, u32[]{:S(2)}, u32[]{:S(2)}) collective-permute-start(f32[256,256]{1,0:T(8,128)S(1)} %get-tuple-element.112.refs_8_), channel_id=1, source_target_pairs={{0,1},{1,2},{2,3},{3,4},{4,5},{5,6},{6,7},{7,0},{8,9},{9,10},{10,1... | collective-permute-start | bytes 786440 | tf_op jit(solution)/shard_map/ppermute | solution.py:67
